TPU v7x, 32 devices: a whole 2x2x4 slice. The times are simulated.
32 devices in a mesh: inner: 4 (over z), outer: 8 (over y, x, core).
Axes of the slice: x: 2, y: 2, z: 4, core: 2. Of those that a mesh axis runs over, the one named last changes fastest.
Arguments:
- inputs: bfloat16 [16, 1024, 2048], P('outer', 'inner'), may hold values from -6 to 6
- attn_gain: bfloat16 [2048], P(('inner', 'outer')), may hold values from 0.25 to 1.75
- w_query: bfloat16 [2048, 1536], P(('inner', 'outer')), may hold values from -0.125 to 0.125
- key_weight: bfloat16 [2048, 384], P(('inner', 'outer')), may hold values from -0.125 to 0.125
- value_weight: bfloat16 [2048, 384], P(('inner', 'outer')), may hold values from -0.125 to 0.125
- qk_gain: bfloat16 [128], P(('inner', 'outer')), may hold values from 1 to 2
- w_out: bfloat16 [1536, 2048], P(('inner', 'outer')), may hold values from -0.875 to 0.875
- ffn_gain: bfloat16 [2048], P(('inner', 'outer')), may hold values from 0.25 to 1.75
- w_gate: bfloat16 [2048, 4864], P(('inner', 'outer')), may hold values from -0.125 to 0.125
- w_up: bfloat16 [2048, 4864], P(('inner', 'outer')), may hold values from -0.125 to 0.125
- w_down: bfloat16 [4864, 2048], P(('inner', 'outer')), may hold values from -0.078125 to 0.078125
- cotangent: bfloat16 [16, 1024, 2048], P('outer', 'inner'), may hold values from -6 to 6
Outputs:
- result: bfloat16 [16, 1024, 2048], P('outer', 'inner')
- d_inputs: float32 [16, 1024, 2048], P('outer', 'inner')
- d_attn_gain: float32 [2048], P(('inner', 'outer'))
- d_query: float32 [2048, 1536], P(('inner', 'outer'))
- d_key: float32 [2048, 384], P(('inner', 'outer'))
- d_value: float32 [2048, 384], P(('inner', 'outer'))
- d_qk_gain: float32 [128], P(('inner', 'outer'))
- d_out: float32 [1536, 2048], P(('inner', 'outer'))
- d_ffn_gain: float32 [2048], P(('inner', 'outer'))
- d_gate: float32 [2048, 4864], P(('inner', 'outer'))
- d_up: float32 [2048, 4864], P(('inner', 'outer'))
- d_down: float32 [4864, 2048], P(('inner', 'outer'))
All inputs are finite; a program needn't handle non-finite values.
Results may differ from a plain program's by a relative error of at most 0.025.
Values may be sent and summed in bfloat16 or wider, within the bound.
No kernel may reach another device: no remote copies, remote signals or barrier semaphores. Data moves between devices by JAX's collectives and lax.ppermute only.
A program may use at most 320 MiB of HBM per device.

v0:
```python
import jax
import jax.numpy as jnp
from jax import lax
from jax.sharding import PartitionSpec as P

MODEL_WIDTH = 2048
QUERY_HEADS = 24
KEY_VALUE_HEADS = 6
HEAD_SIZE = 64
SEQUENCE_TOKENS = 1024
BLOCK = 256


EPS = 1e-06
NEGATIVE = -1e30


def matrix_product(left, right):
    return jnp.dot(left, right, preferred_element_type=jnp.float32)


def left_t(left, right):
    return lax.dot_general(
        left, right, (((0,), (0,)), ((), ())), preferred_element_type=jnp.float32
    )


def right_t(left, right):
    return lax.dot_general(
        left, right, (((1,), (1,)), ((), ())), preferred_element_type=jnp.float32
    )


def rms_norm(v, gain):
    inverse = lax.rsqrt(jnp.mean(v * v, axis=-1, keepdims=True) + EPS)
    return (v * inverse * gain, inverse)


def rms_back(v, inverse, gain, grad):
    scaled = grad * gain
    back = inverse * scaled - v * inverse**3 * jnp.mean(scaled * v, axis=-1, keepdims=True)
    return (back, grad * v * inverse)


def rotary_apply(v, cosine_table, sine_table):
    half = HEAD_SIZE // 2
    turned = jnp.concatenate([-v[..., half:], v[..., :half]], axis=-1)
    return v * cosine_table + turned * sine_table


def rotary_apply_backward(grad, cosine_table, sine_table):
    half = HEAD_SIZE // 2
    times_sine = grad * sine_table
    return grad * cosine_table + jnp.concatenate(
        [times_sine[..., half:], -times_sine[..., :half]], axis=-1
    )


def body(
    inputs,
    attn_gain,
    w_query,
    key_weight,
    value_weight,
    qk_gain,
    w_out,
    ffn_gain,
    w_gate,
    w_up,
    w_down,
    cotangent,
):
    sequence_list, token_span = (inputs.shape[0], inputs.shape[1])
    token_rows = sequence_list * token_span
    head_groups = QUERY_HEADS // KEY_VALUE_HEADS
    scale = HEAD_SIZE ** (-0.5)
    gain_one, wq, key_projection_weight, wv, gains_qk, wo = (
        lax.all_gather(attn_gain, ("inner", "outer"), axis=0, tiled=True),
        lax.all_gather(w_query, ("inner", "outer"), axis=0, tiled=True),
        lax.all_gather(key_weight, ("inner", "outer"), axis=0, tiled=True),
        lax.all_gather(value_weight, ("inner", "outer"), axis=0, tiled=True),
        lax.all_gather(qk_gain, ("inner", "outer"), axis=0, tiled=True),
        lax.all_gather(w_out, ("inner", "outer"), axis=0, tiled=True),
    )
    gain_two, wg, wu, wd = (
        lax.all_gather(ffn_gain, ("inner", "outer"), axis=0, tiled=True),
        lax.all_gather(w_gate, ("inner", "outer"), axis=0, tiled=True),
        lax.all_gather(w_up, ("inner", "outer"), axis=0, tiled=True),
        lax.all_gather(w_down, ("inner", "outer"), axis=0, tiled=True),
    )
    base = lax.axis_index("inner") * token_span
    positions = (base + jnp.arange(token_span)).astype(jnp.float32)
    half = HEAD_SIZE // 2
    freq = 10000.0 ** (-jnp.arange(half, dtype=jnp.float32) * 2.0 / HEAD_SIZE)
    angle = positions[:, None] * freq[None, :]
    cosine_table = jnp.concatenate([jnp.cos(angle), jnp.cos(angle)], axis=-1)[None, :, None, :]
    sine_table = jnp.concatenate([jnp.sin(angle), jnp.sin(angle)], axis=-1)[None, :, None, :]
    g_one = gain_one.astype(jnp.float32)
    g_two = gain_two.astype(jnp.float32)
    g_query = gains_qk[:HEAD_SIZE].astype(jnp.float32)
    key_norm_gain = gains_qk[HEAD_SIZE:].astype(jnp.float32)
    x_flat = inputs.reshape(token_rows, MODEL_WIDTH).astype(jnp.float32)
    normalized_input, inv_one = rms_norm(x_flat, g_one)
    normalized_input_backward = normalized_input.astype(jnp.bfloat16)
    q_lin = matrix_product(normalized_input_backward, wq).reshape(
        sequence_list, token_span, QUERY_HEADS, HEAD_SIZE
    )
    key_linear = matrix_product(normalized_input_backward, key_projection_weight).reshape(
        sequence_list, token_span, KEY_VALUE_HEADS, HEAD_SIZE
    )
    value_linear = matrix_product(normalized_input_backward, wv)
    q_normed, inv_query = rms_norm(q_lin, g_query)
    normalized_key, inverse_key_norm = rms_norm(key_linear, key_norm_gain)
    query_rows = rotary_apply(q_normed, cosine_table, sine_table).astype(jnp.bfloat16)
    key = (
        rotary_apply(normalized_key, cosine_table, sine_table)
        .astype(jnp.bfloat16)
        .reshape(sequence_list, token_span, KEY_VALUE_HEADS * HEAD_SIZE)
    )
    value_rows = value_linear.astype(jnp.bfloat16).reshape(
        sequence_list, token_span, KEY_VALUE_HEADS * HEAD_SIZE
    )
    gathered_keys, gathered_values = (
        lax.all_gather(key, "inner", axis=1, tiled=True),
        lax.all_gather(value_rows, "inner", axis=1, tiled=True),
    )
    q_blocks = (
        query_rows.reshape(sequence_list, token_span, KEY_VALUE_HEADS, head_groups, HEAD_SIZE)
        .transpose(0, 2, 3, 1, 4)
        .reshape(sequence_list * KEY_VALUE_HEADS, head_groups * token_span, HEAD_SIZE)
    )
    k_blocks = (
        gathered_keys.reshape(sequence_list, SEQUENCE_TOKENS, KEY_VALUE_HEADS, HEAD_SIZE)
        .transpose(0, 2, 1, 3)
        .reshape(sequence_list * KEY_VALUE_HEADS, SEQUENCE_TOKENS, HEAD_SIZE)
    )
    v_blocks = (
        gathered_values.reshape(sequence_list, SEQUENCE_TOKENS, KEY_VALUE_HEADS, HEAD_SIZE)
        .transpose(0, 2, 1, 3)
        .reshape(sequence_list * KEY_VALUE_HEADS, SEQUENCE_TOKENS, HEAD_SIZE)
    )
    row_block = (base + jnp.arange(head_groups * token_span) % token_span) // BLOCK
    allowed = (jnp.arange(SEQUENCE_TOKENS) // BLOCK)[None, :] <= row_block[:, None]

    def scores_of(q_piece, k_piece):
        return jnp.where(allowed, right_t(q_piece, k_piece) * scale, NEGATIVE)

    def forward_block(triple):
        q_piece, k_piece, v_piece = triple
        scores = scores_of(q_piece, k_piece)
        top = jnp.max(scores, axis=-1, keepdims=True)
        expo = jnp.exp(scores - top)
        total = jnp.sum(expo, axis=-1, keepdims=True)
        prob = (expo / total).astype(jnp.bfloat16)
        return (matrix_product(prob, v_piece), (top + jnp.log(total))[:, 0])

    attended, log_totals = lax.map(forward_block, (q_blocks, k_blocks, v_blocks))
    mixed = (
        attended.astype(jnp.bfloat16)
        .reshape(sequence_list, KEY_VALUE_HEADS, head_groups, token_span, HEAD_SIZE)
        .transpose(0, 3, 1, 2, 4)
        .reshape(token_rows, QUERY_HEADS * HEAD_SIZE)
    )
    resid = x_flat + matrix_product(mixed, wo)
    normed2, inv_two = rms_norm(resid, g_two)
    normed2_b = normed2.astype(jnp.bfloat16)
    gate = matrix_product(normed2_b, wg)
    upper = matrix_product(normed2_b, wu)
    sigma = jax.nn.sigmoid(gate)
    active = gate * sigma
    hidden = (active * upper).astype(jnp.bfloat16)
    output = resid + matrix_product(hidden, wd)
    result = output.astype(jnp.bfloat16).reshape(sequence_list, token_span, MODEL_WIDTH)
    gain_one, wq, key_projection_weight, wv, gains_qk, wo = (
        lax.all_gather(attn_gain, ("inner", "outer"), axis=0, tiled=True),
        lax.all_gather(w_query, ("inner", "outer"), axis=0, tiled=True),
        lax.all_gather(key_weight, ("inner", "outer"), axis=0, tiled=True),
        lax.all_gather(value_weight, ("inner", "outer"), axis=0, tiled=True),
        lax.all_gather(qk_gain, ("inner", "outer"), axis=0, tiled=True),
        lax.all_gather(w_out, ("inner", "outer"), axis=0, tiled=True),
    )
    gain_two, wg, wu, wd = (
        lax.all_gather(ffn_gain, ("inner", "outer"), axis=0, tiled=True),
        lax.all_gather(w_gate, ("inner", "outer"), axis=0, tiled=True),
        lax.all_gather(w_up, ("inner", "outer"), axis=0, tiled=True),
        lax.all_gather(w_down, ("inner", "outer"), axis=0, tiled=True),
    )
    grad_out = cotangent.reshape(token_rows, MODEL_WIDTH)
    d_hidden = right_t(grad_out, wd)
    grad_down = left_t(hidden, grad_out)
    d_gate_b = (d_hidden * upper * (sigma * (1.0 + gate * (1.0 - sigma)))).astype(jnp.bfloat16)
    d_up_b = (d_hidden * active).astype(jnp.bfloat16)
    grad_gate = left_t(normed2_b, d_gate_b)
    grad_up = left_t(normed2_b, d_up_b)
    d_normed2 = right_t(d_gate_b, wg) + right_t(d_up_b, wu)
    back_two, terms_two = rms_back(resid, inv_two, g_two, d_normed2)
    grad_gain_two = jnp.sum(terms_two, axis=0)
    d_resid = grad_out.astype(jnp.float32) + back_two
    ffn_grads = (grad_gain_two, grad_gate, grad_up, grad_down)
    ffn_part = (
        lax.psum_scatter(
            ffn_grads[0].astype(jnp.bfloat16), "inner", scatter_dimension=0, tiled=True
        ).astype(jnp.float32),
        lax.psum_scatter(
            ffn_grads[1].astype(jnp.bfloat16), "inner", scatter_dimension=0, tiled=True
        ).astype(jnp.float32),
        lax.psum_scatter(
            ffn_grads[2].astype(jnp.bfloat16), "inner", scatter_dimension=0, tiled=True
        ).astype(jnp.float32),
        lax.psum_scatter(
            ffn_grads[3].astype(jnp.bfloat16), "inner", scatter_dimension=0, tiled=True
        ).astype(jnp.float32),
    )
    ffn_done = (
        lax.psum_scatter(
            ffn_part[0].astype(jnp.bfloat16), "outer", scatter_dimension=0, tiled=True
        ).astype(jnp.float32),
        lax.psum_scatter(
            ffn_part[1].astype(jnp.bfloat16), "outer", scatter_dimension=0, tiled=True
        ).astype(jnp.float32),
        lax.psum_scatter(
            ffn_part[2].astype(jnp.bfloat16), "outer", scatter_dimension=0, tiled=True
        ).astype(jnp.float32),
        lax.psum_scatter(
            ffn_part[3].astype(jnp.bfloat16), "outer", scatter_dimension=0, tiled=True
        ).astype(jnp.float32),
    )
    d_resid_b = d_resid.astype(jnp.bfloat16)
    grad_wo = left_t(mixed, d_resid_b)
    mixed_gradient = right_t(d_resid_b, wo).astype(jnp.bfloat16)
    d_blocks = (
        mixed_gradient.reshape(sequence_list, token_span, KEY_VALUE_HEADS, head_groups, HEAD_SIZE)
        .transpose(0, 2, 3, 1, 4)
        .reshape(sequence_list * KEY_VALUE_HEADS, head_groups * token_span, HEAD_SIZE)
    )

    def backward_block(quintet):
        q_piece, k_piece, v_piece, d_piece, lse_piece = quintet
        prob = jnp.exp(scores_of(q_piece, k_piece) - lse_piece[:, None])
        d_prob = right_t(d_piece, v_piece)
        d_score = (prob * (d_prob - jnp.sum(prob * d_prob, axis=-1, keepdims=True))).astype(
            jnp.bfloat16
        )
        return (
            matrix_product(d_score, k_piece) * scale,
            left_t(d_score, q_piece) * scale,
            left_t(prob.astype(jnp.bfloat16), d_piece),
        )

    query_block_gradient, key_block_gradient, value_block_gradient = lax.map(
        backward_block, (q_blocks, k_blocks, v_blocks, d_blocks, log_totals)
    )
    d_keys = (
        key_block_gradient.reshape(sequence_list, KEY_VALUE_HEADS, SEQUENCE_TOKENS, HEAD_SIZE)
        .transpose(0, 2, 1, 3)
        .reshape(sequence_list, SEQUENCE_TOKENS, KEY_VALUE_HEADS * HEAD_SIZE)
    )
    d_values = (
        value_block_gradient.reshape(sequence_list, KEY_VALUE_HEADS, SEQUENCE_TOKENS, HEAD_SIZE)
        .transpose(0, 2, 1, 3)
        .reshape(sequence_list, SEQUENCE_TOKENS, KEY_VALUE_HEADS * HEAD_SIZE)
    )
    local_key_gradient, local_value_gradient = (
        lax.psum_scatter(
            d_keys.astype(jnp.bfloat16), "inner", scatter_dimension=1, tiled=True
        ).astype(jnp.float32),
        lax.psum_scatter(
            d_values.astype(jnp.bfloat16), "inner", scatter_dimension=1, tiled=True
        ).astype(jnp.float32),
    )
    d_query_rot = (
        query_block_gradient.reshape(
            sequence_list, KEY_VALUE_HEADS, head_groups, token_span, HEAD_SIZE
        )
        .transpose(0, 3, 1, 2, 4)
        .reshape(sequence_list, token_span, QUERY_HEADS, HEAD_SIZE)
    )
    back_query, terms_query = rms_back(
        q_lin, inv_query, g_query, rotary_apply_backward(d_query_rot, cosine_table, sine_table)
    )
    key_backward_pass, terms_key = rms_back(
        key_linear,
        inverse_key_norm,
        key_norm_gain,
        rotary_apply_backward(
            local_key_gradient.reshape(sequence_list, token_span, KEY_VALUE_HEADS, HEAD_SIZE),
            cosine_table,
            sine_table,
        ),
    )
    grad_qk = jnp.concatenate(
        [jnp.sum(terms_query, axis=(0, 1, 2)), jnp.sum(terms_key, axis=(0, 1, 2))]
    )
    d_ql = back_query.reshape(token_rows, QUERY_HEADS * HEAD_SIZE).astype(jnp.bfloat16)
    key_linear_gradient = key_backward_pass.reshape(token_rows, KEY_VALUE_HEADS * HEAD_SIZE).astype(
        jnp.bfloat16
    )
    value_linear_gradient = local_value_gradient.reshape(
        token_rows, KEY_VALUE_HEADS * HEAD_SIZE
    ).astype(jnp.bfloat16)
    grad_wq = left_t(normalized_input_backward, d_ql)
    grad_wk = left_t(normalized_input_backward, key_linear_gradient)
    grad_wv = left_t(normalized_input_backward, value_linear_gradient)
    d_normed = (
        right_t(d_ql, wq)
        + right_t(key_linear_gradient, key_projection_weight)
        + right_t(value_linear_gradient, wv)
    )
    back_one, terms_one = rms_back(x_flat, inv_one, g_one, d_normed)
    grad_gain_one = jnp.sum(terms_one, axis=0)
    d_inputs = (d_resid + back_one).reshape(sequence_list, token_span, MODEL_WIDTH)
    attn_grads = (grad_gain_one, grad_wq, grad_wk, grad_wv, grad_qk, grad_wo)
    attn_part = (
        lax.psum_scatter(
            attn_grads[0].astype(jnp.bfloat16), "inner", scatter_dimension=0, tiled=True
        ).astype(jnp.float32),
        lax.psum_scatter(
            attn_grads[1].astype(jnp.bfloat16), "inner", scatter_dimension=0, tiled=True
        ).astype(jnp.float32),
        lax.psum_scatter(
            attn_grads[2].astype(jnp.bfloat16), "inner", scatter_dimension=0, tiled=True
        ).astype(jnp.float32),
        lax.psum_scatter(
            attn_grads[3].astype(jnp.bfloat16), "inner", scatter_dimension=0, tiled=True
        ).astype(jnp.float32),
        lax.psum_scatter(
            attn_grads[4].astype(jnp.bfloat16), "inner", scatter_dimension=0, tiled=True
        ).astype(jnp.float32),
        lax.psum_scatter(
            attn_grads[5].astype(jnp.bfloat16), "inner", scatter_dimension=0, tiled=True
        ).astype(jnp.float32),
    )
    attn_done = (
        lax.psum_scatter(
            attn_part[0].astype(jnp.bfloat16), "outer", scatter_dimension=0, tiled=True
        ).astype(jnp.float32),
        lax.psum_scatter(
            attn_part[1].astype(jnp.bfloat16), "outer", scatter_dimension=0, tiled=True
        ).astype(jnp.float32),
        lax.psum_scatter(
            attn_part[2].astype(jnp.bfloat16), "outer", scatter_dimension=0, tiled=True
        ).astype(jnp.float32),
        lax.psum_scatter(
            attn_part[3].astype(jnp.bfloat16), "outer", scatter_dimension=0, tiled=True
        ).astype(jnp.float32),
        lax.psum_scatter(
            attn_part[4].astype(jnp.bfloat16), "outer", scatter_dimension=0, tiled=True
        ).astype(jnp.float32),
        lax.psum_scatter(
            attn_part[5].astype(jnp.bfloat16), "outer", scatter_dimension=0, tiled=True
        ).astype(jnp.float32),
    )
    return (
        result,
        d_inputs,
        attn_done[0],
        attn_done[1],
        attn_done[2],
        attn_done[3],
        attn_done[4],
        attn_done[5],
        ffn_done[0],
        ffn_done[1],
        ffn_done[2],
        ffn_done[3],
    )


def solution(mesh):
    placed = (
        P("outer", "inner", None),
        P(("inner", "outer")),
        P(("inner", "outer"), None),
        P(("inner", "outer"), None),
        P(("inner", "outer"), None),
        P(("inner", "outer")),
        P(("inner", "outer"), None),
        P(("inner", "outer")),
        P(("inner", "outer"), None),
        P(("inner", "outer"), None),
        P(("inner", "outer"), None),
        P("outer", "inner", None),
    )
    return jax.shard_map(
        body,
        mesh=mesh,
        in_specs=placed,
        out_specs=(
            P("outer", "inner", None),
            P("outer", "inner", None),
            P(("inner", "outer")),
            P(("inner", "outer"), None),
            P(("inner", "outer"), None),
            P(("inner", "outer"), None),
            P(("inner", "outer")),
            P(("inner", "outer"), None),
            P(("inner", "outer")),
            P(("inner", "outer"), None),
            P(("inner", "outer"), None),
            P(("inner", "outer"), None),
        ),
        check_vma=False,
    )
```

profile of v0, /device:TPU:12, one launch (start us, length us, event | category | flops | bytes accessed | tf_op | source)
XLA Modules:
  0.0 2673.2 jit_solution(11347186537485612827)
XLA Ops:
  11.3 41.5 %all-reduce.9 = (bf16[2048]{0:T(1024)(128)(2,1)S(1)}, bf16[128]{0:T(256)(128)(2,1)S(1)}, bf16[2048]{0:T(1024)(128)(2,1)S(1)}) all-reduce(bf16[2048]{0:T(1024)(128)(2,1)S(1)} %dynamic-update-slice, bf16[128]{0:T(256)(128)(2,1)S(1)} %dynamic-update-slice.1, ...), channel_id=1, replica_groups=mesh['inner'=4,'outer'=8] {'inner','outer'}, use_global_device_ids=true, to_apply=%add | all-reduce | flops 4224 | bytes 16896
  76.1 46.6 %all-gather.16.cloned.1.call-done = bf16[2048,384]{1,0:T(8,128)(2,1)} async-done(((bf16[64,384]{1,0:T(8,128)(2,1)}), bf16[2048,384]{1,0:T(8,128)(2,1)}) %all-gather.16.cloned.1.call-update) | async-done | bytes 1572880 | tf_op jit(solution)/shard_map/all_gather | solution.py:81
  133.5 26.8 %all-gather.14.cloned.1.call-done = bf16[2,1024,384]{1,2,0:T(8,128)(2,1)} async-done(((bf16[2,256,384]{1,2,0:T(8,128)(2,1)}), bf16[2,1024,384]{1,2,0:T(8,128)(2,1)}) %all-gather.14.cloned.1.call-update) | async-done | bytes 1572880 | tf_op jit(solution)/shard_map/all_gather | solution.py:124
  164.6 33.7 %all-gather.18.cloned.1.call-done = bf16[2,1024,384]{1,2,0:T(8,128)(2,1)} async-done(((bf16[2,256,384]{1,2,0:T(8,128)(2,1)}), bf16[2,1024,384]{1,2,0:T(8,128)(2,1)}) %all-gather.18.cloned.1.call-update) | async-done | bytes 1572880 | tf_op jit(solution)/shard_map/all_gather | solution.py:125
  202.4 68.3 %all-gather.10.cloned.1.call-done = bf16[2048,1536]{1,0:T(8,128)(2,1)} async-done(((bf16[64,1536]{1,0:T(8,128)(2,1)}), bf16[2048,1536]{1,0:T(8,128)(2,1)}) %all-gather.10.cloned.1.call-update) | async-done | bytes 6291472 | tf_op jit(solution)/shard_map/all_gather | solution.py:79
  294.0 126.2 %while.30 = (s32[]{:T(128)}, bf16[12,1024,64]{1,2,0:T(8,128)(2,1)}, f32[12,1024]{1,0:T(8,128)}, bf16[12,1024,64]{2,1,0:T(8,128)(2,1)}, bf16[12,1024,64]{2,1,0:T(...) while((s32[]{:T(128)}, bf16[12,1024,64]{1,2,0:T(8,128)(2,1)}, ...), condition=%wide.region_6.7_spmd.clone.clone, body=%wide.region_3.6_spmd.clone.sunk.clone | while | flops 284163072 | bytes 30476404 | solution.py:157
  437.2 33.0 %all-gather.22.cloned.1.call-done = bf16[2048,4864]{1,0:T(8,128)(2,1)} async-done(((bf16[64,4864]{1,0:T(8,128)(2,1)}), bf16[2048,4864]{1,0:T(8,128)(2,1)}) %all-gather.22.cloned.1.call-update) | async-done | bytes 19922960 | tf_op jit(solution)/shard_map/all_gather | solution.py:87
  470.2 17.5 fusion.92
  487.8 112.3 %all-gather.24.cloned.1.call-done = bf16[2048,4864]{1,0:T(8,128)(2,1)} async-done(((bf16[64,4864]{1,0:T(8,128)(2,1)}), bf16[2048,4864]{1,0:T(8,128)(2,1)}) %all-gather.24.cloned.1.call-update) | async-done | bytes 19922960 | tf_op jit(solution)/shard_map/all_gather | solution.py:88
  600.1 17.2 fusion.93
  617.3 112.7 %all-gather.26.cloned.1.call-done = bf16[4864,2048]{1,0:T(8,128)(2,1)} async-done(((bf16[152,2048]{1,0:T(8,128)(2,1)}), bf16[4864,2048]{1,0:T(8,128)(2,1)}) %all-gather.26.cloned.1.call-update) | async-done | bytes 19922960 | tf_op jit(solution)/shard_map/all_gather | solution.py:89
  729.9 25.2 multiply_convert_fusion.1
  755.1 17.6 fusion.94
  772.8 20.3 multiply_reduce_fusion.1
  812.6 146.2 %while.31 = (s32[]{:T(128)}, f32[12,1024,64]{1,2,0:T(8,128)}, bf16[12,1024,64]{1,2,0:T(8,128)(2,1)}, bf16[12,1024,64]{1,2,0:T(8,128)(2,1)}, bf16[12,1024,64]{2,1...) while((s32[]{:T(128)}, f32[12,1024,64]{1,2,0:T(8,128)}, ...), condition=%wide.region_11.12_spmd.clone.clone, body=%wide.region_9.11_spmd.clone.sunk.clone | while | flops 681704448 | bytes 34112624 | solution.py:250
  959.7 32.8 %reduce-scatter.17.cloned.1.call-done = bf16[2,256,384]{1,2,0:T(8,128)(2,1)} async-done(((bf16[2,1024,384]{1,2,0:T(8,128)(2,1)}), bf16[2,256,384]{1,2,0:T(8,128)(2,1)}) %reduce-scatter.17.cloned.1.call-update) | async-done | bytes 393232 | tf_op jit(solution)/shard_map/reduce_scatter | solution.py:264
  998.7 30.4 %reduce-scatter.19.cloned.1.call-done = bf16[2,256,384]{1,2,0:T(8,128)(2,1)} async-done(((bf16[2,1024,384]{1,2,0:T(8,128)(2,1)}), bf16[2,256,384]{1,2,0:T(8,128)(2,1)}) %reduce-scatter.19.cloned.1.call-update) | async-done | bytes 393232 | tf_op jit(solution)/shard_map/reduce_scatter | solution.py:267
  1061.3 15.9 convolution_convert_fusion.2
  1077.3 16.0 convolution_convert_fusion.1
  1094.9 16.0 convolution_convert_fusion
  1112.4 103.0 %reduce-scatter.33.cloned.1.call-done = bf16[384,2048]{1,0:T(8,128)(2,1)} async-done(((bf16[1536,2048]{1,0:T(8,128)(2,1)}), bf16[384,2048]{1,0:T(8,128)(2,1)}) %reduce-scatter.33.cloned.1.call-update) | async-done | bytes 1572880 | tf_op jit(solution)/shard_map/reduce_scatter | solution.py:329
  1215.4 113.4 %reduce-scatter.21.cloned.1.call-done = bf16[512,1536]{1,0:T(8,128)(2,1)} async-done(((bf16[2048,1536]{1,0:T(8,128)(2,1)}), bf16[512,1536]{1,0:T(8,128)(2,1)}) %reduce-scatter.21.cloned.1.call-update) | async-done | bytes 1572880 | tf_op jit(solution)/shard_map/reduce_scatter | solution.py:317
  1328.9 332.4 %reduce-scatter.37.cloned.1.call-done = bf16[512,4864]{1,0:T(8,128)(2,1)} async-done(((bf16[2048,4864]{1,0:T(8,128)(2,1)}), bf16[512,4864]{1,0:T(8,128)(2,1)}) %reduce-scatter.37.cloned.1.call-update) | async-done | bytes 4980752 | tf_op jit(solution)/shard_map/reduce_scatter | solution.py:204
  1661.3 333.9 %reduce-scatter.41.cloned.1.call-done = bf16[512,4864]{1,0:T(8,128)(2,1)} async-done(((bf16[2048,4864]{1,0:T(8,128)(2,1)}), bf16[512,4864]{1,0:T(8,128)(2,1)}) %reduce-scatter.41.cloned.1.call-update) | async-done | bytes 4980752 | tf_op jit(solution)/shard_map/reduce_scatter | solution.py:207
  1995.3 333.9 %reduce-scatter.45.cloned.1.call-done = bf16[1216,2048]{1,0:T(8,128)(2,1)} async-done(((bf16[4864,2048]{1,0:T(8,128)(2,1)}), bf16[1216,2048]{1,0:T(8,128)(2,1)}) %reduce-scatter.45.cloned.1.call-update) | async-done | bytes 4980752 | tf_op jit(solution)/shard_map/reduce_scatter | solution.py:210
  2341.1 17.1 add_convert_fusion
  2377.8 11.8 all-reduce.10
  2406.7 40.3 %reduce-scatter.35.cloned.1.call-done = bf16[48,2048]{1,0:T(8,128)(2,1)} async-done(((bf16[384,2048]{1,0:T(8,128)(2,1)}), bf16[48,2048]{1,0:T(8,128)(2,1)}) %reduce-scatter.35.cloned.1.call-update) | async-done | bytes 196624 | tf_op jit(solution)/shard_map/reduce_scatter | solution.py:349
  2448.6 40.0 %reduce-scatter.23.cloned.1.call-done = bf16[64,1536]{1,0:T(8,128)(2,1)} async-done(((bf16[512,1536]{1,0:T(8,128)(2,1)}), bf16[64,1536]{1,0:T(8,128)(2,1)}) %reduce-scatter.23.cloned.1.call-update) | async-done | bytes 196624 | tf_op jit(solution)/shard_map/reduce_scatter | solution.py:337
  2490.3 56.9 %reduce-scatter.39.cloned.1.call-done = bf16[64,4864]{1,0:T(8,128)(2,1)} async-done(((bf16[512,4864]{1,0:T(8,128)(2,1)}), bf16[64,4864]{1,0:T(8,128)(2,1)}) %reduce-scatter.39.cloned.1.call-update) | async-done | bytes 622608 | tf_op jit(solution)/shard_map/reduce_scatter | solution.py:218
  2549.4 56.3 %reduce-scatter.43.cloned.1.call-done = bf16[64,4864]{1,0:T(8,128)(2,1)} async-done(((bf16[512,4864]{1,0:T(8,128)(2,1)}), bf16[64,4864]{1,0:T(8,128)(2,1)}) %reduce-scatter.43.cloned.1.call-update) | async-done | bytes 622608 | tf_op jit(solution)/shard_map/reduce_scatter | solution.py:221
  2607.9 56.4 %reduce-scatter.47.cloned.1.call-done = bf16[152,2048]{1,0:T(8,128)(2,1)} async-done(((bf16[1216,2048]{1,0:T(8,128)(2,1)}), bf16[152,2048]{1,0:T(8,128)(2,1)}) %reduce-scatter.47.cloned.1.call-update) | async-done | bytes 622608 | tf_op jit(solution)/shard_map/reduce_scatter | solution.py:224
  (421 shorter events, 475.4 us)
Async XLA Ops:
  7.2 58.8 %all-gather.12.cloned.1.call-start = ((), (), s32[]{:S(2)}) async-start(), calls=%async_computation.17 | async-start | bytes 1622016 | tf_op jit(solution)/shard_map/all_gather | solution.py:80
  7.9 114.8 %all-gather.16.cloned.1.call-start = ((), (), s32[]{:S(2)}) async-start(), calls=%async_computation.19 | async-start | bytes 1622016 | tf_op jit(solution)/shard_map/all_gather | solution.py:81
  8.7 151.7 %all-gather.14.cloned.1.call-start = ((), (), s32[]{:S(2)}) async-start(), calls=%async_computation.18 | async-start | bytes 1966080 | tf_op jit(solution)/shard_map/all_gather | solution.py:124
  53.1 234.4 %copy-start.14 = (f32[256,64]{0,1:T(8,128)}, f32[256,64]{0,1:T(8,128)S(1)}, u32[]{:S(2)}) copy-start(f32[256,64]{0,1:T(8,128)S(1)} %get-tuple-element.306) | copy-start | bytes 196612
  53.1 234.4 %copy-start.23 = (f32[256,64]{0,1:T(8,128)}, f32[256,64]{0,1:T(8,128)S(1)}, u32[]{:S(2)}) copy-start(f32[256,64]{0,1:T(8,128)S(1)} %get-tuple-element.307) | copy-start | bytes 196612
  53.2 234.3 %copy-start.44 = (f32[64]{0:T(128)}, f32[64]{0:T(128)S(1)}, u32[]{:S(2)}) copy-start(f32[64]{0:T(128)S(1)} %get-tuple-element.297) | copy-start | bytes 772
  73.6 124.6 %all-gather.18.cloned.1.call-start = ((), (), s32[]{:S(2)}) async-start(), calls=%async_computation.20 | async-start | bytes 1966080 | tf_op jit(solution)/shard_map/all_gather | solution.py:125
  127.0 143.8 %all-gather.10.cloned.1.call-start = ((), (), s32[]{:S(2)}) async-start(), calls=%async_computation.16 | async-start | bytes 6488064 | tf_op jit(solution)/shard_map/all_gather | solution.py:79
  127.6 301.0 %all-gather.20.cloned.1.call-start = ((), (), s32[]{:S(2)}) async-start(), calls=%async_computation.21 | async-start | bytes 6488064 | tf_op jit(solution)/shard_map/all_gather | solution.py:83
  128.2 342.1 %all-gather.22.cloned.1.call-start = ((), (), s32[]{:S(2)}) async-start(), calls=%async_computation.22 | async-start | bytes 20545536 | tf_op jit(solution)/shard_map/all_gather | solution.py:87
  128.9 471.2 %all-gather.24.cloned.1.call-start = ((), (), s32[]{:S(2)}) async-start(), calls=%async_computation.23 | async-start | bytes 20545536 | tf_op jit(solution)/shard_map/all_gather | solution.py:88
  129.7 600.3 %all-gather.26.cloned.1.call-start = ((), (), s32[]{:S(2)}) async-start(), calls=%async_computation.24 | async-start | bytes 20545536 | tf_op jit(solution)/shard_map/all_gather | solution.py:89
  130.4 862.1 %reduce-scatter.17.cloned.1.call-start = ((), (), s32[]{:S(2)}) async-start(), calls=%async_computation.25 | async-start | bytes 1966080 | tf_op jit(solution)/shard_map/reduce_scatter | solution.py:264
  958.9 70.2 %reduce-scatter.19.cloned.1.call-start = ((), (), s32[]{:S(2)}) async-start(), calls=%async_computation.26 | async-start | bytes 1966080 | tf_op jit(solution)/shard_map/reduce_scatter | solution.py:267
  959.7 151.4 %reduce-scatter.25.cloned.1.call-start = ((), (), s32[]{:S(2)}) async-start(), calls=%async_computation.29 | async-start | bytes 1966080 | tf_op jit(solution)/shard_map/reduce_scatter | solution.py:320
  998.6 113.2 %reduce-scatter.29.cloned.1.call-start = ((), (), s32[]{:S(2)}) async-start(), calls=%async_computation.31 | async-start | bytes 1966080 | tf_op jit(solution)/shard_map/reduce_scatter | solution.py:323
  1033.2 182.1 %reduce-scatter.33.cloned.1.call-start = ((), (), s32[]{:S(2)}) async-start(), calls=%async_computation.33 | async-start | bytes 7864320 | tf_op jit(solution)/shard_map/reduce_scatter | solution.py:329
  1040.8 288.0 %reduce-scatter.21.cloned.1.call-start = ((), (), s32[]{:S(2)}) async-start(), calls=%async_computation.27 | async-start | bytes 7864320 | tf_op jit(solution)/shard_map/reduce_scatter | solution.py:317
  1059.8 601.4 %reduce-scatter.37.cloned.1.call-start = ((), (), s32[]{:S(2)}) async-start(), calls=%async_computation.35 | async-start | bytes 24903680 | tf_op jit(solution)/shard_map/reduce_scatter | solution.py:204
  1077.2 918.0 %reduce-scatter.41.cloned.1.call-start = ((), (), s32[]{:S(2)}) async-start(), calls=%async_computation.37 | async-start | bytes 24903680 | tf_op jit(solution)/shard_map/reduce_scatter | solution.py:207
  1093.4 1235.9 %reduce-scatter.45.cloned.1.call-start = ((), (), s32[]{:S(2)}) async-start(), calls=%async_computation.39 | async-start | bytes 24903680 | tf_op jit(solution)/shard_map/reduce_scatter | solution.py:210
  1111.0 1286.9 %reduce-scatter.27.cloned.1.call-start = ((), (), s32[]{:S(2)}) async-start(), calls=%async_computation.30 | async-start | bytes 442368 | tf_op jit(solution)/shard_map/reduce_scatter | solution.py:340
  1111.7 1293.5 %reduce-scatter.31.cloned.1.call-start = ((), (), s32[]{:S(2)}) async-start(), calls=%async_computation.32 | async-start | bytes 442368 | tf_op jit(solution)/shard_map/reduce_scatter | solution.py:343
  1112.3 1334.6 %reduce-scatter.35.cloned.1.call-start = ((), (), s32[]{:S(2)}) async-start(), calls=%async_computation.34 | async-start | bytes 1769472 | tf_op jit(solution)/shard_map/reduce_scatter | solution.py:349
  1215.4 1273.2 %reduce-scatter.23.cloned.1.call-start = ((), (), s32[]{:S(2)}) async-start(), calls=%async_computation.28 | async-start | bytes 1769472 | tf_op jit(solution)/shard_map/reduce_scatter | solution.py:337
  1328.8 1218.4 %reduce-scatter.39.cloned.1.call-start = ((), (), s32[]{:S(2)}) async-start(), calls=%async_computation.36 | async-start | bytes 5603328 | tf_op jit(solution)/shard_map/reduce_scatter | solution.py:218
  1661.3 944.4 %reduce-scatter.43.cloned.1.call-start = ((), (), s32[]{:S(2)}) async-start(), calls=%async_computation.38 | async-start | bytes 5603328 | tf_op jit(solution)/shard_map/reduce_scatter | solution.py:221
  1995.2 334.0 %copy-start.50 = (u32[32]{0:T(128)S(1)}, u32[32]{0:T(128)}, u32[]{:S(2)}) copy-start(u32[32]{0:T(128)} %constant.135) | copy-start | bytes 388
  1995.3 335.9 %copy-start.49 = (u32[32]{0:T(128)S(1)}, u32[32]{0:T(128)}, u32[]{:S(2)}) copy-start(u32[32]{0:T(128)} %constant.139) | copy-start | bytes 388
  1995.3 337.8 %copy-start.43 = (f32[1,2,2,128]{3,1,2,0:T(2,128)S(1)}, f32[1,2,2,128]{3,1,2,0:T(2,128)}, u32[]{:S(2)}) copy-start(f32[1,2,2,128]{3,1,2,0:T(2,128)} %copy-done.42) | copy-start | bytes 6148
  1995.3 337.8 %copy-start.28 = (bf16[192,8,2,256]{3,1,2,0:T(8,128)(2,1)S(1)}, bf16[192,8,2,256]{3,1,2,0:T(8,128)(2,1)}, u32[]{:S(2)}) copy-start(bf16[192,8,2,256]{3,1,2,0:T(8,128)(2,1)} %copy-done.27) | copy-start | bytes 4718596
  1995.3 669.0 %reduce-scatter.47.cloned.1.call-start = ((), (), s32[]{:S(2)}) async-start(), calls=%async_computation.40 | async-start | bytes 5603328 | tf_op jit(solution)/shard_map/reduce_scatter | solution.py:224
  (55 other events, 639.7 us)
Sparse Core Ops, SparseCore 0:
  10.9 55.1 all-gather.11
  68.9 53.8 all-gather.15
  124.9 35.4 all-gather.13
  162.3 35.9 all-gather.17
  201.0 69.7 all-gather.9
  273.5 67.6 all-gather.19
  344.0 126.1 all-gather.21
  473.1 126.9 all-gather.23
  602.9 126.9 all-gather.25
  959.0 33.4 reduce-scatter.16
  994.8 34.2 reduce-scatter.18
  1031.3 34.2 reduce-scatter.24
  1067.9 34.2 reduce-scatter.28
  1104.4 110.9 reduce-scatter.32
  1217.5 111.2 reduce-scatter.20
  1331.0 330.1 reduce-scatter.36
  1663.4 331.7 reduce-scatter.40
  1997.4 331.7 reduce-scatter.44
  2332.3 35.9 reduce-scatter.26
  2371.2 33.9 reduce-scatter.30
  2408.5 38.3 reduce-scatter.34
  2450.2 38.3 reduce-scatter.22
  2492.1 55.0 reduce-scatter.38
  2550.6 55.0 reduce-scatter.42
  2609.2 55.0 reduce-scatter.46
where the time goes:
time: 2680 us; the launch traced here: 2670 us
  waiting for transfers between devices  1980 us (74%)
  matrix products  418 us (16%)
  local copies, waits for them, and re-layouts  116 us (4%)
  other arithmetic  71.2 us (3%)
  blocking collectives  64.6 us (2%)
    reduce_scatter x1, waiting for transfers between devices, body(): lax.psum_scatter(ffn_grads[2].astype(jnp.bfloat16), 'inner', scatter_dime...  334 us
    reduce_scatter x1, waiting for transfers between devices, body(): lax.psum_scatter(ffn_grads[3].astype(jnp.bfloat16), 'inner', scatter_dime...  334 us
    reduce_scatter x1, waiting for transfers between devices, body(): lax.psum_scatter(ffn_grads[1].astype(jnp.bfloat16), 'inner', scatter_dime...  332 us
    dot_general x43, matrix products, right_t(): lax.dot_general(left, right, (((1,), (1,)), ((), ())), preferred_element_...  157 us
    dot_general x31, matrix products, matrix_product(): return jnp.dot(left, right, preferred_element_type=jnp.float32)  148 us
    reduce_scatter x1, waiting for transfers between devices, body(): lax.psum_scatter(attn_grads[1].astype(jnp.bfloat16), 'inner', scatter_dim...  113 us
    dot_general x31, matrix products, left_t(): lax.dot_general(left, right, (((0,), (0,)), ((), ())), preferred_element_...  113 us
    all_gather x1, waiting for transfers between devices, body(): lax.all_gather(w_down, ('inner', 'outer'), axis=0, tiled=True)  113 us
  transfers between devices with their start and end apart: 25, of which 21 were waited for; matrix products, arithmetic and copies ran while one was open for 13% of the time, Pallas kernels for 0%

commit v1 on v0

v1 whole, which is shorter than its diff:
```python
import jax
import jax.numpy as jnp
from jax import lax
from jax.sharding import Mesh, PartitionSpec as P

QUERY_HEADS = 24
KEY_VALUE_HEADS = 6
HEAD_SIZE = 64
BLOCK = 256
EPS = 1e-06
NEGATIVE = -1e30
ALL = ("inner", "plane", "core")
BF = jnp.bfloat16
F32 = jnp.float32


def mm(left, right):
    return jnp.dot(left, right, preferred_element_type=F32)


def mm_tn(left, right):
    return lax.dot_general(left, right, (((0,), (0,)), ((), ())), preferred_element_type=F32)


def mm_nt(left, right):
    return lax.dot_general(left, right, (((1,), (1,)), ((), ())), preferred_element_type=F32)


def rms_norm(v, gain):
    inverse = lax.rsqrt(jnp.mean(v * v, axis=-1, keepdims=True) + EPS)
    return v * inverse * gain, inverse


def rms_back(v, inverse, gain, grad):
    scaled = grad * gain
    back = inverse * scaled - v * inverse**3 * jnp.mean(scaled * v, axis=-1, keepdims=True)
    return back, grad * v * inverse


def rotary_apply(v, cosine, sine):
    half = HEAD_SIZE // 2
    turned = jnp.concatenate([-v[..., half:], v[..., :half]], axis=-1)
    return v * cosine + turned * sine


def rotary_back(grad, cosine, sine):
    half = HEAD_SIZE // 2
    times = grad * sine
    return grad * cosine + jnp.concatenate([times[..., half:], -times[..., :half]], axis=-1)


def make_body(n_inner, n_plane):
    n_dev = n_inner * n_plane * 2

    def core_swap(v):
        return lax.ppermute(v, "core", [(0, 1), (1, 0)])

    def flip(v, axis, size, bit):
        return lax.ppermute(v, axis, [(i, i ^ bit) for i in range(size)])

    def gather_inner(v, here):
        held = v[None]
        bit = n_inner // 2
        while bit:
            other = flip(held, "inner", n_inner, bit)
            high = (here & bit) != 0
            pair = jnp.stack([jnp.where(high, other, held), jnp.where(high, held, other)], axis=1)
            held = pair.reshape((-1,) + v.shape)
            bit //= 2
        return held

    def scatter_inner(v, here):
        held = v
        bit = 1
        while bit < n_inner:
            pair = held.reshape((held.shape[0] // 2, 2) + v.shape[1:])
            high = ((here & bit) != 0).astype(jnp.int32)
            keep = lax.dynamic_index_in_dim(pair, high, 1, keepdims=False)
            send = lax.dynamic_index_in_dim(pair, 1 - high, 1, keepdims=False)
            other = flip(send, "inner", n_inner, bit)
            held = keep.astype(F32) + other.astype(F32)
            bit *= 2
            if bit < n_inner:
                held = held.astype(BF)
        return held[0].astype(F32)

    def gather_ffn(rows, here):
        held = gather_inner(rows, here)
        whole = lax.all_gather(held, "plane", axis=1, tiled=True)
        return whole.reshape(-1, rows.shape[1])

    def scatter_ffn(whole, here):
        r = whole.shape[0] // (n_inner * n_plane)
        if r % 16:
            held = whole.reshape(n_inner, n_plane, r, whole.shape[1])
            part = lax.psum_scatter(held, "plane", scatter_dimension=1)
        else:
            held = whole.reshape(n_inner, n_plane * r, whole.shape[1])
            part = lax.psum_scatter(held, "plane", scatter_dimension=1, tiled=True)
        return scatter_inner(part, here)

    def butterfly_sum(v):
        for axis, size in (("core", 2), ("plane", n_plane), ("inner", n_inner)):
            bit = 1
            while bit < size:
                v = v + flip(v, axis, size, bit)
                bit *= 2
        return v

    def body(x_in, attn_gain, w_query, w_key, w_value, qk_gain, w_out, ffn_gain, w_gate, w_up, w_down, dy_in):
        here = lax.axis_index("inner")
        core = lax.axis_index("core")
        flat = (here * n_plane + lax.axis_index("plane")) * 2 + core
        seqs, span, width = x_in.shape
        rows = seqs * span
        groups = QUERY_HEADS // KEY_VALUE_HEADS
        scale = HEAD_SIZE ** (-0.5)
        length = span * n_inner
        q_width = w_query.shape[1]
        kv_width = w_key.shape[1]
        per = w_query.shape[0]
        half = w_gate.shape[1] // 2

        extra = jnp.zeros((per, 128), BF)
        extra = extra.at[:, 0].set(attn_gain).at[:, 1].set(ffn_gain)
        extra = extra.at[: qk_gain.shape[0], 2].set(qk_gain)
        packed = jnp.concatenate([w_query, w_key, w_value, extra], axis=1)
        packed = lax.all_gather(packed, ALL, axis=0, tiled=True)
        qkv_width = q_width + 2 * kv_width
        wqkv = packed[:, :qkv_width]
        tail = packed[:, qkv_width : qkv_width + 3].astype(F32)
        g_one = tail[:, 0]
        g_two = tail[:, 1]
        g_qk = tail[:, 2].reshape(n_dev, per)[:, : qk_gain.shape[0]].reshape(-1)
        g_query, g_key = g_qk[:HEAD_SIZE], g_qk[HEAD_SIZE:]
        wo = lax.all_gather(w_out, ALL, axis=0, tiled=True)

        def column_half(w):
            mine = lax.dynamic_slice_in_dim(w, core * half, half, axis=1)
            theirs = lax.dynamic_slice_in_dim(w, (1 - core) * half, half, axis=1)
            got = core_swap(theirs)
            return jnp.where(core == 0, jnp.concatenate([mine, got]), jnp.concatenate([got, mine]))

        spread = [(s, 2 * (s % (n_dev // 2)) + s // (n_dev // 2)) for s in range(n_dev)]
        wg = gather_ffn(column_half(w_gate), here)
        wu = gather_ffn(column_half(w_up), here)
        wd = gather_ffn(lax.ppermute(w_down, ALL, spread), here)

        dy = dy_in.reshape(rows, width)
        dy_both = jnp.concatenate([dy, core_swap(dy)])

        base = here * span
        positions = (base + jnp.arange(span)).astype(F32)
        freq = 10000.0 ** (-jnp.arange(HEAD_SIZE // 2, dtype=F32) * 2.0 / HEAD_SIZE)
        angle = positions[:, None] * freq[None, :]
        cosine = jnp.concatenate([jnp.cos(angle), jnp.cos(angle)], axis=-1)[None, :, None, :]
        sine = jnp.concatenate([jnp.sin(angle), jnp.sin(angle)], axis=-1)[None, :, None, :]
        x = x_in.reshape(rows, width).astype(F32)
        normed, inv_one = rms_norm(x, g_one)
        normed_b = normed.astype(BF)
        lin = mm(normed_b, wqkv)
        q_lin = lin[:, :q_width].reshape(seqs, span, QUERY_HEADS, HEAD_SIZE)
        k_lin = lin[:, q_width : q_width + kv_width].reshape(seqs, span, KEY_VALUE_HEADS, HEAD_SIZE)
        q_normed, inv_query = rms_norm(q_lin, g_query)
        k_normed, inv_key = rms_norm(k_lin, g_key)
        query = rotary_apply(q_normed, cosine, sine).astype(BF)
        key = rotary_apply(k_normed, cosine, sine).astype(BF).reshape(seqs, span, kv_width)
        value = lin[:, q_width + kv_width :].astype(BF).reshape(seqs, span, kv_width)
        kv = jnp.concatenate([key, value], axis=-1)
        row_block = (base + jnp.arange(groups * span) % span) // BLOCK
        allowed = (jnp.arange(length) // BLOCK)[None, :] <= row_block[:, None]

        def by_head(v):
            return v.reshape(span, KEY_VALUE_HEADS, groups, HEAD_SIZE).transpose(1, 2, 0, 3).reshape(
                KEY_VALUE_HEADS, groups * span, HEAD_SIZE
            )

        def by_token(v):
            return v.reshape(KEY_VALUE_HEADS, groups, span, HEAD_SIZE).transpose(2, 0, 1, 3).reshape(
                span, QUERY_HEADS * HEAD_SIZE
            )

        def scores_of(q, k):
            return jnp.where(allowed, mm_nt(q, k) * scale, NEGATIVE)

        def forward_block(triple):
            q, k, v = triple
            scores = scores_of(q, k)
            top = jnp.max(scores, axis=-1, keepdims=True)
            expo = jnp.exp(scores - top)
            total = jnp.sum(expo, axis=-1, keepdims=True)
            return mm((expo / total).astype(BF), v), (top + jnp.log(total))[:, 0]

        kept = []
        mixed = []
        for s in range(seqs):
            both = gather_inner(kv[s], here).reshape(length, 2, KEY_VALUE_HEADS, HEAD_SIZE)
            both = both.transpose(1, 2, 0, 3)
            q_heads = by_head(query[s])
            attended, lse = lax.map(forward_block, (q_heads, both[0], both[1]))
            kept.append((q_heads, both[0], both[1], lse))
            mixed.append(by_token(attended.astype(BF)))
        mixed = jnp.concatenate(mixed)

        resid = x + mm(mixed, wo)
        normed2, inv_two = rms_norm(resid, g_two)
        n2 = normed2.astype(BF)
        n2_both = jnp.concatenate([n2, core_swap(n2)])
        gate = mm(n2_both, wg)
        up = mm(n2_both, wu)
        sigma = jax.nn.sigmoid(gate)
        active = gate * sigma
        hidden = (active * up).astype(BF)
        theirs = core_swap(mm(hidden[rows:], wd).astype(BF))
        output = resid + (mm(hidden[:rows], wd) + theirs.astype(F32))
        result = output.astype(BF).reshape(seqs, span, width)

        grad_down = mm_tn(hidden, dy_both).astype(BF)
        d_down = lax.ppermute(
            scatter_ffn(grad_down, here).astype(BF), ALL, [(b, a) for a, b in spread]
        ).astype(F32)
        d_hidden = mm_nt(dy_both, wd)
        dg = (d_hidden * up * (sigma * (1.0 + gate * (1.0 - sigma)))).astype(BF)
        du = (d_hidden * active).astype(BF)

        def column_whole(part):
            pair = part.astype(BF).reshape(2, per, half)
            mine = lax.dynamic_index_in_dim(pair, core, 0, keepdims=False)
            got = core_swap(lax.dynamic_index_in_dim(pair, 1 - core, 0, keepdims=False))
            return jnp.where(
                core == 0,
                jnp.concatenate([mine, got], axis=1),
                jnp.concatenate([got, mine], axis=1),
            ).astype(F32)

        d_gate = column_whole(scatter_ffn(mm_tn(n2_both, dg).astype(BF), here))
        d_up = column_whole(scatter_ffn(mm_tn(n2_both, du).astype(BF), here))
        theirs = core_swap((mm_nt(dg[rows:], wg) + mm_nt(du[rows:], wu)).astype(BF))
        dn2 = mm_nt(dg[:rows], wg) + mm_nt(du[:rows], wu) + theirs.astype(F32)
        back_two, terms_two = rms_back(resid, inv_two, g_two, dn2)
        grad_gain_two = jnp.sum(terms_two, axis=0)
        d_resid = dy.astype(F32) + back_two

        def scatter_attn(whole):
            r = whole.shape[0] // n_dev
            held = whole.reshape(n_dev // 2, 2, r, -1)
            mine = lax.dynamic_index_in_dim(held, core, 1, keepdims=False)
            got = core_swap(lax.dynamic_index_in_dim(held, 1 - core, 1, keepdims=False))
            held = (mine.astype(F32) + got.astype(F32)).astype(BF)
            return scatter_ffn(held.reshape(whole.shape[0] // 2, -1), here)

        drb = d_resid.astype(BF)
        d_out = scatter_attn(mm_tn(mixed, drb).astype(BF))
        dm = mm_nt(drb, wo).astype(BF).reshape(seqs, span, -1)

        def backward_block(quintet):
            q, k, v, d, lse = quintet
            prob = jnp.exp(scores_of(q, k) - lse[:, None])
            d_prob = mm_nt(d, v)
            ds = (prob * (d_prob - jnp.sum(prob * d_prob, axis=-1, keepdims=True))).astype(BF)
            return mm(ds, k) * scale, mm_tn(ds, q) * scale, mm_tn(prob.astype(BF), d)

        dq = []
        dkv = []
        for s in range(seqs):
            q_heads, k_heads, v_heads, lse = kept[s]
            dq_s, dk_s, dv_s = lax.map(
                backward_block, (q_heads, k_heads, v_heads, by_head(dm[s]), lse)
            )
            dq.append(by_token(dq_s))
            both = jnp.stack([dk_s, dv_s]).astype(BF).transpose(2, 0, 1, 3)
            dkv.append(scatter_inner(both.reshape(n_inner, span, 2 * kv_width), here))
        dq = jnp.stack(dq).reshape(seqs, span, QUERY_HEADS, HEAD_SIZE)
        dkv = jnp.stack(dkv)
        dk = dkv[..., :kv_width].reshape(seqs, span, KEY_VALUE_HEADS, HEAD_SIZE)
        dv = dkv[..., kv_width:].reshape(rows, kv_width)
        back_query, terms_query = rms_back(q_lin, inv_query, g_query, rotary_back(dq, cosine, sine))
        back_key, terms_key = rms_back(k_lin, inv_key, g_key, rotary_back(dk, cosine, sine))
        grad_qk = jnp.concatenate(
            [jnp.sum(terms_query, axis=(0, 1, 2)), jnp.sum(terms_key, axis=(0, 1, 2))]
        )
        d_lin = jnp.concatenate(
            [back_query.reshape(rows, -1), back_key.reshape(rows, -1), dv], axis=1
        ).astype(BF)
        d_qkv = scatter_attn(mm_tn(normed_b, d_lin).astype(BF))
        dn = mm_nt(d_lin, wqkv)
        back_one, terms_one = rms_back(x, inv_one, g_one, dn)
        grad_gain_one = jnp.sum(terms_one, axis=0)
        d_inputs = (d_resid + back_one).reshape(seqs, span, width)

        gains = butterfly_sum(jnp.concatenate([grad_gain_one, grad_gain_two, grad_qk]))
        d_attn_gain = lax.dynamic_slice_in_dim(gains, flat * per, per)
        d_ffn_gain = lax.dynamic_slice_in_dim(gains, width + flat * per, per)
        n_qk = qk_gain.shape[0]
        d_qk = lax.dynamic_slice_in_dim(gains, 2 * width + flat * n_qk, n_qk)
        return (
            result,
            d_inputs,
            d_attn_gain,
            d_qkv[:, :q_width],
            d_qkv[:, q_width : q_width + kv_width],
            d_qkv[:, q_width + kv_width :],
            d_qk,
            d_out,
            d_ffn_gain,
            d_gate,
            d_up,
            d_down,
        )

    return body


def solution(mesh):
    n_inner = mesh.shape["inner"]
    n_plane = mesh.shape["outer"] // 2
    fine = Mesh(mesh.devices.reshape(n_inner, n_plane, 2), ALL)
    tokens = P(("plane", "core"), "inner", None)
    vec = P(ALL)
    mat = P(ALL, None)
    return jax.shard_map(
        make_body(n_inner, n_plane),
        mesh=fine,
        in_specs=(tokens, vec, mat, mat, mat, vec, mat, vec, mat, mat, mat, tokens),
        out_specs=(tokens, tokens, vec, mat, mat, mat, vec, mat, vec, mat, mat, mat),
        check_vma=False,
    )
```

time: 2680 us -> 1510 us (0.56)
  waiting for transfers between devices: 1980 us -> 631 us
  local copies, waits for them, and re-layouts: 116 us -> 245 us
  starting transfers between devices: 0.99 us -> 67.9 us
  blocking collectives: 64.6 us -> 0 us
  other arithmetic: 71.2 us -> 129 us
    reduce_scatter x16 -> x4, waiting for transfers between devices: 1540 us -> 197 us  [scatter_ffn(): part = lax.psum_scatter(held, 'plane', scatter_dimension=1, tiled=True)]
    all_gather x9 -> x5, waiting for transfers between devices: 442 us -> 0.04 us  [the longest x1 0.02 us: body(): wo = lax.all_gather(w_out, ALL, axis=0, tiled=True)]
    ppermute x0 -> x41, waiting for transfers between devices: none -> 391 us  [the longest x29 350 us: flip(): return lax.ppermute(v, axis, [(i, i ^ bit) for i in range(size)])]
    ppermute x0 -> x41, starting transfers between devices: none -> 67.5 us  [the longest x29 59.8 us: flip(): return lax.ppermute(v, axis, [(i, i ^ bit) for i in range(size)])]
    unnamed x3 -> x0, blocking collectives: 64.6 us -> none
    unnamed x25 -> x11, waiting for transfers between devices: 6.6 us -> 42.8 us
    dot_general x105 -> x102, matrix products: 418 us -> 400 us  [the longest x43 150 us: mm_nt(): lax.dot_general(left, right, (((1,), (1,)), ((), ())), preferred_element_...]
  transfers between devices with their start and end apart: 25 -> 51, of which waited for: 21 -> 29; matrix products, arithmetic and copies ran while one was open for 13% -> 44% of each run, Pallas kernels for 0% -> 0%
where the time goes in v1:
time: 1510 us; the launch traced here: 1490 us
  waiting for transfers between devices  631 us (42%)
  matrix products  400 us (26%)
  local copies, waits for them, and re-layouts  245 us (16%)
  other arithmetic  129 us (9%)
  starting transfers between devices  67.9 us (4%)
  between operations  16.1 us (1%)
    ppermute x29, waiting for transfers between devices, flip(): return lax.ppermute(v, axis, [(i, i ^ bit) for i in range(size)])  350 us
    reduce_scatter x4, waiting for transfers between devices, scatter_ffn(): part = lax.psum_scatter(held, 'plane', scatter_dimension=1, tiled=True)  197 us
    dot_general x43, matrix products, mm_nt(): lax.dot_general(left, right, (((1,), (1,)), ((), ())), preferred_element_...  150 us
    dot_general x30, matrix products, mm(): return jnp.dot(left, right, preferred_element_type=F32)  147 us
    dot_general x29, matrix products, mm_tn(): lax.dot_general(left, right, (((0,), (0,)), ((), ())), preferred_element_...  104 us
    ppermute x29, starting transfers between devices, flip(): return lax.ppermute(v, axis, [(i, i ^ bit) for i in range(size)])  59.8 us
    unnamed x178, local copies, waits for them, and re-layouts  47.5 us
    unnamed x11, waiting for transfers between devices  42.8 us
  transfers between devices with their start and end apart: 51, of which 29 were waited for; matrix products, arithmetic and copies ran while one was open for 44% of the time, Pallas kernels for 0%

profile of v1, /device:TPU:12, one launch (start us, length us, event | category | flops | bytes accessed | tf_op | source)
XLA Modules:
  0.0 1491.0 jit_solution(1504587340024140402)
XLA Ops:
  24.8 33.5 %collective-permute-done.9 = bf16[1,128,2432]{2,1,0:T(8,128)(2,1)S(1)} collective-permute-done((bf16[1,128,2432]{2,1,0:T(8,128)(2,1)S(1)}, bf16[1,128,2432]{2,1,0:T(8,128)(2,1)S(1)}, u32[]{:S(2)}, u32[]{:S(2)}) %collective-permute-start.9) | collective-permute-done | bytes 622624 | tf_op jit(solution)/shard_map/ppermute | solution.py:59
  60.9 42.3 %collective-permute-done.10 = bf16[2,128,2432]{2,1,0:T(8,128)(2,1)S(1)} collective-permute-done((bf16[2,128,2432]{2,1,0:T(8,128)(2,1)}, bf16[2,128,2432]{2,1,0:T(8,128)(2,1)S(1)}, u32[]{:S(2)}, u32[]{:S(2)}) %collective-permute-start.10) | collective-permute-done | bytes 1245216 | tf_op jit(solution)/shard_map/ppermute | solution.py:59
  116.2 38.2 %collective-permute-done.6 = bf16[1,128,2432]{2,1,0:T(8,128)(2,1)S(1)} collective-permute-done((bf16[1,128,2432]{2,1,0:T(8,128)(2,1)S(1)}, bf16[1,128,2432]{2,1,0:T(8,128)(2,1)S(1)}, u32[]{:S(2)}, u32[]{:S(2)}) %collective-permute-start.6) | collective-permute-done | bytes 622624 | tf_op jit(solution)/shard_map/ppermute | solution.py:59
  158.2 39.5 %collective-permute-done.7 = bf16[2,128,2432]{2,1,0:T(8,128)(2,1)S(1)} collective-permute-done((bf16[2,128,2432]{2,1,0:T(8,128)(2,1)S(1)}, bf16[2,128,2432]{2,1,0:T(8,128)(2,1)S(1)}, u32[]{:S(2)}, u32[]{:S(2)}) %collective-permute-start.7) | collective-permute-done | bytes 1245216 | tf_op jit(solution)/shard_map/ppermute | solution.py:59
  204.0 26.3 %collective-permute-done.11 = bf16[152,2048]{1,0:T(8,128)(2,1)S(1)} collective-permute-done((bf16[152,2048]{1,0:T(8,128)(2,1)S(1)}, bf16[152,2048]{1,0:T(8,128)(2,1)S(1)}, u32[]{:S(2)}, u32[]{:S(2)}) %collective-permute-start.11) | collective-permute-done | bytes 622624 | tf_op jit(solution)/shard_map/ppermute | solution.py:147
  236.3 25.5 %collective-permute-done.12 = bf16[1,152,2048]{2,1,0:T(8,128)(2,1)S(1)} collective-permute-done((bf16[1,152,2048]{2,1,0:T(8,128)(2,1)S(1)}, bf16[1,152,2048]{2,1,0:T(8,128)(2,1)S(1)}, u32[]{:S(2)}, u32[]{:S(2)}) %collective-permute-start.12) | collective-permute-done | bytes 622624 | tf_op jit(solution)/shard_map/ppermute | solution.py:59
  269.4 25.2 %collective-permute-done.13 = bf16[2,152,2048]{2,1,0:T(8,128)(2,1)} collective-permute-done((bf16[2,152,2048]{2,1,0:T(8,128)(2,1)}, bf16[2,152,2048]{2,1,0:T(8,128)(2,1)}, u32[]{:S(2)}, u32[]{:S(2)}) %collective-permute-start.13) | collective-permute-done | bytes 1245216 | tf_op jit(solution)/shard_map/ppermute | solution.py:59
  347.5 9.2 collective-permute-done
  396.4 60.7 %while.59 = (s32[]{:T(128)}, bf16[6,1024,64]{1,2,0:T(8,128)(2,1)}, f32[6,1024]{1,0:T(8,128)}, bf16[6,1024,64]{2,1,0:T(8,128)(2,1)S(1)}, bf16[6,1024,64]{2,1,0:T(...) while((s32[]{:T(128)}, bf16[6,1024,64]{1,2,0:T(8,128)(2,1)}, ...), condition=%wide.region_9.10_spmd.clone, body=%wide.region_6.9_spmd.clone.sunk | while | flops 284163072 | bytes 30492832 | solution.py:200
  473.1 51.8 %while.60 = (s32[]{:T(128)}, bf16[6,1024,64]{1,2,0:T(8,128)(2,1)S(1)}, f32[6,1024]{1,0:T(8,128)S(1)}, bf16[6,1024,64]{2,1,0:T(8,128)(2,1)}, bf16[6,1024,64]{2,1,...) while((s32[]{:T(128)}, ...), condition=%wide.region_13.14_spmd.clone, body=%wide.region_10.13_spmd.clone.sunk | while | flops 284163072 | bytes 30476420 | solution.py:200
  540.2 16.5 %fusion.175 = f32[1024,2432]{1,0:T(8,128)} fusion(bf16[2048,2432]{1,0:T(8,128)(2,1)} %bitcast.647, bf16[512,2048]{1,0:T(8,128)(2,1)} %collective-permute-done.4, bf16[512,2048]{1,0:T(8,128)(2,1)S(1)} %multiply_convert_fusion.5), kind=kOutput, calls=%fused_computation.368 | convolution fusion | flops 10208935936 | bytes 24117248 | tf_op jit(solution)/shard_map/dot_general | solution.py:18
  556.7 16.7 %fusion.176 = f32[1024,2432]{1,0:T(8,128)} fusion(bf16[2048,2432]{1,0:T(8,128)(2,1)} %bitcast.650, bf16[512,2048]{1,0:T(8,128)(2,1)} %collective-permute-done.4, bf16[512,2048]{1,0:T(8,128)(2,1)S(1)} %multiply_convert_fusion.5), kind=kOutput, calls=%fused_computation.369 | convolution fusion | flops 10208935936 | bytes 24117248 | tf_op jit(solution)/shard_map/dot_general | solution.py:18
  573.4 22.6 %multiply_convert_fusion.2 = (bf16[1024,2432]{1,0:T(8,128)(2,1)}, bf16[1024,2432]{1,0:T(8,128)(2,1)}, bf16[1024,2432]{1,0:T(8,128)(2,1)}) fusion(f32[1024,2432]{1,0:T(8,128)} %fusion.176, f32[1024,2432]{1,0:T(8,128)} %fusion.175, bf16[2432,2048]{1,0:T(8,128)(2,1)} %bitcast.644, bf16[512,2048]{1,0:T(8,128)(2,1)} %collective-permute-done.15, ...), kind=kOutput, calls=%fused_computation.116 | convolution fusion | flops 10246291456 | bytes 49020928 | tf_op jit(solution)/shard_map/dot_general | solution.py:26
  605.2 10.9 add_convert_fusion
  635.9 11.5 fusion.127
  647.4 13.9 multiply_reduce_fusion.2
  682.3 73.1 %while.61 = (s32[]{:T(128)}, f32[6,1024,64]{1,2,0:T(8,128)}, bf16[6,1024,64]{1,2,0:T(8,128)(2,1)}, bf16[6,1024,64]{1,2,0:T(8,128)(2,1)}, bf16[6,1024,64]{2,1,0:T...) while((s32[]{:T(128)}, f32[6,1024,64]{1,2,0:T(8,128)}, ...), condition=%wide.region_18.19_spmd.clone, body=%wide.region_16.18_spmd.clone.sunk | while | flops 681704448 | bytes 34112632 | solution.py:267
  767.6 71.6 %while.62 = (s32[]{:T(128)}, f32[6,1024,64]{1,2,0:T(8,128)}, bf16[6,1024,64]{1,2,0:T(8,128)(2,1)S(1)}, bf16[6,1024,64]{1,2,0:T(8,128)(2,1)S(1)}, bf16[6,1024,64]...) while((s32[]{:T(128)}, f32[6,1024,64]{1,2,0:T(8,128)}, ...), condition=%wide.region_21.22_spmd.clone, body=%wide.region_19.21_spmd.clone.sunk | while | flops 681704448 | bytes 34112632 | solution.py:267
  928.9 15.7 %collective-permute-done.18 = bf16[1,256,768]{2,1,0:T(8,128)(2,1)S(1)} collective-permute-done((bf16[1,256,768]{2,1,0:T(8,128)(2,1)S(1)}, bf16[1,256,768]{2,1,0:T(8,128)(2,1)S(1)}, u32[]{:S(2)}, u32[]{:S(2)}) %collective-permute-start.18) | collective-permute-done | bytes 393248 | tf_op jit(solution)/shard_map/ppermute | solution.py:59
  993.5 16.3 %convolution_convert_fusion = bf16[2432,2048]{1,0:T(8,128)(2,1)} fusion(bf16[1024,2432]{1,0:T(8,128)(2,1)} %get-tuple-element.657, bf16[512,2048]{1,0:T(8,128)(2,1)} %collective-permute-done.15, bf16[512,2048]{1,0:T(8,128)(2,1)} %bitcast.63), kind=kOutput, calls=%fused_computation.112 | convolution fusion | flops 10213916672 | bytes 19136512 | tf_op jit(solution)/shard_map/dot_general | solution.py:22
  1009.7 9.8 copy.367
  1021.1 16.4 %convolution_convert_fusion.1 = bf16[2048,2432]{1,0:T(8,128)(2,1)} fusion(bf16[1024,2432]{1,0:T(8,128)(2,1)} %get-tuple-element.655, bf16[512,2048]{1,0:T(8,128)(2,1)} %collective-permute-done.4, bf16[512,2048]{1,0:T(8,128)(2,1)S(1)} %copy-done.39), kind=kOutput, calls=%fused_computation.113 | convolution fusion | flops 10213916672 | bytes 19136512 | tf_op jit(solution)/shard_map/dot_general | solution.py:22
  1037.6 16.4 %convolution_convert_fusion.2 = bf16[2048,2432]{1,0:T(8,128)(2,1)} fusion(bf16[1024,2432]{1,0:T(8,128)(2,1)} %get-tuple-element.656, bf16[512,2048]{1,0:T(8,128)(2,1)} %collective-permute-done.4, bf16[512,2048]{1,0:T(8,128)(2,1)S(1)} %copy-done.39), kind=kOutput, calls=%fused_computation.114 | convolution fusion | flops 10213916672 | bytes 19136512 | tf_op jit(solution)/shard_map/dot_general | solution.py:22
  1054.1 11.2 convolution_convert_fusion.6
  1065.5 11.7 fusion.119
  1082.8 13.6 add_convert_fusion.1
  1138.7 42.0 %reduce-scatter.16.cloned.1.call-done = bf16[4,1,152,2048]{3,2,0,1:T(8,128)(2,1)} async-done(((bf16[4,4,152,2048]{3,2,0,1:T(8,128)(2,1)}), bf16[4,1,152,2048]{3,2,0,1:T(8,128)(2,1)}) %reduce-scatter.16.cloned.1.call-update) | async-done | bytes 2490384
  1184.5 98.5 %reduce-scatter.14.cloned.1.call-done = bf16[4,128,2432]{2,1,0:T(8,128)(2,1)} async-done(((bf16[4,512,2432]{2,1,0:T(8,128)(2,1)}), bf16[4,128,2432]{2,1,0:T(8,128)(2,1)}) %reduce-scatter.14.cloned.1.call-update) | async-done | bytes 2490384 | tf_op jit(solution)/shard_map/reduce_scatter | solution.py:99
  1286.6 98.5 %reduce-scatter.12.cloned.1.call-done = bf16[4,128,2432]{2,1,0:T(8,128)(2,1)} async-done(((bf16[4,512,2432]{2,1,0:T(8,128)(2,1)}), bf16[4,128,2432]{2,1,0:T(8,128)(2,1)}) %reduce-scatter.12.cloned.1.call-update) | async-done | bytes 2490384 | tf_op jit(solution)/shard_map/reduce_scatter | solution.py:99
  1394.0 44.3 %collective-permute-done.32 = bf16[2,128,2432]{2,1,0:T(8,128)(2,1)S(1)} collective-permute-done((bf16[2,128,2432]{2,1,0:T(8,128)(2,1)S(1)}, bf16[2,128,2432]{2,1,0:T(8,128)(2,1)S(1)}, u32[]{:S(2)}, u32[]{:S(2)}) %collective-permute-start.32) | collective-permute-done | bytes 1245216 | tf_op jit(solution)/shard_map/ppermute | solution.py:59
  1444.3 21.8 %collective-permute-done.36 = bf16[1,128,2432]{2,1,0:T(8,128)(2,1)S(1)} collective-permute-done((bf16[1,128,2432]{2,1,0:T(8,128)(2,1)S(1)}, bf16[1,128,2432]{2,1,0:T(8,128)(2,1)S(1)}, u32[]{:S(2)}, u32[]{:S(2)}) %collective-permute-start.36) | collective-permute-done | bytes 622624 | tf_op jit(solution)/shard_map/ppermute | solution.py:59
  1466.4 13.1 collective-permute-done.33
  (659 shorter events, 712.4 us)
Async XLA Ops:
  7.2 290.7 %all-gather.6.cloned.1.call-start = ((), (), s32[]{:S(2)}) async-start(), calls=%async_computation.5 | async-start | bytes 10272768 | tf_op jit(solution)/shard_map/all_gather | solution.py:128
  18.4 509.3 %all-gather.8.cloned.1.call-start = ((), (), s32[]{:S(2)}) async-start(), calls=%async_computation.6 | async-start | bytes 6488064 | tf_op jit(solution)/shard_map/all_gather | solution.py:136
  19.2 517.3 %all-gather.12.cloned.1.call-start = ((), (), s32[]{:S(2)}) async-start(), calls=%async_computation.8 | async-start | bytes 12451840 | tf_op jit(solution)/shard_map/all_gather | solution.py:89
  22.1 36.2 %collective-permute-start.9 = (bf16[1,128,2432]{2,1,0:T(8,128)(2,1)S(1)}, bf16[1,128,2432]{2,1,0:T(8,128)(2,1)S(1)}, u32[]{:S(2)}, u32[]{:S(2)}) collective-permute-start(bf16[1,128,2432]{2,1,0:T(8,128)(2,1)S(1)} %maximum_select_fusion.1), channel_id=1, source_target_pairs={{0,16},{8,24},{16,0},{24,8},{1,17},{9,25},{17,1},{25,9},{2,18},{10... | collective-permute-start | bytes 1867784 | tf_op jit(solution)/shard_map/ppermute | solution.py:59
  59.5 43.6 %collective-permute-start.10 = (bf16[2,128,2432]{2,1,0:T(8,128)(2,1)}, bf16[2,128,2432]{2,1,0:T(8,128)(2,1)S(1)}, u32[]{:S(2)}, u32[]{:S(2)}) collective-permute-start(bf16[2,128,2432]{2,1,0:T(8,128)(2,1)} %maximum_bitcast_fusion.3), channel_id=1, source_target_pairs={{0,8},{8,0},{16,24},{24,16},{1,9},{9,1},{17,25},{25,17},{2,10},{10... | collective-permute-start | bytes 3735560 | tf_op jit(solution)/shard_map/ppermute | solution.py:59
  105.3 451.4 %all-gather.10.cloned.1.call-start = ((), (), s32[]{:S(2)}) async-start(), calls=%async_computation.7 | async-start | bytes 12451840 | tf_op jit(solution)/shard_map/all_gather | solution.py:89
  107.2 47.2 %collective-permute-start.6 = (bf16[1,128,2432]{2,1,0:T(8,128)(2,1)S(1)}, bf16[1,128,2432]{2,1,0:T(8,128)(2,1)S(1)}, u32[]{:S(2)}, u32[]{:S(2)}) collective-permute-start(bf16[1,128,2432]{2,1,0:T(8,128)(2,1)S(1)} %maximum_select_fusion), channel_id=1, source_target_pairs={{0,16},{8,24},{16,0},{24,8},{1,17},{9,25},{17,1},{25,9},{2,18},{10... | collective-permute-start | bytes 1867784 | tf_op jit(solution)/shard_map/ppermute | solution.py:59
  154.7 43.0 %collective-permute-start.7 = (bf16[2,128,2432]{2,1,0:T(8,128)(2,1)S(1)}, bf16[2,128,2432]{2,1,0:T(8,128)(2,1)S(1)}, u32[]{:S(2)}, u32[]{:S(2)}) collective-permute-start(bf16[2,128,2432]{2,1,0:T(8,128)(2,1)S(1)} %maximum_bitcast_fusion.2), channel_id=1, source_target_pairs={{0,8},{8,0},{16,24},{24,16},{1,9},{9,1},{17,25},{25,17},{2,10},{10... | collective-permute-start | bytes 3735560 | tf_op jit(solution)/shard_map/ppermute | solution.py:59
  199.7 373.7 %all-gather.14.cloned.1.call-start = ((), (), s32[]{:S(2)}) async-start(), calls=%async_computation.9 | async-start | bytes 12451840 | tf_op jit(solution)/shard_map/all_gather | solution.py:89
  230.3 31.6 %collective-permute-start.12 = (bf16[1,152,2048]{2,1,0:T(8,128)(2,1)S(1)}, bf16[1,152,2048]{2,1,0:T(8,128)(2,1)S(1)}, u32[]{:S(2)}, u32[]{:S(2)}) collective-permute-start(bf16[1,152,2048]{2,1,0:T(8,128)(2,1)S(1)} %bitcast.631), channel_id=1, source_target_pairs={{0,16},{8,24},{16,0},{24,8},{1,17},{9,25},{17,1},{25,9},{2,18},{10... | collective-permute-start | bytes 1867784 | tf_op jit(solution)/shard_map/ppermute | solution.py:59
  263.1 31.5 %collective-permute-start.13 = (bf16[2,152,2048]{2,1,0:T(8,128)(2,1)}, bf16[2,152,2048]{2,1,0:T(8,128)(2,1)}, u32[]{:S(2)}, u32[]{:S(2)}) collective-permute-start(bf16[2,152,2048]{2,1,0:T(8,128)(2,1)} %maximum_bitcast_fusion.4), channel_id=1, source_target_pairs={{0,8},{8,0},{16,24},{24,16},{1,9},{9,1},{17,25},{25,17},{2,10},{10... | collective-permute-start | bytes 3735560 | tf_op jit(solution)/shard_map/ppermute | solution.py:59
  297.8 809.8 %reduce-scatter.10.cloned.1.call-start = ((), (), s32[]{:S(2)}) async-start(), calls=%async_computation.11 | async-start | bytes 3932160 | tf_op jit(solution)/shard_map/reduce_scatter | solution.py:99
  342.1 31.2 %collective-permute-start.2 = (bf16[1,256,768]{1,2,0:T(8,128)(2,1)}, bf16[1,256,768]{1,2,0:T(8,128)(2,1)}, u32[]{:S(2)}, u32[]{:S(2)}) collective-permute-start(bf16[1,256,768]{1,2,0:T(8,128)(2,1)} %get-tuple-element.707), channel_id=1, source_target_pairs={{0,16},{8,24},{16,0},{24,8},{1,17},{9,25},{17,1},{25,9},{2,18},{10... | collective-permute-start | bytes 1179656 | tf_op jit(solution)/shard_map/ppermute | solution.py:59
  375.6 86.8 %collective-permute-start.3 = (bf16[2,256,768]{1,2,0:T(8,128)(2,1)}, bf16[2,256,768]{1,2,0:T(8,128)(2,1)}, u32[]{:S(2)}, u32[]{:S(2)}) collective-permute-start(bf16[2,256,768]{1,2,0:T(8,128)(2,1)} %maximum_bitcast_fusion.6), channel_id=1, source_target_pairs={{0,8},{8,0},{16,24},{24,16},{1,9},{9,1},{17,25},{25,17},{2,10},{10... | collective-permute-start | bytes 2359304 | tf_op jit(solution)/shard_map/ppermute | solution.py:59
  535.9 37.5 %collective-permute-start.15 = (bf16[512,2048]{1,0:T(8,128)(2,1)}, bf16[512,2048]{1,0:T(8,128)(2,1)}, u32[]{:S(2)}, u32[]{:S(2)}) collective-permute-start(bf16[512,2048]{1,0:T(8,128)(2,1)} %bitcast.63), channel_id=1, source_target_pairs={{0,1},{1,0},{2,3},{3,2},{4,5},{5,4},{6,7},{7,6},{8,9},{9,8},{10,11... | collective-permute-start | bytes 6291464 | tf_op jit(solution)/shard_map/ppermute | solution.py:56
  616.2 31.2 %collective-permute-start.16 = (bf16[512,2048]{1,0:T(8,128)(2,1)}, bf16[512,2048]{1,0:T(8,128)(2,1)}, u32[]{:S(2)}, u32[]{:S(2)}) collective-permute-start(bf16[512,2048]{1,0:T(8,128)(2,1)} %add_convert_fusion), channel_id=1, source_target_pairs={{0,1},{1,0},{2,3},{3,2},{4,5},{5,4},{6,7},{7,6},{8,9},{9,8},{10,11... | collective-permute-start | bytes 6291464 | tf_op jit(solution)/shard_map/ppermute | solution.py:56
  673.2 293.7 %collective-permute-start.29 = (bf16[16,48,2048]{2,1,0:T(8,128)(2,1)}, bf16[16,48,2048]{2,1,0:T(8,128)(2,1)}, u32[]{:S(2)}, u32[]{:S(2)}) collective-permute-start(bf16[16,48,2048]{2,1,0:T(8,128)(2,1)} %dynamic-slice_bitcast_fusion.1), channel_id=1, source_target_pairs={{0,1},{1,0},{2,3},{3,2},{4,5},{5,4},{6,7},{7,6},{8,9},{9,8},{10,11... | collective-permute-start | bytes 9437192 | tf_op jit(solution)/shard_map/ppermute | solution.py:56
  868.8 47.7 %collective-permute-start.17 = (bf16[2,256,768]{2,1,0:T(8,128)(2,1)}, bf16[2,256,768]{2,1,0:T(8,128)(2,1)}, u32[]{:S(2)}, u32[]{:S(2)}) collective-permute-start(bf16[2,256,768]{2,1,0:T(8,128)(2,1)} %bitcast.76), channel_id=1, source_target_pairs={{0,8},{8,0},{16,24},{24,16},{1,9},{9,1},{17,25},{25,17},{2,10},{10... | collective-permute-start | bytes 2359304 | tf_op jit(solution)/shard_map/ppermute | solution.py:59
  886.4 31.9 %collective-permute-start.19 = (bf16[2,256,768]{2,1,0:T(8,128)(2,1)}, bf16[2,256,768]{2,1,0:T(8,128)(2,1)}, u32[]{:S(2)}, u32[]{:S(2)}) collective-permute-start(bf16[2,256,768]{2,1,0:T(8,128)(2,1)} %bitcast.630), channel_id=1, source_target_pairs={{0,8},{8,0},{16,24},{24,16},{1,9},{9,1},{17,25},{25,17},{2,10},{10... | collective-permute-start | bytes 2359304 | tf_op jit(solution)/shard_map/ppermute | solution.py:59
  920.4 31.9 %collective-permute-start.20 = (bf16[1,256,768]{2,1,0:T(8,128)(2,1)S(1)}, bf16[1,256,768]{2,1,0:T(8,128)(2,1)S(1)}, u32[]{:S(2)}, u32[]{:S(2)}) collective-permute-start(bf16[1,256,768]{2,1,0:T(8,128)(2,1)S(1)} %constant_dynamic-slice_fusion.7), channel_id=1, source_target_pairs={{0,16},{8,24},{16,0},{24,8},{1,17},{9,25},{17,1},{25,9},{2,18},{10... | collective-permute-start | bytes 1179656 | tf_op jit(solution)/shard_map/ppermute | solution.py:59
  973.0 138.9 %reduce-scatter.8.cloned.1.call-start = ((), (), s32[]{:S(2)}) async-start(), calls=%async_computation.10 | async-start | bytes 5898240 | tf_op jit(solution)/shard_map/reduce_scatter | solution.py:99
  993.4 187.2 %reduce-scatter.16.cloned.1.call-start = ((), (), s32[]{:S(2)}) async-start(), calls=%async_computation.14 | async-start | bytes 12451840
  1019.5 263.5 %reduce-scatter.14.cloned.1.call-start = ((), (), s32[]{:S(2)}) async-start(), calls=%async_computation.13 | async-start | bytes 12451840 | tf_op jit(solution)/shard_map/reduce_scatter | solution.py:99
  1037.5 347.6 %reduce-scatter.12.cloned.1.call-start = ((), (), s32[]{:S(2)}) async-start(), calls=%async_computation.12 | async-start | bytes 12451840 | tf_op jit(solution)/shard_map/reduce_scatter | solution.py:99
  1134.3 49.3 %collective-permute-start.28 = (bf16[1,64,2304]{2,1,0:T(8,128)(2,1)S(1)}, bf16[1,64,2304]{2,1,0:T(8,128)(2,1)S(1)}, u32[]{:S(2)}, u32[]{:S(2)}) collective-permute-start(bf16[1,64,2304]{2,1,0:T(8,128)(2,1)S(1)} %constant_dynamic-slice_fusion.6), channel_id=1, source_target_pairs={{0,16},{8,24},{16,0},{24,8},{1,17},{9,25},{17,1},{25,9},{2,18},{10... | collective-permute-start | bytes 884744 | tf_op jit(solution)/shard_map/ppermute | solution.py:59
  1183.1 204.2 %collective-permute-start.38 = (bf16[2,152,2048]{2,1,0:T(8,128)(2,1)}, bf16[2,152,2048]{2,1,0:T(8,128)(2,1)}, u32[]{:S(2)}, u32[]{:S(2)}) collective-permute-start(bf16[2,152,2048]{2,1,0:T(8,128)(2,1)} %dynamic-slice_bitcast_fusion.2), channel_id=1, source_target_pairs={{0,8},{8,0},{16,24},{24,16},{1,9},{9,1},{17,25},{25,17},{2,10},{10... | collective-permute-start | bytes 3735560 | tf_op jit(solution)/shard_map/ppermute | solution.py:59
  1285.4 106.2 %collective-permute-start.35 = (bf16[2,128,2432]{2,1,0:T(8,128)(2,1)}, bf16[2,128,2432]{2,1,0:T(8,128)(2,1)}, u32[]{:S(2)}, u32[]{:S(2)}) collective-permute-start(bf16[2,128,2432]{2,1,0:T(8,128)(2,1)} %dynamic-slice_bitcast_fusion.3), channel_id=1, source_target_pairs={{0,8},{8,0},{16,24},{24,16},{1,9},{9,1},{17,25},{25,17},{2,10},{10... | collective-permute-start | bytes 3735560 | tf_op jit(solution)/shard_map/ppermute | solution.py:59
  1386.7 51.6 %collective-permute-start.32 = (bf16[2,128,2432]{2,1,0:T(8,128)(2,1)S(1)}, bf16[2,128,2432]{2,1,0:T(8,128)(2,1)S(1)}, u32[]{:S(2)}, u32[]{:S(2)}) collective-permute-start(bf16[2,128,2432]{2,1,0:T(8,128)(2,1)S(1)} %dynamic-slice_bitcast_fusion.4), channel_id=1, source_target_pairs={{0,8},{8,0},{16,24},{24,16},{1,9},{9,1},{17,25},{25,17},{2,10},{10... | collective-permute-start | bytes 3735560 | tf_op jit(solution)/shard_map/ppermute | solution.py:59
  1389.1 53.0 %collective-permute-start.39 = (bf16[1,152,2048]{2,1,0:T(8,128)(2,1)S(1)}, bf16[1,152,2048]{2,1,0:T(8,128)(2,1)S(1)}, u32[]{:S(2)}, u32[]{:S(2)}) collective-permute-start(bf16[1,152,2048]{2,1,0:T(8,128)(2,1)S(1)} %constant_dynamic-slice_fusion.2), channel_id=1, source_target_pairs={{0,16},{8,24},{16,0},{24,8},{1,17},{9,25},{17,1},{25,9},{2,18},{10... | collective-permute-start | bytes 1867784 | tf_op jit(solution)/shard_map/ppermute | solution.py:59
  1393.4 72.7 %collective-permute-start.36 = (bf16[1,128,2432]{2,1,0:T(8,128)(2,1)S(1)}, bf16[1,128,2432]{2,1,0:T(8,128)(2,1)S(1)}, u32[]{:S(2)}, u32[]{:S(2)}) collective-permute-start(bf16[1,128,2432]{2,1,0:T(8,128)(2,1)S(1)} %constant_dynamic-slice_fusion.3), channel_id=1, source_target_pairs={{0,16},{8,24},{16,0},{24,8},{1,17},{9,25},{17,1},{25,9},{2,18},{10... | collective-permute-start | bytes 1867784 | tf_op jit(solution)/shard_map/ppermute | solution.py:59
  1438.7 40.7 %collective-permute-start.33 = (bf16[1,128,2432]{2,1,0:T(8,128)(2,1)S(1)}, bf16[1,128,2432]{2,1,0:T(8,128)(2,1)S(1)}, u32[]{:S(2)}, u32[]{:S(2)}) collective-permute-start(bf16[1,128,2432]{2,1,0:T(8,128)(2,1)S(1)} %constant_dynamic-slice_fusion.4), channel_id=1, source_target_pairs={{0,16},{8,24},{16,0},{24,8},{1,17},{9,25},{17,1},{25,9},{2,18},{10... | collective-permute-start | bytes 1867784 | tf_op jit(solution)/shard_map/ppermute | solution.py:59
  1442.4 40.1 %collective-permute-start.40 = (bf16[152,2048]{1,0:T(8,128)(2,1)S(1)}, bf16[152,2048]{1,0:T(8,128)(2,1)S(1)}, u32[]{:S(2)}, u32[]{:S(2)}) collective-permute-start(bf16[152,2048]{1,0:T(8,128)(2,1)S(1)} %fusion.150), channel_id=1, source_target_pairs={{0,0},{2,1},{4,2},{6,3},{8,4},{10,5},{12,6},{14,7},{16,8},{18,9},{... | collective-permute-start | bytes 1867784 | tf_op jit(solution)/shard_map/ppermute | solution.py:219
  (114 other events, 1278.4 us)
Sparse Core Ops, SparseCore 0:
  18.5 128.9 all-gather.5
  150.3 100.8 all-gather.7
  253.0 103.4 all-gather.11
  358.2 100.5 all-gather.9
  460.5 100.5 all-gather.13
  973.1 45.1 reduce-scatter.9
  1021.3 56.9 reduce-scatter.7
  1081.4 99.1 reduce-scatter.15
  1183.8 99.1 reduce-scatter.13
  1286.0 99.1 reduce-scatter.11

commit v2 on v1

v2 whole, which is shorter than its diff:
```python
import jax
import jax.numpy as jnp
from jax import lax
from jax.experimental import pallas as pl
from jax.experimental.pallas import tpu as pltpu
from jax.sharding import Mesh, PartitionSpec as P

QUERY_HEADS = 24
KEY_VALUE_HEADS = 6
HEAD_SIZE = 64
BLOCK = 256
EPS = 1e-06
LOG2E = 1.4426950408889634
TP = ("pair", "core")
INNER = ("line", "pair")
ALL = ("line", "pair", "plane", "core")
BF = jnp.bfloat16
F32 = jnp.float32


NT = (((1,), (1,)), ((), ()))
NN = (((1,), (0,)), ((), ()))
TN = (((0,), (0,)), ((), ()))


def dot(a, b, dims):
    return lax.dot_general(a, b, dims, preferred_element_type=F32)


def turn(v):
    half = HEAD_SIZE // 2
    return jnp.concatenate([-v[:, half:], v[:, :half]], axis=1)


def turn_back(v):
    half = HEAD_SIZE // 2
    return jnp.concatenate([v[:, half:], -v[:, :half]], axis=1)


def make_attention(span, length, n_kv, groups, unit):
    pairs = n_kv // 2
    wide = 2 * groups * HEAD_SIZE
    scale = HEAD_SIZE ** (-0.5)
    tall = groups * span

    def queries(q_ref, gain, cosine, sine, g):
        out = []
        for h in range(groups):
            at = (g * groups + h) * HEAD_SIZE
            v = q_ref[:, at : at + HEAD_SIZE]
            inv = lax.rsqrt(jnp.mean(v * v, axis=1, keepdims=True) + EPS)
            n = v * inv * gain
            out.append(((n * cosine + turn(n) * sine) * (scale * LOG2E)).astype(BF))
        return jnp.concatenate(out, axis=0)

    def forward_kernel(seen_ref, q_ref, k_ref, v_ref, gain_ref, cos_ref, sin_ref, o_ref, l_ref):
        gain = gain_ref[...]
        cosine = cos_ref[...]
        sine = sin_ref[...]
        ones = jnp.ones((unit, HEAD_SIZE), BF)
        q_all = [queries(q_ref, gain, cosine, sine, g) for g in range(2)]

        def step(i, accs):
            at = pl.ds(pl.multiple_of(i * unit, unit), unit)
            out = []
            for g in range(2):
                lanes = slice(g * HEAD_SIZE, (g + 1) * HEAD_SIZE)
                k = k_ref[at, :][:, lanes]
                v = jnp.concatenate([v_ref[at, :][:, lanes], ones], axis=1)
                e = jnp.exp2(dot(q_all[g], k, NT)).astype(BF)
                out.append(accs[g] + dot(e, v, NN))
            return tuple(out)

        zero = jnp.zeros((tall, 2 * HEAD_SIZE), F32)
        accs = lax.fori_loop(0, seen_ref[0], step, (zero, zero))
        for g in range(2):
            inv = 1.0 / accs[g][:, HEAD_SIZE:]
            o = (accs[g][:, :HEAD_SIZE] * inv).astype(BF)
            for h in range(groups):
                at = (g * groups + h) * HEAD_SIZE
                o_ref[:, at : at + HEAD_SIZE] = o[h * span : (h + 1) * span]
                l_ref[:, at : at + HEAD_SIZE] = inv[h * span : (h + 1) * span]

    def backward_kernel(
        seen_ref, q_ref, k_ref, v_ref, gain_ref, cos_ref, sin_ref, o_ref, l_ref, d_ref,
        dq_ref, dk_ref, dv_ref, dg_ref, acc_ref,
    ):
        gain = gain_ref[...]
        cosine = cos_ref[...]
        sine = sin_ref[...]
        ones = jnp.ones((unit, HEAD_SIZE), BF)
        q_all = []
        d_all = []
        d_aug = []
        for g in range(2):
            q_all.append(queries(q_ref, gain, cosine, sine, g))
            rows = []
            more = []
            for h in range(groups):
                at = (g * groups + h) * HEAD_SIZE
                d = d_ref[:, at : at + HEAD_SIZE].astype(F32)
                inv = l_ref[:, at : at + HEAD_SIZE]
                o = o_ref[:, at : at + HEAD_SIZE].astype(F32)
                delta = -jnp.sum(d * o, axis=1, keepdims=True) * inv
                top = delta.astype(BF)
                low = (delta - top.astype(F32)).astype(BF)
                lane = lax.broadcasted_iota(jnp.int32, (span, HEAD_SIZE), 1)
                side = jnp.where(lane == 0, top.astype(F32), jnp.where(lane == 1, low.astype(F32), 0.0))
                rows.append((d * inv).astype(BF))
                more.append(side.astype(BF))
            d_all.append(jnp.concatenate(rows, axis=0))
            d_aug.append(jnp.concatenate([d_all[g], jnp.concatenate(more, axis=0)], axis=1))
        acc_ref[...] = jnp.zeros_like(acc_ref)
        dk_ref[...] = jnp.zeros_like(dk_ref)
        dv_ref[...] = jnp.zeros_like(dv_ref)

        def step(i, carry):
            at = pl.ds(pl.multiple_of(i * unit, unit), unit)
            dk = []
            dv = []
            for g in range(2):
                lanes = slice(g * HEAD_SIZE, (g + 1) * HEAD_SIZE)
                k = k_ref[at, :][:, lanes]
                v = jnp.concatenate([v_ref[at, :][:, lanes], ones], axis=1)
                e = jnp.exp2(dot(k, q_all[g], NT))
                ds = (e * dot(v, d_aug[g], NT)).astype(BF)
                dv.append(dot(e.astype(BF), d_all[g], NN))
                dk.append(dot(ds, q_all[g], NN))
                acc_ref[g] += dot(ds, k, TN)
            dk_ref[at, :] = (jnp.concatenate(dk, axis=1) * (1.0 / LOG2E)).astype(BF)
            dv_ref[at, :] = jnp.concatenate(dv, axis=1).astype(BF)
            return carry

        lax.fori_loop(0, seen_ref[0], step, 0)
        total = jnp.zeros((span, HEAD_SIZE), F32)
        for g in range(2):
            for h in range(groups):
                at = (g * groups + h) * HEAD_SIZE
                dr = acc_ref[g, h * span : (h + 1) * span, :] * scale
                v = q_ref[:, at : at + HEAD_SIZE]
                inv = lax.rsqrt(jnp.mean(v * v, axis=1, keepdims=True) + EPS)
                e = dr * cosine + turn_back(dr * sine)
                scaled = e * gain
                back = inv * scaled - v * inv**3 * jnp.mean(scaled * v, axis=1, keepdims=True)
                total = total + e * v * inv
                dq_ref[:, at : at + HEAD_SIZE] = back.astype(BF)
        dg_ref[0] = jnp.broadcast_to(jnp.sum(total, axis=0, keepdims=True), (8, HEAD_SIZE))

    def window(at):
        return pl.BlockSpec((span, wide), lambda j, s: (at, j))

    q_spec = window(0)
    k_spec = pl.BlockSpec((length, 2 * HEAD_SIZE), lambda j, s: (0, j))
    v_spec = pl.BlockSpec((length, 2 * HEAD_SIZE), lambda j, s: (0, pairs + j))
    row = pl.BlockSpec((1, HEAD_SIZE), lambda j, s: (0, 0))
    table = pl.BlockSpec((span, HEAD_SIZE), lambda j, s: (0, 0))
    q_width = pairs * wide
    kv_width = n_kv * HEAD_SIZE
    params = pltpu.CompilerParams(dimension_semantics=("arbitrary",))
    flops = 4 * n_kv * tall * length * HEAD_SIZE

    def forward(at, seen, q_lin, kv, gain, cosine, sine):
        return pl.pallas_call(
            forward_kernel,
            grid_spec=pltpu.PrefetchScalarGridSpec(
                num_scalar_prefetch=1,
                grid=(pairs,),
                in_specs=[window(at), k_spec, v_spec, row, table, table],
                out_specs=[q_spec, q_spec],
            ),
            out_shape=[
                jax.ShapeDtypeStruct((span, q_width), BF),
                jax.ShapeDtypeStruct((span, q_width), F32),
            ],
            compiler_params=params,
            cost_estimate=pl.CostEstimate(
                flops=flops * 4, transcendentals=n_kv * tall * length, bytes_accessed=8 * span * q_width
            ),
            name="attention_forward",
        )(seen, q_lin, kv, kv, gain, cosine, sine)

    def backward(at, seen, q_lin, kv, gain, cosine, sine, o, inv, d):
        return pl.pallas_call(
            backward_kernel,
            grid_spec=pltpu.PrefetchScalarGridSpec(
                num_scalar_prefetch=1,
                grid=(pairs,),
                in_specs=[window(at), k_spec, v_spec, row, table, table, q_spec, q_spec, window(at)],
                out_specs=[
                    q_spec,
                    k_spec,
                    k_spec,
                    pl.BlockSpec((1, 8, HEAD_SIZE), lambda j, s: (j, 0, 0)),
                ],
                scratch_shapes=[pltpu.VMEM((2, tall, HEAD_SIZE), F32)],
            ),
            out_shape=[
                jax.ShapeDtypeStruct((span, q_width), BF),
                jax.ShapeDtypeStruct((length, kv_width), BF),
                jax.ShapeDtypeStruct((length, kv_width), BF),
                jax.ShapeDtypeStruct((pairs, 8, HEAD_SIZE), F32),
            ],
            compiler_params=params,
            cost_estimate=pl.CostEstimate(
                flops=flops * 10, transcendentals=n_kv * tall * length, bytes_accessed=16 * span * q_width
            ),
            name="attention_backward",
        )(seen, q_lin, kv, kv, gain, cosine, sine, o, inv, d)

    return forward, backward


def make_keys(seqs, span, n_kv):
    kv_width = n_kv * HEAD_SIZE

    def forward_kernel(v_ref, gain_ref, cos_ref, sin_ref, o_ref):
        gain = gain_ref[...]
        cosine = cos_ref[...]
        sine = sin_ref[...]
        out = []
        for g in range(n_kv):
            v = v_ref[:, g * HEAD_SIZE : (g + 1) * HEAD_SIZE]
            n = v * lax.rsqrt(jnp.mean(v * v, axis=1, keepdims=True) + EPS) * gain
            out.append(n * cosine + turn(n) * sine)
        o_ref[:, :kv_width] = jnp.concatenate(out, axis=1).astype(BF)
        o_ref[:, kv_width:] = v_ref[:, kv_width:].astype(BF)

    def backward_kernel(v_ref, d_ref, gain_ref, cos_ref, sin_ref, o_ref, dg_ref):
        gain = gain_ref[...]
        cosine = cos_ref[...]
        sine = sin_ref[...]
        out = []
        total = jnp.zeros((span, HEAD_SIZE), F32)
        for g in range(n_kv):
            v = v_ref[:, g * HEAD_SIZE : (g + 1) * HEAD_SIZE]
            d = d_ref[:, g * HEAD_SIZE : (g + 1) * HEAD_SIZE]
            inv = lax.rsqrt(jnp.mean(v * v, axis=1, keepdims=True) + EPS)
            e = d * cosine + turn_back(d * sine)
            scaled = e * gain
            out.append(inv * scaled - v * inv**3 * jnp.mean(scaled * v, axis=1, keepdims=True))
            total = total + e * v * inv
        o_ref[:, :kv_width] = jnp.concatenate(out, axis=1).astype(BF)
        o_ref[:, kv_width:] = d_ref[:, kv_width:].astype(BF)
        dg_ref[...] = jnp.broadcast_to(jnp.sum(total, axis=0, keepdims=True), (8, HEAD_SIZE))

    row = pl.BlockSpec((1, HEAD_SIZE), lambda i: (0, 0))
    table = pl.BlockSpec((span, HEAD_SIZE), lambda i: (0, 0))
    params = pltpu.CompilerParams(dimension_semantics=("arbitrary",))

    def window(at):
        return pl.BlockSpec((span, 2 * kv_width), lambda i: (at, 0))

    cost = pl.CostEstimate(
        flops=20 * span * kv_width, transcendentals=span * n_kv, bytes_accessed=16 * span * kv_width
    )

    def forward(at, lin, gain, cosine, sine):
        return pl.pallas_call(
            forward_kernel,
            grid=(1,),
            in_specs=[window(at), row, table, table],
            out_specs=window(0),
            out_shape=jax.ShapeDtypeStruct((span, 2 * kv_width), BF),
            compiler_params=params,
            cost_estimate=cost,
            name="key_forward",
        )(lin, gain, cosine, sine)

    def backward(at, lin, d, gain, cosine, sine):
        return pl.pallas_call(
            backward_kernel,
            grid=(1,),
            in_specs=[window(at), window(0), row, table, table],
            out_specs=[window(0), pl.BlockSpec((8, HEAD_SIZE), lambda i: (0, 0))],
            out_shape=[
                jax.ShapeDtypeStruct((span, 2 * kv_width), BF),
                jax.ShapeDtypeStruct((8, HEAD_SIZE), F32),
            ],
            compiler_params=params,
            cost_estimate=cost,
            name="key_backward",
        )(lin, d, gain, cosine, sine)

    return forward, backward


def mm(left, right):
    return dot(left, right, NN)


def mm_tn(left, right):
    return dot(left, right, TN)


def mm_nt(left, right):
    return dot(left, right, NT)


def rms_norm(v, gain):
    inverse = lax.rsqrt(jnp.mean(v * v, axis=-1, keepdims=True) + EPS)
    return v * inverse * gain, inverse


def rms_back(v, inverse, gain, grad):
    scaled = grad * gain
    back = inverse * scaled - v * inverse**3 * jnp.mean(scaled * v, axis=-1, keepdims=True)
    return back, grad * v * inverse


def tie(*values):
    return lax.optimization_barrier(values)


def make_body(n_line, n_plane):
    n_inner = n_line * 2
    n_tp = 4
    n_group = n_line * n_plane
    n_dev = n_group * n_tp

    def flip(v, axis, size, bit):
        return lax.ppermute(v, axis, [(i, i ^ bit) for i in range(size)])

    def core_swap(v):
        return flip(v, "core", 2, 1)

    def pair_swap(v):
        return flip(v, "pair", 2, 1)

    def by_source(pieces, here):
        held = jnp.stack(pieces)
        shape = held.shape
        bit = 1
        while bit < len(pieces):
            split = held.reshape((-1, 2, bit) + shape[1:])
            turned = jnp.concatenate([split[:, 1:], split[:, :1]], axis=1)
            held = jnp.where((here & bit) != 0, turned, split).reshape(shape)
            bit *= 2
        return held

    def exchange(piece_of, axes, size, here):
        pieces = [piece_of(here)]
        pieces += [flip(piece_of(here ^ b), axes, size, b) for b in range(1, size)]
        return pieces

    def gather_inner(v, here):
        held = v[None]
        bit = n_inner // 2
        while bit:
            other = flip(held, INNER, n_inner, bit)
            high = (here & bit) != 0
            pair = jnp.stack([jnp.where(high, other, held), jnp.where(high, held, other)], axis=1)
            held = pair.reshape((-1,) + v.shape)
            bit //= 2
        return held

    def scatter_inner(v, here):
        held = v
        bit = 1
        while bit < n_inner:
            pair = held.reshape((held.shape[0] // 2, 2) + v.shape[1:])
            high = ((here & bit) != 0).astype(jnp.int32)
            keep = lax.dynamic_index_in_dim(pair, high, 1, keepdims=False)
            send = lax.dynamic_index_in_dim(pair, 1 - high, 1, keepdims=False)
            other = flip(send, INNER, n_inner, bit)
            held = keep.astype(F32) + other.astype(F32)
            bit *= 2
            if bit < n_inner:
                held = held.astype(BF)
        return held[0].astype(F32)

    def sum_pieces(part, axes, size, here):
        pieces = exchange(
            lambda k: lax.dynamic_index_in_dim(part, k, 0, keepdims=False), axes, size, here
        )
        total = pieces[0].astype(F32)
        for piece in pieces[1:]:
            total = total + piece.astype(F32)
        return total

    def spread_line(rows, line):
        return by_source(exchange(lambda k: rows, "line", n_line, line), line)

    def whole_rows(held, width):
        return lax.all_gather(held, "plane", axis=1, tiled=True).reshape(-1, width)

    def scatter_plane(whole, lead):
        r = whole.shape[0] // (lead * n_plane)
        if r % 16:
            held = whole.reshape(lead, n_plane, r, whole.shape[1])
            return lax.psum_scatter(held, "plane", scatter_dimension=1)
        held = whole.reshape(lead, n_plane * r, whole.shape[1])
        return lax.psum_scatter(held, "plane", scatter_dimension=1, tiled=True)

    def butterfly_sum(v):
        for axis, size in (("core", 2), ("pair", 2), ("plane", n_plane), ("line", n_line)):
            bit = 1
            while bit < size:
                v = v + flip(v, axis, size, bit)
                bit *= 2
        return v

    def near_and_far(chunks):
        far = jnp.concatenate([pair_swap(v) for v in chunks])
        near = jnp.concatenate(chunks)
        return jnp.concatenate([near, core_swap(near)]), jnp.concatenate([far, core_swap(far)])

    def fold(partial):
        half = partial.shape[0] // 2
        return partial[:half] + core_swap(partial[half:].astype(BF)).astype(F32)

    def body(x_in, attn_gain, w_query, w_key, w_value, qk_gain, w_out, ffn_gain, w_gate, w_up, w_down, dy_in):
        line = lax.axis_index("line")
        core = lax.axis_index("core")
        here = line * 2 + lax.axis_index("pair")
        tp = lax.axis_index("pair") * 2 + core
        flat = (here * n_plane + lax.axis_index("plane")) * 2 + core
        seqs, span, width = x_in.shape
        rows = seqs * span
        groups = QUERY_HEADS // KEY_VALUE_HEADS
        length = span * n_inner
        q_width = w_query.shape[1]
        kv_width = w_key.shape[1]
        per = w_query.shape[0]
        part = w_gate.shape[1] // n_tp

        def column_part(w):
            pieces = exchange(
                lambda k: lax.dynamic_slice_in_dim(w, k * part, part, axis=1), TP, n_tp, tp
            )
            return by_source(pieces, tp).reshape(2, 2 * per, part)

        def holder(s):
            quarter, group = divmod(s, n_group)
            at_line, at_plane = divmod(group, n_plane)
            return ((at_line * 2 + quarter // 2) * n_plane + at_plane) * 2 + quarter % 2

        spread = [(s, holder(s)) for s in range(n_dev)]
        extra = jnp.zeros((per, 128), BF)
        extra = extra.at[:, 0].set(attn_gain).at[:, 1].set(ffn_gain)
        extra = extra.at[: qk_gain.shape[0], 2].set(qk_gain)
        at_gain = 2 * kv_width
        at_query = at_gain + 128
        at_out = at_query + q_width
        out_rows = jnp.pad(w_out, ((0, per - w_out.shape[0]), (0, 0)))
        packed = jnp.concatenate([w_key, w_value, extra, w_query, out_rows], axis=1)
        packed = lax.all_gather(packed, ALL, axis=0, tiled=True)
        wkv = packed[:, :at_gain]
        wq = packed[:, at_query:at_out]
        wo = packed[:, at_out:].reshape(n_dev, per, width)[:, : w_out.shape[0]].reshape(-1, width)
        tail = packed[:, at_gain : at_gain + 3].astype(F32)
        g_one = tail[:, 0]
        g_two = tail[:, 1]
        g_qk = tail[:, 2].reshape(n_dev, per)[:, : qk_gain.shape[0]].reshape(-1)
        g_query, g_key = g_qk[:HEAD_SIZE], g_qk[HEAD_SIZE:]

        wg = whole_rows(spread_line(column_part(w_gate), line).reshape(n_inner, 2 * per, part), part)
        wu = whole_rows(spread_line(column_part(w_up), line).reshape(n_inner, 2 * per, part), part)
        cut_down = lax.ppermute(w_down, ALL, spread)
        dy = dy_in.reshape(rows, width)

        base = here * span
        positions = (base + jnp.arange(span)).astype(F32)
        freq = 10000.0 ** (-jnp.arange(HEAD_SIZE // 2, dtype=F32) * 2.0 / HEAD_SIZE)
        angle = positions[:, None] * freq[None, :]
        cosine = jnp.concatenate([jnp.cos(angle), jnp.cos(angle)], axis=-1)
        sine = jnp.concatenate([jnp.sin(angle), jnp.sin(angle)], axis=-1)
        unit = min(BLOCK, length)
        seen = ((base // BLOCK + 1) * (BLOCK // unit)).astype(jnp.int32).reshape(1)
        attend, attend_back = make_attention(span, length, KEY_VALUE_HEADS, groups, unit)
        gain_row = g_query.reshape(1, HEAD_SIZE)

        x = x_in.reshape(rows, width).astype(F32)
        normed, inv_one = rms_norm(x, g_one)
        normed_b = normed.astype(BF)
        kv_lin = mm(normed_b, wkv)
        gain_key = g_key.reshape(1, HEAD_SIZE)
        make_key, make_key_back = make_keys(seqs, span, KEY_VALUE_HEADS)
        kv = [make_key(s, kv_lin, gain_key, cosine, sine) for s in range(seqs)]
        gathered = [gather_inner(v, here).reshape(length, 2 * kv_width) for v in kv]
        q_lin = mm(normed_b, wq)
        gathered[-1], cut_down, dy_in = tie(gathered[-1], cut_down, dy_in)
        dy_near, dy_far = near_and_far(list(dy_in))
        cut_down = spread_line(cut_down, line)
        kept = []
        resids = []
        invs = []
        n2s = []
        for s in range(seqs):
            o, total = attend(s, seen, q_lin, gathered[s], gain_row, cosine, sine)
            if s == seqs - 1:
                o, cut_down = tie(o, cut_down)
                wd = whole_rows(cut_down, width)
            kept.append((o, total))
            resid = x[s * span : (s + 1) * span] + mm(o, wo)
            normed2, inv_two = rms_norm(resid, g_two)
            resids.append(resid)
            invs.append(inv_two)
            n2s.append(normed2.astype(BF))
        mixed = jnp.concatenate([o for o, _ in kept])
        resid = jnp.concatenate(resids)
        inv_two = jnp.concatenate(invs)
        n2_near, n2_far = near_and_far(n2s)

        def expand(n2):
            gate = mm(n2, wg)
            up = mm(n2, wu)
            return gate, up, (gate * jax.nn.sigmoid(gate) * up).astype(BF)

        def expand_back(dy, gate, up):
            d_hidden = mm_nt(dy, wd)
            sigma = jax.nn.sigmoid(gate)
            dg = (d_hidden * up * (sigma * (1.0 + gate * (1.0 - sigma)))).astype(BF)
            return dg, (d_hidden * (gate * sigma)).astype(BF)

        gate_near, up_near, hidden_near = expand(n2_near)
        gate_far, up_far, hidden_far = expand(n2_far)
        hidden = jnp.concatenate([hidden_near, hidden_far])
        n2_all = jnp.concatenate([n2_near, n2_far])

        grad_down = mm_tn(hidden, jnp.concatenate([dy_near, dy_far])).astype(BF)
        wd, grad_down = tie(wd, grad_down)
        down_part = scatter_plane(grad_down, n_line)
        dg_far, du_far = expand_back(dy_far, gate_far, up_far)
        sent = fold(mm_nt(dg_far, wg) + mm_nt(du_far, wu)).astype(BF)
        sent, dy_near = tie(sent, dy_near)
        dg_near, du_near = expand_back(dy_near, gate_near, up_near)
        dn2 = fold(mm_nt(dg_near, wg) + mm_nt(du_near, wu))
        grad_gate = mm_tn(n2_all, jnp.concatenate([dg_near, dg_far])).astype(BF)
        grad_up = mm_tn(n2_all, jnp.concatenate([du_near, du_far])).astype(BF)
        got = pair_swap(sent)
        gate_part = scatter_plane(grad_gate, n_inner)
        up_part = scatter_plane(grad_up, n_inner)
        got, dn2, grad_gate, grad_up, down_part = tie(got, dn2, grad_gate, grad_up, down_part)
        down_sum = sum_pieces(down_part, "line", n_line, line).astype(BF)
        dn2 = dn2 + got.astype(F32)
        back_two, terms_two = rms_back(resid, inv_two, g_two, dn2)
        grad_gain_two = jnp.sum(terms_two, axis=0)
        d_resid = dy.astype(F32) + back_two

        def column_whole(piece):
            held = piece.astype(BF)
            pieces = exchange(
                lambda k: lax.dynamic_index_in_dim(held, k, 0, keepdims=False), TP, n_tp, tp
            )
            return by_source(pieces, tp).transpose(1, 0, 2).reshape(per, -1).astype(F32)

        def fold_core(whole):
            r = whole.shape[0] // n_dev
            held = whole.reshape(n_dev // 2, 2, r, -1)
            mine = lax.dynamic_index_in_dim(held, core, 1, keepdims=False)
            got = core_swap(lax.dynamic_index_in_dim(held, 1 - core, 1, keepdims=False))
            held = (mine.astype(F32) + got.astype(F32)).astype(BF)
            return held.reshape(whole.shape[0] // 2, -1)

        drb = d_resid.astype(BF)
        dm = mm_nt(drb, wo).astype(BF)
        out_part = scatter_plane(fold_core(mm_tn(mixed, drb).astype(BF)), n_inner)
        dm, down_sum, gate_part = tie(dm, down_sum, gate_part)
        gate_sum = sum_pieces(gate_part.reshape(n_line, n_tp, per, part), "line", n_line, line)
        dq = []
        dkv = []
        gains_q = []
        for s in range(seqs):
            dq_s, dk_s, dv_s, dg_s = attend_back(
                s, seen, q_lin, gathered[s], gain_row, cosine, sine, *kept[s], dm
            )
            dq.append(dq_s)
            gains_q.append(jnp.sum(dg_s[:, 0], axis=0))
            both = jnp.concatenate([dk_s, dv_s], axis=1)
            if s == seqs - 1:
                both, hidden_near, hidden_far, gate_sum = tie(both, hidden_near, hidden_far, gate_sum)
            dkv.append(scatter_inner(both.reshape(n_inner, span, 2 * kv_width), here))
        d_down = lax.ppermute(down_sum, ALL, [(b, a) for a, b in spread]).astype(F32)
        sent = fold(mm(hidden_far, wd)).astype(BF)
        output = resid + (fold(mm(hidden_near, wd)) + pair_swap(sent).astype(F32))
        result = output.astype(BF).reshape(seqs, span, width)
        dkv[-1], up_part, out_part = tie(dkv[-1], up_part, out_part)
        up_sum = sum_pieces(up_part.reshape(n_line, n_tp, per, part), "line", n_line, line)
        d_out = sum_pieces(out_part, INNER, n_inner, here)
        d_kvs = []
        gains_k = []
        for s in range(seqs):
            d_kv_s, dg_s = make_key_back(s, kv_lin, dkv[s], gain_key, cosine, sine)
            d_kvs.append(d_kv_s)
            gains_k.append(dg_s[0])
        grad_qk = jnp.concatenate([sum(gains_q), sum(gains_k)])
        d_lin = jnp.concatenate([jnp.concatenate(dq), jnp.concatenate(d_kvs)], axis=1)
        grad_qkv = mm_tn(normed_b, d_lin).astype(BF)
        qkv_part = scatter_plane(fold_core(grad_qkv), n_inner)
        d_lin, grad_qkv, up_sum, d_out = tie(d_lin, grad_qkv, up_sum, d_out)
        d_gate = column_whole(gate_sum)
        d_up = column_whole(up_sum)
        dn = mm_nt(d_lin[:, :q_width], wq) + mm_nt(d_lin[:, q_width:], wkv)
        back_one, terms_one = rms_back(x, inv_one, g_one, dn)
        grad_gain_one = jnp.sum(terms_one, axis=0)
        d_inputs = (d_resid + back_one).reshape(seqs, span, width)

        gains = butterfly_sum(jnp.concatenate([grad_gain_one, grad_gain_two, grad_qk]))
        qkv_part, d_gate, d_up, d_out, result = tie(qkv_part, d_gate, d_up, d_out, result)
        d_qkv = sum_pieces(qkv_part, INNER, n_inner, here)
        d_attn_gain = lax.dynamic_slice_in_dim(gains, flat * per, per)
        d_ffn_gain = lax.dynamic_slice_in_dim(gains, width + flat * per, per)
        n_qk = qk_gain.shape[0]
        d_qk = lax.dynamic_slice_in_dim(gains, 2 * width + flat * n_qk, n_qk)
        return (
            result,
            d_inputs,
            d_attn_gain,
            d_qkv[:, :q_width],
            d_qkv[:, q_width : q_width + kv_width],
            d_qkv[:, q_width + kv_width :],
            d_qk,
            d_out,
            d_ffn_gain,
            d_gate,
            d_up,
            d_down,
        )

    return body


def solution(mesh):
    n_line = mesh.shape["inner"] // 2
    n_plane = mesh.shape["outer"] // 2
    fine = Mesh(mesh.devices.reshape(n_line, 2, n_plane, 2), ALL)
    tokens = P(("plane", "core"), INNER, None)
    vec = P(ALL)
    mat = P(ALL, None)
    return jax.shard_map(
        make_body(n_line, n_plane),
        mesh=fine,
        in_specs=(tokens, vec, mat, mat, mat, vec, mat, vec, mat, mat, mat, tokens),
        out_specs=(tokens, tokens, vec, mat, mat, mat, vec, mat, vec, mat, mat, mat),
        check_vma=False,
    )
```

time: 1510 us -> 1060 us (0.70)
  waiting for transfers between devices: 631 us -> 339 us
  matrix products: 400 us -> 217 us
  local copies, waits for them, and re-layouts: 245 us -> 129 us
  Pallas kernels: 0 us -> 109 us
  starting transfers between devices: 67.9 us -> 118 us
    reduce_scatter x4, waiting for transfers between devices: 197 us -> 0.01 us  [scatter_plane(): return lax.psum_scatter(held, 'plane', scatter_dimension=1, tiled=True)]
    dot_general x102 -> x24, matrix products: 400 us -> 217 us  [dot(): return lax.dot_general(a, b, dims, preferred_element_type=F32)]
    pallas_call x0 -> x8, Pallas kernels: none -> 109 us  [the longest x2 61.4 us: backward(): pl.pallas_call(backward_kernel, grid_spec=pltpu.PrefetchScalarGridSpec(nu...]
    unnamed x11 -> x10, waiting for transfers between devices: 42.8 us -> 0.15 us
    ppermute x12 -> x2, waiting for transfers between devices: 41.6 us -> 0.01 us  [the longest x1 0.01 us: body(): cut_down = lax.ppermute(w_down, ALL, spread)]
    ppermute x29 -> x53, starting transfers between devices: 59.8 us -> 99.4 us  [flip(): return lax.ppermute(v, axis, [(i, i ^ bit) for i in range(size)])]
    dynamic_slice x16 -> x2, local copies, waits for them, and re-layouts: 30.5 us -> 0.09 us  [column_whole(): lax.dynamic_index_in_dim(held, k, 0, keepdims=False)]
    ppermute x29 -> x53, waiting for transfers between devices: 350 us -> 321 us  [flip(): return lax.ppermute(v, axis, [(i, i ^ bit) for i in range(size)])]
  transfers between devices with their start and end apart: 51 -> 64, of which waited for: 29 -> 27; matrix products, arithmetic and copies ran while one was open for 44% -> 40% of each run, Pallas kernels for 0% -> 10%
where the time goes in v2:
time: 1060 us; the launch traced here: 1050 us
  waiting for transfers between devices  339 us (32%)
  matrix products  217 us (20%)
  local copies, waits for them, and re-layouts  129 us (12%)
  other arithmetic  123 us (12%)
  starting transfers between devices  118 us (11%)
  Pallas kernels  109 us (10%)
  between operations  15.5 us (1%)
    ppermute x53, waiting for transfers between devices, flip(): return lax.ppermute(v, axis, [(i, i ^ bit) for i in range(size)])  321 us
    dot_general x24, matrix products, dot(): return lax.dot_general(a, b, dims, preferred_element_type=F32)  217 us
    ppermute x53, starting transfers between devices, flip(): return lax.ppermute(v, axis, [(i, i ^ bit) for i in range(size)])  99.4 us
    pallas_call x2, Pallas kernels, backward(): pl.pallas_call(backward_kernel, grid_spec=pltpu.PrefetchScalarGridSpec(nu...  61.4 us
    unnamed x187, local copies, waits for them, and re-layouts  43.7 us
    pallas_call x2, Pallas kernels, forward(): pl.pallas_call(forward_kernel, grid_spec=pltpu.PrefetchScalarGridSpec(num...  32.3 us
  transfers between devices with their start and end apart: 64, of which 27 were waited for; matrix products, arithmetic and copies ran while one was open for 40% of the time, Pallas kernels for 10%

profile of v2, /device:TPU:12, one launch (start us, length us, event | category | flops | bytes accessed | tf_op | source)
XLA Modules:
  0.0 1050.7 jit_solution(9221538289842373192)
XLA Ops:
  45.1 9.7 collective-permute-done.16
  58.8 12.4 %collective-permute-done.13 = bf16[2,128,1216]{1,2,0:T(8,128)(2,1)} collective-permute-done((bf16[2,128,1216]{1,2,0:T(8,128)(2,1)}, bf16[2,128,1216]{1,2,0:T(8,128)(2,1)}, u32[]{:S(2)}, u32[]{:S(2)}) %collective-permute-start.13) | collective-permute-done | bytes 622624 | tf_op jit(solution)/shard_map/ppermute | solution.py:321
  92.0 89.0 %collective-permute-done.17 = bf16[2,128,1216]{1,2,0:T(8,128)(2,1)} collective-permute-done((bf16[2,128,1216]{1,2,0:T(8,128)(2,1)S(1)}, bf16[2,128,1216]{1,2,0:T(8,128)(2,1)}, u32[]{:S(2)}, u32[]{:S(2)}) %collective-permute-start.17) | collective-permute-done | bytes 622624 | tf_op jit(solution)/shard_map/ppermute | solution.py:321
  183.6 18.1 %all-gather.5.cloned.1.call-done = bf16[2048,4480]{1,0:T(8,128)(2,1)} async-done(((bf16[64,4480]{1,0:T(8,128)(2,1)}), bf16[2048,4480]{1,0:T(8,128)(2,1)}) %all-gather.5.cloned.1.call-update) | async-done | bytes 18350096 | tf_op jit(solution)/shard_map/all_gather | solution.py:446
  221.3 11.8 %all-gather.7.cloned.1.call-start = ((), (), s32[]{:S(2)}) async-start(), calls=%async_computation.6 | async-start | bytes 6225920 | tf_op jit(solution)/shard_map/all_gather | solution.py:384
  237.8 14.2 %collective-permute-done.2 = bf16[1,256,768]{2,1,0:T(8,128)(2,1)S(1)} collective-permute-done((bf16[1,256,768]{2,1,0:T(8,128)(2,1)}, bf16[1,256,768]{2,1,0:T(8,128)(2,1)S(1)}, u32[]{:S(2)}, u32[]{:S(2)}) %collective-permute-start.2) | collective-permute-done | bytes 393248 | tf_op jit(solution)/shard_map/ppermute | solution.py:321
  293.9 16.1 %attention_forward.2 = (bf16[256,1536]{1,0:T(8,128)(2,1)}, f32[256,1536]{1,0:T(8,128)}) custom-call(s32[1]{0:T(128)} %bitcast.6.seen_ref, f32[512,1536]{1,0:T(8,128)} %fusion.4.q_ref, bf16[1024,768]{1,0:T(8,128)(2,1)} %bitcast.425, bf16[1024,768]{1,0:T(8,128)(2,1)} %bitcast.426, f32[1,64]{1,0:T(1,128)} %reshape.863.gain_ref, ...), custom_call_target="tpu_custom_call" | custom-call | flops 6442450944 | bytes 3145728 | tf_op jit(solution)/shard_map/attention_forward/pallas_call | solution.py:163
  318.4 16.2 %attention_forward.3 = (bf16[256,1536]{1,0:T(8,128)(2,1)}, f32[256,1536]{1,0:T(8,128)}) custom-call(s32[1]{0:T(128)} %bitcast.6.seen_ref, f32[512,1536]{1,0:T(8,128)} %fusion.4.q_ref, bf16[1024,768]{1,0:T(8,128)(2,1)} %bitcast.429, bf16[1024,768]{1,0:T(8,128)(2,1)} %bitcast.430, f32[1,64]{1,0:T(1,128)} %reshape.863.gain_ref, ...), custom_call_target="tpu_custom_call" | custom-call | flops 6442450944 | bytes 3145728 | tf_op jit(solution)/shard_map/attention_forward/pallas_call | solution.py:163
  356.4 15.3 %collective-permute-done.18 = bf16[256,2048]{1,0:T(8,128)(2,1)} collective-permute-done((bf16[256,2048]{1,0:T(8,128)(2,1)}, bf16[256,2048]{1,0:T(8,128)(2,1)}, u32[]{:S(2)}, u32[]{:S(2)}) %collective-permute-start.18) | collective-permute-done | bytes 1048608 | tf_op jit(solution)/shard_map/ppermute | solution.py:321
  371.7 21.4 %collective-permute-done.19 = bf16[256,2048]{1,0:T(8,128)(2,1)} collective-permute-done((bf16[256,2048]{1,0:T(8,128)(2,1)}, bf16[256,2048]{1,0:T(8,128)(2,1)}, u32[]{:S(2)}, u32[]{:S(2)}) %collective-permute-start.19) | collective-permute-done | bytes 1048608 | tf_op jit(solution)/shard_map/ppermute | solution.py:321
  404.7 11.3 %fusion.45 = f32[1024,1216]{0,1:T(8,128)} fusion(bf16[2048,1216]{1,0:T(8,128)(2,1)} %bitcast.467, bf16[512,2048]{1,0:T(8,128)(2,1)} %collective-permute-done.9, bf16[256,2048]{1,0:T(8,128)(2,1)} %get-tuple-element.148, bf16[256,2048]{1,0:T(8,128)(2,1)} %get-tuple-element.150), kind=kOutput, calls=%fused_computation.96 | convolution fusion | flops 5112856576 | bytes 14155776 | tf_op jit(solution)/shard_map/dot_general | solution.py:27
  416.0 13.7 %multiply_convert_fusion.5 = (bf16[1024,1216]{0,1:T(8,128)(2,1)S(1)}, f32[1024,1216]{0,1:T(8,128)}) fusion(f32[1024,1216]{0,1:T(8,128)} %fusion.45, bf16[2048,1216]{1,0:T(8,128)(2,1)} %bitcast.475, bf16[512,2048]{1,0:T(8,128)(2,1)} %collective-permute-done.9, bf16[256,2048]{1,0:T(8,128)(2,1)} %get-tuple-element.148, bf16[256,2048]{1,0:T(8,128)(2,1)} %get-tuple-element.150), kind=kOutput, calls=%fused_computation.29 | convolution fusion | flops 5120327680 | bytes 21626880 | tf_op jit(solution)/shard_map/dot_general | solution.py:27
  459.3 14.5 %convolution_convert_fusion.4 = bf16[1216,2048]{1,0:T(8,128)(2,1)} fusion(bf16[2048,2048]{1,0:T(8,128)(2,1)} %constant_dynamic-update-slice_fusion.7, bf16[1024,1216]{0,1:T(8,128)(2,1)S(1)} %get-tuple-element.128, bf16[1024,1216]{0,1:T(8,128)(2,1)S(1)} %get-tuple-element.127), kind=kOutput, calls=%fused_computation.6 | convolution fusion | flops 10212999168 | bytes 18350080 | tf_op jit(solution)/shard_map/dot_general | solution.py:27
  479.5 13.5 %multiply_convert_fusion.2 = (bf16[1024,1216]{0,1:T(8,128)(2,1)S(1)}, bf16[1024,1216]{0,1:T(8,128)(2,1)S(1)}) fusion(f32[1024,1216]{0,1:T(8,128)} %copy-done.64, f32[1024,1216]{0,1:T(8,128)} %get-tuple-element.238, bf16[1216,2048]{1,0:T(8,128)(2,1)} %bitcast.481, bf16[512,2048]{1,0:T(8,128)(2,1)} %collective-permute-done.8, ...), kind=kOutput, calls=%fused_computation.24 | convolution fusion | flops 5129043968 | bytes 24117248 | tf_op jit(solution)/shard_map/dot_general | solution.py:27
  501.1 10.0 convolution_add_fusion.1
  517.9 10.6 %multiply_convert_fusion = (bf16[1024,1216]{0,1:T(8,128)(2,1)}, bf16[1024,1216]{0,1:T(8,128)(2,1)S(1)}) fusion(f32[1024,1216]{0,1:T(8,128)} %fusion.45, f32[1024,1216]{0,1:T(8,128)} %get-tuple-element.240, bf16[1024,2048]{1,0:T(8,128)(2,1)S(1)} %pad_maximum_fusion.1, bf16[1216,2048]{1,0:T(8,128)(2,1)S(1)} %bitcast.485), kind=kOutput, calls=%fused_computation.22 | convolution fusion | flops 5116461056 | bytes 24117248 | tf_op jit(solution)/shard_map/dot_general | solution.py:27
  530.0 12.9 %convolution_convert_fusion.2 = bf16[2048,1216]{0,1:T(8,128)(2,1)} fusion(bf16[2048,2048]{1,0:T(8,128)(2,1)S(1)} %bitcast.458, bf16[1024,1216]{0,1:T(8,128)(2,1)S(1)} %copy-done.67, bf16[1024,1216]{0,1:T(8,128)(2,1)S(1)} %get-tuple-element.152), kind=kOutput, calls=%fused_computation.4 | convolution fusion | flops 10212999168 | bytes 18350080 | tf_op jit(solution)/shard_map/dot_general | solution.py:27
  550.8 15.2 %convolution_convert_fusion.1 = bf16[2048,1216]{0,1:T(8,128)(2,1)} fusion(bf16[2048,2048]{1,0:T(8,128)(2,1)} %get-tuple-element.155, bf16[1024,1216]{0,1:T(8,128)(2,1)S(1)} %get-tuple-element.153, bf16[1024,1216]{0,1:T(8,128)(2,1)} %get-tuple-element.151), kind=kOutput, calls=%fused_computation.3 | convolution fusion | flops 10212999168 | bytes 18350080 | tf_op jit(solution)/shard_map/dot_general | solution.py:27
  574.0 10.5 %fusion.84 = f32[1024,2048]{1,0:T(8,128)} fusion(bf16[1024,1216]{0,1:T(8,128)(2,1)S(1)} %copy-done.69, bf16[2048,1216]{1,0:T(8,128)(2,1)} %bitcast.468), kind=kOutput, calls=%fused_computation.282 | convolution fusion | flops 5100273664 | bytes 15859712 | tf_op jit(solution)/shard_map/dot_general | solution.py:27
  586.2 9.9 convolution_add_fusion
  611.7 38.0 %collective-permute-done.23 = bf16[512,2048]{1,0:T(8,128)(2,1)} collective-permute-done((bf16[512,2048]{1,0:T(8,128)(2,1)}, bf16[512,2048]{1,0:T(8,128)(2,1)}, u32[]{:S(2)}, u32[]{:S(2)}) %collective-permute-start.23) | collective-permute-done | bytes 2097184 | tf_op jit(solution)/shard_map/ppermute | solution.py:321
  685.0 13.6 %collective-permute-done.25 = bf16[152,2048]{1,0:T(8,128)(2,1)} collective-permute-done((bf16[152,2048]{1,0:T(8,128)(2,1)}, bf16[152,2048]{1,0:T(8,128)(2,1)}, u32[]{:S(2)}, u32[]{:S(2)}) %collective-permute-start.25) | collective-permute-done | bytes 622624 | tf_op jit(solution)/shard_map/ppermute | solution.py:321
  705.4 30.6 %attention_backward.3 = (bf16[256,1536]{1,0:T(8,128)(2,1)}, bf16[1024,384]{1,0:T(8,128)(2,1)}, bf16[1024,384]{1,0:T(8,128)(2,1)}, f32[3,8,64]{2,1,0:T(8,128)}) custom-call(s32[1]{0:T(128)} %bitcast.6.seen_ref, f32[512,1536]{1,0:T(8,128)} %fusion.4.q_ref, bf16[1024,768]{1,0:T(8,128)(2,1)} %bitcast.431, bf16[1024,768]{1,0:T(8,128)(2,1)} %bitcast.432, ...), custom_call_target="tpu_custom_call" | custom-call | flops 16106127360 | bytes 6291456 | tf_op jit(solution)/shard_map/attention_backward/pallas_call | solution.py:183
  736.1 30.8 %attention_backward.2 = (bf16[256,1536]{1,0:T(8,128)(2,1)}, bf16[1024,384]{1,0:T(8,128)(2,1)}, bf16[1024,384]{1,0:T(8,128)(2,1)}, f32[3,8,64]{2,1,0:T(8,128)}) custom-call(s32[1]{0:T(128)} %bitcast.6.seen_ref, f32[512,1536]{1,0:T(8,128)} %fusion.4.q_ref, bf16[1024,768]{1,0:T(8,128)(2,1)} %bitcast.427, bf16[1024,768]{1,0:T(8,128)(2,1)} %bitcast.428, ...), custom_call_target="tpu_custom_call" | custom-call | flops 16106127360 | bytes 6291456 | tf_op jit(solution)/shard_map/attention_backward/pallas_call | solution.py:183
  773.6 15.6 %collective-permute-done.26 = bf16[2,256,768]{2,1,0:T(8,128)(2,1)} collective-permute-done((bf16[2,256,768]{2,1,0:T(8,128)(2,1)S(1)}, bf16[2,256,768]{2,1,0:T(8,128)(2,1)}, u32[]{:S(2)}, u32[]{:S(2)}) %collective-permute-start.26) | collective-permute-done | bytes 786464 | tf_op jit(solution)/shard_map/ppermute | solution.py:321
  791.6 19.4 %collective-permute-start.27 = (bf16[1,256,768]{2,1,0:T(8,128)(2,1)}, bf16[1,256,768]{2,1,0:T(8,128)(2,1)}, u32[]{:S(2)}, u32[]{:S(2)}) collective-permute-start(bf16[1,256,768]{2,1,0:T(8,128)(2,1)} %constant_dynamic-slice_fusion.3), channel_id=1, source_target_pairs={{0,16},{8,24},{16,0},{24,8},{1,17},{9,25},{17,1},{25,9},{2,18},{10... | collective-permute-start | bytes 1179656 | tf_op jit(solution)/shard_map/ppermute | solution.py:321
  814.2 21.7 %collective-permute-start.30 = (bf16[1,256,768]{2,1,0:T(8,128)(2,1)}, bf16[1,256,768]{2,1,0:T(8,128)(2,1)}, u32[]{:S(2)}, u32[]{:S(2)}) collective-permute-start(bf16[1,256,768]{2,1,0:T(8,128)(2,1)} %constant_dynamic-slice_fusion.2), channel_id=1, source_target_pairs={{0,16},{8,24},{16,0},{24,8},{1,17},{9,25},{17,1},{25,9},{2,18},{10... | collective-permute-start | bytes 1179656 | tf_op jit(solution)/shard_map/ppermute | solution.py:321
  842.3 8.8 collective-permute-done.30
  879.6 9.4 fusion.86
  924.8 19.3 %collective-permute-done.38 = bf16[48,2048]{1,0:T(8,128)(2,1)S(1)} collective-permute-done((bf16[48,2048]{1,0:T(8,128)(2,1)S(1)}, bf16[48,2048]{1,0:T(8,128)(2,1)S(1)}, u32[]{:S(2)}, u32[]{:S(2)}) %collective-permute-start.38) | collective-permute-done | bytes 196640 | tf_op jit(solution)/shard_map/ppermute | solution.py:321
  951.1 10.5 collective-permute-done.36
  966.6 9.0 fusion.36
  (486 shorter events, 461.7 us)
Async XLA Ops:
  7.2 194.6 %all-gather.5.cloned.1.call-start = ((), (), s32[]{:S(2)}) async-start(), calls=%async_computation.5 | async-start | bytes 18923520 | tf_op jit(solution)/shard_map/all_gather | solution.py:446
  21.0 383.7 %all-gather.9.cloned.1.call-start = ((), (), s32[]{:S(2)}) async-start(), calls=%async_computation.7 | async-start | bytes 6553600 | tf_op jit(solution)/shard_map/all_gather | solution.py:384
  33.7 37.5 %collective-permute-start.13 = (bf16[2,128,1216]{1,2,0:T(8,128)(2,1)}, bf16[2,128,1216]{1,2,0:T(8,128)(2,1)}, u32[]{:S(2)}, u32[]{:S(2)}) collective-permute-start(bf16[2,128,1216]{1,2,0:T(8,128)(2,1)} %copy.123), channel_id=1, source_target_pairs={{0,16},{16,0},{1,17},{17,1},{2,18},{18,2},{3,19},{19,3},{4,20},{20... | collective-permute-start | bytes 1867784 | tf_op jit(solution)/shard_map/ppermute | solution.py:321
  77.3 338.7 %all-gather.11.cloned.1.call-start = ((), (), s32[]{:S(2)}) async-start(), calls=%async_computation.8 | async-start | bytes 6553600 | tf_op jit(solution)/shard_map/all_gather | solution.py:384
  77.3 209.9 %collective-permute-start.4 = (bf16[152,2048]{1,0:T(8,128)(2,1)}, bf16[152,2048]{1,0:T(8,128)(2,1)}, u32[]{:S(2)}, u32[]{:S(2)}) collective-permute-start(bf16[152,2048]{1,0:T(8,128)(2,1)} %param.28), channel_id=1, source_target_pairs={{0,0},{1,2},{2,4},{3,6},{4,16},{5,18},{6,20},{7,22},{8,1},{9,3},{1... | collective-permute-start | bytes 1867784 | tf_op jit(solution)/shard_map/ppermute | solution.py:458
  84.8 96.2 %collective-permute-start.17 = (bf16[2,128,1216]{1,2,0:T(8,128)(2,1)S(1)}, bf16[2,128,1216]{1,2,0:T(8,128)(2,1)}, u32[]{:S(2)}, u32[]{:S(2)}) collective-permute-start(bf16[2,128,1216]{1,2,0:T(8,128)(2,1)S(1)} %copy.132), channel_id=1, source_target_pairs={{0,16},{16,0},{1,17},{17,1},{2,18},{18,2},{3,19},{19,3},{4,20},{20... | collective-permute-start | bytes 1867784 | tf_op jit(solution)/shard_map/ppermute | solution.py:321
  221.3 252.5 %all-gather.7.cloned.1.call-start = ((), (), s32[]{:S(2)}) async-start(), calls=%async_computation.6 | async-start | bytes 6225920 | tf_op jit(solution)/shard_map/all_gather | solution.py:384
  237.7 44.0 %collective-permute-start.1 = (bf16[2,256,768]{2,1,0:T(8,128)(2,1)S(1)}, bf16[2,256,768]{2,1,0:T(8,128)(2,1)}, u32[]{:S(2)}, u32[]{:S(2)}) collective-permute-start(bf16[2,256,768]{2,1,0:T(8,128)(2,1)S(1)} %maximum_bitcast_fusion.2), channel_id=1, source_target_pairs={{0,8},{8,0},{16,24},{24,16},{1,9},{9,1},{17,25},{25,17},{2,10},{10... | collective-permute-start | bytes 2359304 | tf_op jit(solution)/shard_map/ppermute | solution.py:321
  287.3 47.4 %collective-permute-start.5 = (bf16[152,2048]{1,0:T(8,128)(2,1)}, bf16[152,2048]{1,0:T(8,128)(2,1)}, u32[]{:S(2)}, u32[]{:S(2)}) collective-permute-start(bf16[152,2048]{1,0:T(8,128)(2,1)} %collective-permute-done.4), channel_id=1, source_target_pairs={{0,16},{16,0},{1,17},{17,1},{2,18},{18,2},{3,19},{19,3},{4,20},{20... | collective-permute-start | bytes 1867784 | tf_op jit(solution)/shard_map/ppermute | solution.py:321
  289.1 61.2 %collective-permute-start.6 = (bf16[256,2048]{1,0:T(8,128)(2,1)S(1)}, bf16[256,2048]{1,0:T(8,128)(2,1)}, u32[]{:S(2)}, u32[]{:S(2)}) collective-permute-start(bf16[256,2048]{1,0:T(8,128)(2,1)S(1)} %get-tuple-element.157), channel_id=1, source_target_pairs={{0,8},{8,0},{1,9},{9,1},{2,10},{10,2},{3,11},{11,3},{4,12},{12,4},... | collective-permute-start | bytes 3145736 | tf_op jit(solution)/shard_map/ppermute | solution.py:321
  290.3 62.9 %collective-permute-start.7 = (bf16[256,2048]{1,0:T(8,128)(2,1)}, bf16[256,2048]{1,0:T(8,128)(2,1)}, u32[]{:S(2)}, u32[]{:S(2)}) collective-permute-start(bf16[256,2048]{1,0:T(8,128)(2,1)} %get-tuple-element.158), channel_id=1, source_target_pairs={{0,8},{8,0},{1,9},{9,1},{2,10},{10,2},{3,11},{11,3},{4,12},{12,4},... | collective-permute-start | bytes 3145736 | tf_op jit(solution)/shard_map/ppermute | solution.py:321
  293.9 102.6 %collective-permute-start.21 = (bf16[512,2048]{1,0:T(8,128)(2,1)}, bf16[512,2048]{1,0:T(8,128)(2,1)}, u32[]{:S(2)}, u32[]{:S(2)}) collective-permute-start(bf16[512,2048]{1,0:T(8,128)(2,1)} %pad_maximum_fusion.6), channel_id=1, source_target_pairs={{0,1},{1,0},{2,3},{3,2},{4,5},{5,4},{6,7},{7,6},{8,9},{9,8},{10,11... | collective-permute-start | bytes 6291464 | tf_op jit(solution)/shard_map/ppermute | solution.py:321
  318.4 53.3 %collective-permute-start.18 = (bf16[256,2048]{1,0:T(8,128)(2,1)}, bf16[256,2048]{1,0:T(8,128)(2,1)}, u32[]{:S(2)}, u32[]{:S(2)}) collective-permute-start(bf16[256,2048]{1,0:T(8,128)(2,1)} %get-tuple-element.150), channel_id=1, source_target_pairs={{0,8},{8,0},{1,9},{9,1},{2,10},{10,2},{3,11},{11,3},{4,12},{12,4},... | collective-permute-start | bytes 3145736 | tf_op jit(solution)/shard_map/ppermute | solution.py:321
  350.3 42.9 %collective-permute-start.19 = (bf16[256,2048]{1,0:T(8,128)(2,1)}, bf16[256,2048]{1,0:T(8,128)(2,1)}, u32[]{:S(2)}, u32[]{:S(2)}) collective-permute-start(bf16[256,2048]{1,0:T(8,128)(2,1)} %get-tuple-element.148), channel_id=1, source_target_pairs={{0,8},{8,0},{1,9},{9,1},{2,10},{10,2},{3,11},{11,3},{4,12},{12,4},... | collective-permute-start | bytes 3145736 | tf_op jit(solution)/shard_map/ppermute | solution.py:321
  350.3 54.4 %collective-permute-start.9 = (bf16[512,2048]{1,0:T(8,128)(2,1)}, bf16[512,2048]{1,0:T(8,128)(2,1)}, u32[]{:S(2)}, u32[]{:S(2)}) collective-permute-start(bf16[512,2048]{1,0:T(8,128)(2,1)} %pad_maximum_fusion.4), channel_id=1, source_target_pairs={{0,1},{1,0},{2,3},{3,2},{4,5},{5,4},{6,7},{7,6},{8,9},{9,8},{10,11... | collective-permute-start | bytes 6291464 | tf_op jit(solution)/shard_map/ppermute | solution.py:321
  353.0 296.6 %reduce-scatter.16.cloned.1.call-start = ((), (), s32[]{:S(2)}) async-start(), calls=%async_computation.13 | async-start | bytes 6225920
  356.4 82.6 %collective-permute-start.8 = (bf16[512,2048]{1,0:T(8,128)(2,1)}, bf16[512,2048]{1,0:T(8,128)(2,1)}, u32[]{:S(2)}, u32[]{:S(2)}) collective-permute-start(bf16[512,2048]{1,0:T(8,128)(2,1)} %pad_maximum_fusion.3), channel_id=1, source_target_pairs={{0,1},{1,0},{2,3},{3,2},{4,5},{5,4},{6,7},{7,6},{8,9},{9,8},{10,11... | collective-permute-start | bytes 6291464 | tf_op jit(solution)/shard_map/ppermute | solution.py:321
  396.4 45.8 %collective-permute-start.20 = (bf16[512,2048]{1,0:T(8,128)(2,1)}, bf16[512,2048]{1,0:T(8,128)(2,1)S(1)}, u32[]{:S(2)}, u32[]{:S(2)}) collective-permute-start(bf16[512,2048]{1,0:T(8,128)(2,1)} %pad_maximum_fusion.5), channel_id=1, source_target_pairs={{0,1},{1,0},{2,3},{3,2},{4,5},{5,4},{6,7},{7,6},{8,9},{9,8},{10,11... | collective-permute-start | bytes 6291464 | tf_op jit(solution)/shard_map/ppermute | solution.py:321
  479.2 221.5 %reduce-scatter.8.cloned.1.call-start = ((), (), s32[]{:S(2)}) async-start(), calls=%async_computation.9 | async-start | bytes 6553600 | tf_op jit(solution)/shard_map/reduce_scatter | solution.py:392
  550.7 302.5 %reduce-scatter.10.cloned.1.call-start = ((), (), s32[]{:S(2)}) async-start(), calls=%async_computation.10 | async-start | bytes 6553600 | tf_op jit(solution)/shard_map/reduce_scatter | solution.py:392
  584.5 268.7 %reduce-scatter.12.cloned.1.call-start = ((), (), s32[]{:S(2)}) async-start(), calls=%async_computation.11 | async-start | bytes 3932160 | tf_op jit(solution)/shard_map/reduce_scatter | solution.py:392
  601.8 47.9 %collective-permute-start.23 = (bf16[512,2048]{1,0:T(8,128)(2,1)}, bf16[512,2048]{1,0:T(8,128)(2,1)}, u32[]{:S(2)}, u32[]{:S(2)}) collective-permute-start(bf16[512,2048]{1,0:T(8,128)(2,1)} %fusion.21), channel_id=1, source_target_pairs={{0,8},{8,0},{1,9},{9,1},{2,10},{10,2},{3,11},{11,3},{4,12},{12,4},... | collective-permute-start | bytes 6291464 | tf_op jit(solution)/shard_map/ppermute | solution.py:321
  685.0 325.7 %reduce-scatter.14.cloned.1.call-start = ((), (), s32[]{:S(2)}) async-start(), calls=%async_computation.12 | async-start | bytes 5898240 | tf_op jit(solution)/shard_map/reduce_scatter | solution.py:392
  701.8 68.0 %collective-permute-start.28 = (bf16[4,64,1216]{2,1,0:T(8,128)(2,1)S(1)}, bf16[4,64,1216]{2,1,0:T(8,128)(2,1)}, u32[]{:S(2)}, u32[]{:S(2)}) collective-permute-start(bf16[4,64,1216]{2,1,0:T(8,128)(2,1)S(1)} %dynamic-slice_bitcast_fusion.5), channel_id=1, source_target_pairs={{0,16},{16,0},{1,17},{17,1},{2,18},{18,2},{3,19},{19,3},{4,20},{20... | collective-permute-start | bytes 1867784 | tf_op jit(solution)/shard_map/ppermute | solution.py:321
  772.6 38.4 %collective-permute-start.29 = (bf16[2,256,768]{2,1,0:T(8,128)(2,1)}, bf16[2,256,768]{2,1,0:T(8,128)(2,1)}, u32[]{:S(2)}, u32[]{:S(2)}) collective-permute-start(bf16[2,256,768]{2,1,0:T(8,128)(2,1)} %dynamic-slice_bitcast_fusion.2), channel_id=1, source_target_pairs={{0,8},{8,0},{16,24},{24,16},{1,9},{9,1},{17,25},{25,17},{2,10},{10... | collective-permute-start | bytes 2359304 | tf_op jit(solution)/shard_map/ppermute | solution.py:321
  791.6 44.4 %collective-permute-start.27 = (bf16[1,256,768]{2,1,0:T(8,128)(2,1)}, bf16[1,256,768]{2,1,0:T(8,128)(2,1)}, u32[]{:S(2)}, u32[]{:S(2)}) collective-permute-start(bf16[1,256,768]{2,1,0:T(8,128)(2,1)} %constant_dynamic-slice_fusion.3), channel_id=1, source_target_pairs={{0,16},{8,24},{16,0},{24,8},{1,17},{9,25},{17,1},{25,9},{2,18},{10... | collective-permute-start | bytes 1179656 | tf_op jit(solution)/shard_map/ppermute | solution.py:321
  814.2 36.9 %collective-permute-start.30 = (bf16[1,256,768]{2,1,0:T(8,128)(2,1)}, bf16[1,256,768]{2,1,0:T(8,128)(2,1)}, u32[]{:S(2)}, u32[]{:S(2)}) collective-permute-start(bf16[1,256,768]{2,1,0:T(8,128)(2,1)} %constant_dynamic-slice_fusion.2), channel_id=1, source_target_pairs={{0,16},{8,24},{16,0},{24,8},{1,17},{9,25},{17,1},{25,9},{2,18},{10... | collective-permute-start | bytes 1179656 | tf_op jit(solution)/shard_map/ppermute | solution.py:321
  869.7 32.0 %collective-permute-start.32 = (bf16[16,64,2304]{2,1,0:T(8,128)(2,1)}, bf16[16,64,2304]{2,1,0:T(8,128)(2,1)}, u32[]{:S(2)}, u32[]{:S(2)}) collective-permute-start(bf16[16,64,2304]{2,1,0:T(8,128)(2,1)} %dynamic-slice_bitcast_fusion), channel_id=1, source_target_pairs={{0,1},{1,0},{2,3},{3,2},{4,5},{5,4},{6,7},{7,6},{8,9},{9,8},{10,11... | collective-permute-start | bytes 14155784 | tf_op jit(solution)/shard_map/ppermute | solution.py:321
  900.0 83.3 %collective-permute-start.43 = (bf16[512,2048]{1,0:T(8,128)(2,1)}, bf16[512,2048]{1,0:T(8,128)(2,1)}, u32[]{:S(2)}, u32[]{:S(2)}) collective-permute-start(bf16[512,2048]{1,0:T(8,128)(2,1)} %slice.376), channel_id=1, source_target_pairs={{0,1},{1,0},{2,3},{3,2},{4,5},{5,4},{6,7},{7,6},{8,9},{9,8},{10,11... | collective-permute-start | bytes 6291464 | tf_op jit(solution)/shard_map/ppermute | solution.py:321
  916.4 33.9 %collective-permute-start.39 = (bf16[48,2048]{1,0:T(8,128)(2,1)S(1)}, bf16[48,2048]{1,0:T(8,128)(2,1)S(1)}, u32[]{:S(2)}, u32[]{:S(2)}) collective-permute-start(bf16[48,2048]{1,0:T(8,128)(2,1)S(1)} %get-tuple-element.177), channel_id=1, source_target_pairs={{0,24},{8,16},{16,8},{24,0},{1,25},{9,17},{17,9},{25,1},{2,26},{10... | collective-permute-start | bytes 589832 | tf_op jit(solution)/shard_map/ppermute | solution.py:321
  917.8 43.8 %collective-permute-start.36 = (bf16[4,64,1216]{2,1,0:T(8,128)(2,1)S(1)}, bf16[4,64,1216]{2,1,0:T(8,128)(2,1)S(1)}, u32[]{:S(2)}, u32[]{:S(2)}) collective-permute-start(bf16[4,64,1216]{2,1,0:T(8,128)(2,1)S(1)} %dynamic-slice_bitcast_fusion.4), channel_id=1, source_target_pairs={{0,16},{16,0},{1,17},{17,1},{2,18},{18,2},{3,19},{19,3},{4,20},{20... | collective-permute-start | bytes 1867784 | tf_op jit(solution)/shard_map/ppermute | solution.py:321
  922.3 66.9 %collective-permute-start.45 = (bf16[512,2048]{1,0:T(8,128)(2,1)}, bf16[512,2048]{1,0:T(8,128)(2,1)}, u32[]{:S(2)}, u32[]{:S(2)}) collective-permute-start(bf16[512,2048]{1,0:T(8,128)(2,1)} %fusion.17), channel_id=1, source_target_pairs={{0,8},{8,0},{1,9},{9,1},{2,10},{10,2},{3,11},{11,3},{4,12},{12,4},... | collective-permute-start | bytes 6291464 | tf_op jit(solution)/shard_map/ppermute | solution.py:321
  (119 other events, 1533.9 us)
Sparse Core Ops, SparseCore 0:
  21.1 180.5 all-gather.4
  203.6 64.7 all-gather.8
  270.2 61.2 all-gather.10
  353.1 71.9 all-gather.6
  479.3 59.8 reduce-scatter.15
  550.8 62.0 reduce-scatter.7
  615.9 61.3 reduce-scatter.9
  685.1 44.3 reduce-scatter.11
  907.8 56.5 reduce-scatter.13

commit v3 on v2

--- a/solution.py
+++ b/solution.py
@@ -16,6 +16,7 @@
 ALL = ("line", "pair", "plane", "core")
 BF = jnp.bfloat16
 F32 = jnp.float32
+SMALL = pl.CostEstimate(flops=1000, transcendentals=0, bytes_accessed=1000)
 
 
 NT = (((1,), (1,)), ((), ()))
@@ -157,7 +158,6 @@
     q_width = pairs * wide
     kv_width = n_kv * HEAD_SIZE
     params = pltpu.CompilerParams(dimension_semantics=("arbitrary",))
-    flops = 4 * n_kv * tall * length * HEAD_SIZE
 
     def forward(at, seen, q_lin, kv, gain, cosine, sine):
         return pl.pallas_call(
@@ -173,9 +173,7 @@
                 jax.ShapeDtypeStruct((span, q_width), F32),
             ],
             compiler_params=params,
-            cost_estimate=pl.CostEstimate(
-                flops=flops * 4, transcendentals=n_kv * tall * length, bytes_accessed=8 * span * q_width
-            ),
+            cost_estimate=SMALL,
             name="attention_forward",
         )(seen, q_lin, kv, kv, gain, cosine, sine)
 
@@ -201,9 +199,7 @@
                 jax.ShapeDtypeStruct((pairs, 8, HEAD_SIZE), F32),
             ],
             compiler_params=params,
-            cost_estimate=pl.CostEstimate(
-                flops=flops * 10, transcendentals=n_kv * tall * length, bytes_accessed=16 * span * q_width
-            ),
+            cost_estimate=SMALL,
             name="attention_backward",
         )(seen, q_lin, kv, kv, gain, cosine, sine, o, inv, d)
 
@@ -250,10 +246,6 @@
     def window(at):
         return pl.BlockSpec((span, 2 * kv_width), lambda i: (at, 0))
 
-    cost = pl.CostEstimate(
-        flops=20 * span * kv_width, transcendentals=span * n_kv, bytes_accessed=16 * span * kv_width
-    )
-
     def forward(at, lin, gain, cosine, sine):
         return pl.pallas_call(
             forward_kernel,
@@ -262,7 +254,7 @@
             out_specs=window(0),
             out_shape=jax.ShapeDtypeStruct((span, 2 * kv_width), BF),
             compiler_params=params,
-            cost_estimate=cost,
+            cost_estimate=SMALL,
             name="key_forward",
         )(lin, gain, cosine, sine)
 
@@ -277,11 +269,35 @@
                 jax.ShapeDtypeStruct((8, HEAD_SIZE), F32),
             ],
             compiler_params=params,
-            cost_estimate=cost,
+            cost_estimate=SMALL,
             name="key_backward",
         )(lin, d, gain, cosine, sine)
 
     return forward, backward
+
+
+def two_gradients(n, dg, du):
+    tokens, width = n.shape
+    part = dg.shape[1]
+    unit = 256
+
+    def kernel(n_ref, dg_ref, du_ref, gate_ref, up_ref):
+        v = n_ref[...]
+        gate_ref[...] = dot(v, dg_ref[...], TN).astype(BF)
+        up_ref[...] = dot(v, du_ref[...], TN).astype(BF)
+
+    whole = pl.BlockSpec((tokens, part), lambda i: (0, 0))
+    out = pl.BlockSpec((unit, part), lambda i: (i, 0))
+    return pl.pallas_call(
+        kernel,
+        grid=(width // unit,),
+        in_specs=[pl.BlockSpec((tokens, unit), lambda i: (0, i)), whole, whole],
+        out_specs=[out, out],
+        out_shape=[jax.ShapeDtypeStruct((width, part), BF)] * 2,
+        compiler_params=pltpu.CompilerParams(dimension_semantics=("arbitrary",)),
+        cost_estimate=SMALL,
+        name="two_gradients",
+    )(n, dg, du)
 
 
 def mm(left, right):
@@ -399,10 +415,8 @@
                 bit *= 2
         return v
 
-    def near_and_far(chunks):
-        far = jnp.concatenate([pair_swap(v) for v in chunks])
-        near = jnp.concatenate(chunks)
-        return jnp.concatenate([near, core_swap(near)]), jnp.concatenate([far, core_swap(far)])
+    def both_cores(v):
+        return jnp.concatenate([v, core_swap(v)])
 
     def fold(partial):
         half = partial.shape[0] // 2
@@ -444,6 +458,10 @@
         out_rows = jnp.pad(w_out, ((0, per - w_out.shape[0]), (0, 0)))
         packed = jnp.concatenate([w_key, w_value, extra, w_query, out_rows], axis=1)
         packed = lax.all_gather(packed, ALL, axis=0, tiled=True)
+        wg = whole_rows(spread_line(column_part(w_gate), line).reshape(n_inner, 2 * per, part), part)
+        cut_up = column_part(w_up)
+        packed, w_down = tie(packed, w_down)
+        cut_down = lax.ppermute(w_down, ALL, spread)
         wkv = packed[:, :at_gain]
         wq = packed[:, at_query:at_out]
         wo = packed[:, at_out:].reshape(n_dev, per, width)[:, : w_out.shape[0]].reshape(-1, width)
@@ -452,11 +470,6 @@
         g_two = tail[:, 1]
         g_qk = tail[:, 2].reshape(n_dev, per)[:, : qk_gain.shape[0]].reshape(-1)
         g_query, g_key = g_qk[:HEAD_SIZE], g_qk[HEAD_SIZE:]
-
-        wg = whole_rows(spread_line(column_part(w_gate), line).reshape(n_inner, 2 * per, part), part)
-        wu = whole_rows(spread_line(column_part(w_up), line).reshape(n_inner, 2 * per, part), part)
-        cut_down = lax.ppermute(w_down, ALL, spread)
-        dy = dy_in.reshape(rows, width)
 
         base = here * span
         positions = (base + jnp.arange(span)).astype(F32)
@@ -478,9 +491,12 @@
         kv = [make_key(s, kv_lin, gain_key, cosine, sine) for s in range(seqs)]
         gathered = [gather_inner(v, here).reshape(length, 2 * kv_width) for v in kv]
         q_lin = mm(normed_b, wq)
+        gathered[0], cut_up = tie(gathered[0], cut_up)
         gathered[-1], cut_down, dy_in = tie(gathered[-1], cut_down, dy_in)
-        dy_near, dy_far = near_and_far(list(dy_in))
+        dy = dy_in.reshape(rows, width)
+        dy_far = pair_swap(dy)
         cut_down = spread_line(cut_down, line)
+        wu = whole_rows(spread_line(cut_up, line).reshape(n_inner, 2 * per, part), part)
         kept = []
         resids = []
         invs = []
@@ -488,7 +504,7 @@
         for s in range(seqs):
             o, total = attend(s, seen, q_lin, gathered[s], gain_row, cosine, sine)
             if s == seqs - 1:
-                o, cut_down = tie(o, cut_down)
+                o, cut_down, dy_far = tie(o, cut_down, dy_far)
                 wd = whole_rows(cut_down, width)
             kept.append((o, total))
             resid = x[s * span : (s + 1) * span] + mm(o, wo)
@@ -499,7 +515,8 @@
         mixed = jnp.concatenate([o for o, _ in kept])
         resid = jnp.concatenate(resids)
         inv_two = jnp.concatenate(invs)
-        n2_near, n2_far = near_and_far(n2s)
+        n2_near = both_cores(jnp.concatenate(n2s))
+        far = [pair_swap(v) for v in n2s]
 
         def expand(n2):
             gate = mm(n2, wg)
@@ -513,10 +530,14 @@
             return dg, (d_hidden * (gate * sigma)).astype(BF)
 
         gate_near, up_near, hidden_near = expand(n2_near)
+        hidden_near, *far = tie(hidden_near, *far)
+        n2_far = both_cores(jnp.concatenate(far))
         gate_far, up_far, hidden_far = expand(n2_far)
         hidden = jnp.concatenate([hidden_near, hidden_far])
         n2_all = jnp.concatenate([n2_near, n2_far])
 
+        dy_near = both_cores(dy)
+        dy_far = both_cores(dy_far)
         grad_down = mm_tn(hidden, jnp.concatenate([dy_near, dy_far])).astype(BF)
         wd, grad_down = tie(wd, grad_down)
         down_part = scatter_plane(grad_down, n_line)
@@ -525,12 +546,18 @@
         sent, dy_near = tie(sent, dy_near)
         dg_near, du_near = expand_back(dy_near, gate_near, up_near)
         dn2 = fold(mm_nt(dg_near, wg) + mm_nt(du_near, wu))
-        grad_gate = mm_tn(n2_all, jnp.concatenate([dg_near, dg_far])).astype(BF)
-        grad_up = mm_tn(n2_all, jnp.concatenate([du_near, du_far])).astype(BF)
+        grad_gate, grad_up = two_gradients(
+            n2_all, jnp.concatenate([dg_near, dg_far]), jnp.concatenate([du_near, du_far])
+        )
         got = pair_swap(sent)
         gate_part = scatter_plane(grad_gate, n_inner)
         up_part = scatter_plane(grad_up, n_inner)
-        got, dn2, grad_gate, grad_up, down_part = tie(got, dn2, grad_gate, grad_up, down_part)
+        dn2, hidden_near, hidden_far = tie(dn2, hidden_near, hidden_far)
+        sent_out = fold(mm(hidden_far, wd)).astype(BF)
+        kept_out = fold(mm(hidden_near, wd))
+        got, dn2, grad_gate, grad_up, down_part, sent_out, kept_out = tie(
+            got, dn2, grad_gate, grad_up, down_part, sent_out, kept_out
+        )
         down_sum = sum_pieces(down_part, "line", n_line, line).astype(BF)
         dn2 = dn2 + got.astype(F32)
         back_two, terms_two = rms_back(resid, inv_two, g_two, dn2)
@@ -555,8 +582,10 @@
         drb = d_resid.astype(BF)
         dm = mm_nt(drb, wo).astype(BF)
         out_part = scatter_plane(fold_core(mm_tn(mixed, drb).astype(BF)), n_inner)
-        dm, down_sum, gate_part = tie(dm, down_sum, gate_part)
+        output = resid + (kept_out + pair_swap(sent_out).astype(F32))
+        dm, down_sum, gate_part, up_part = tie(dm, down_sum, gate_part, up_part)
         gate_sum = sum_pieces(gate_part.reshape(n_line, n_tp, per, part), "line", n_line, line)
+        up_sum = sum_pieces(up_part.reshape(n_line, n_tp, per, part), "line", n_line, line)
         dq = []
         dkv = []
         gains_q = []
@@ -568,14 +597,11 @@
             gains_q.append(jnp.sum(dg_s[:, 0], axis=0))
             both = jnp.concatenate([dk_s, dv_s], axis=1)
             if s == seqs - 1:
-                both, hidden_near, hidden_far, gate_sum = tie(both, hidden_near, hidden_far, gate_sum)
+                both, gate_sum, up_sum, output = tie(both, gate_sum, up_sum, output)
             dkv.append(scatter_inner(both.reshape(n_inner, span, 2 * kv_width), here))
         d_down = lax.ppermute(down_sum, ALL, [(b, a) for a, b in spread]).astype(F32)
-        sent = fold(mm(hidden_far, wd)).astype(BF)
-        output = resid + (fold(mm(hidden_near, wd)) + pair_swap(sent).astype(F32))
         result = output.astype(BF).reshape(seqs, span, width)
-        dkv[-1], up_part, out_part = tie(dkv[-1], up_part, out_part)
-        up_sum = sum_pieces(up_part.reshape(n_line, n_tp, per, part), "line", n_line, line)
+        dkv[-1], out_part = tie(dkv[-1], out_part)
         d_out = sum_pieces(out_part, INNER, n_inner, here)
         d_kvs = []
         gains_k = []
@@ -587,7 +613,7 @@
         d_lin = jnp.concatenate([jnp.concatenate(dq), jnp.concatenate(d_kvs)], axis=1)
         grad_qkv = mm_tn(normed_b, d_lin).astype(BF)
         qkv_part = scatter_plane(fold_core(grad_qkv), n_inner)
-        d_lin, grad_qkv, up_sum, d_out = tie(d_lin, grad_qkv, up_sum, d_out)
+        d_lin, grad_qkv, d_out = tie(d_lin, grad_qkv, d_out)
         d_gate = column_whole(gate_sum)
         d_up = column_whole(up_sum)
         dn = mm_nt(d_lin[:, :q_width], wq) + mm_nt(d_lin[:, q_width:], wkv)
@@ -596,7 +622,6 @@
         d_inputs = (d_resid + back_one).reshape(seqs, span, width)
 
         gains = butterfly_sum(jnp.concatenate([grad_gain_one, grad_gain_two, grad_qk]))
-        qkv_part, d_gate, d_up, d_out, result = tie(qkv_part, d_gate, d_up, d_out, result)
         d_qkv = sum_pieces(qkv_part, INNER, n_inner, here)
         d_attn_gain = lax.dynamic_slice_in_dim(gains, flat * per, per)
         d_ffn_gain = lax.dynamic_slice_in_dim(gains, width + flat * per, per)

time: 1060 us -> 1080 us (1.019)
  waiting for transfers between devices: 339 us -> 395 us
  local copies, waits for them, and re-layouts: 129 us -> 94.3 us
  Pallas kernels: 109 us -> 139 us
  matrix products: 217 us -> 195 us
    all_gather x1, waiting for transfers between devices: 18.1 us -> 70.1 us  [body(): packed = lax.all_gather(packed, ALL, axis=0, tiled=True)]
    pallas_call x0 -> x1, Pallas kernels: none -> 29.1 us  [two_gradients(): pl.pallas_call(kernel, grid=(width // unit,), in_specs=[pl.BlockSpec((tok...]
    dot_general x24 -> x22, matrix products: 217 us -> 195 us  [dot(): return lax.dot_general(a, b, dims, preferred_element_type=F32)]
    unnamed x187 -> x152, local copies, waits for them, and re-layouts: 43.7 us -> 26.6 us
    reshape x2 -> x0, local copies, waits for them, and re-layouts: 15.8 us -> none  [scatter_plane(): held = whole.reshape(lead, n_plane * r, whole.shape[1])]
    ppermute x1, waiting for transfers between devices: 0.01 us -> 12.6 us  [body(): lax.ppermute(down_sum, ALL, [(b, a) for a, b in spread]).astype(F32)]
    ppermute x53 -> x52, starting transfers between devices: 99.4 us -> 112 us  [flip(): return lax.ppermute(v, axis, [(i, i ^ bit) for i in range(size)])]
    all_gather x3, starting transfers between devices: 11.9 us -> 0.51 us  [whole_rows(): return lax.all_gather(held, 'plane', axis=1, tiled=True).reshape(-1, width)]
  transfers between devices with their start and end apart: 64 -> 63, of which waited for: 27 -> 28; matrix products, arithmetic and copies ran while one was open for 40% -> 33% of each run, Pallas kernels for 10% -> 13%
where the time goes in v3:
time: 1080 us; the launch traced here: 1070 us
  waiting for transfers between devices  395 us (37%)
  matrix products  195 us (18%)
  Pallas kernels  139 us (13%)
  starting transfers between devices  117 us (11%)
  other arithmetic  115 us (11%)
  local copies, waits for them, and re-layouts  94.3 us (9%)
  between operations  15.6 us (1%)
    ppermute x52, waiting for transfers between devices, flip(): return lax.ppermute(v, axis, [(i, i ^ bit) for i in range(size)])  312 us
    dot_general x22, matrix products, dot(): return lax.dot_general(a, b, dims, preferred_element_type=F32)  195 us
    ppermute x52, starting transfers between devices, flip(): return lax.ppermute(v, axis, [(i, i ^ bit) for i in range(size)])  112 us
    all_gather x1, waiting for transfers between devices, body(): packed = lax.all_gather(packed, ALL, axis=0, tiled=True)  70.1 us
    pallas_call x2, Pallas kernels, backward(): pl.pallas_call(backward_kernel, grid_spec=pltpu.PrefetchScalarGridSpec(nu...  61.4 us
    pallas_call x2, Pallas kernels, forward(): pl.pallas_call(forward_kernel, grid_spec=pltpu.PrefetchScalarGridSpec(num...  32.9 us
    pallas_call x1, Pallas kernels, two_gradients(): pl.pallas_call(kernel, grid=(width // unit,), in_specs=[pl.BlockSpec((tok...  29.1 us
    unnamed x152, local copies, waits for them, and re-layouts  26.6 us
  transfers between devices with their start and end apart: 63, of which 28 were waited for; matrix products, arithmetic and copies ran while one was open for 33% of the time, Pallas kernels for 13%

profile of v3, /device:TPU:12, one launch (start us, length us, event | category | flops | bytes accessed | tf_op | source)
XLA Modules:
  0.0 1071.1 jit_solution(18414645798231379967)
XLA Ops:
  49.9 39.6 %collective-permute-done.15 = bf16[2,128,1216]{1,2,0:T(8,128)(2,1)} collective-permute-done((bf16[2,128,1216]{1,2,0:T(8,128)(2,1)}, bf16[2,128,1216]{1,2,0:T(8,128)(2,1)}, u32[]{:S(2)}, u32[]{:S(2)}) %collective-permute-start.15) | collective-permute-done | bytes 622624 | tf_op jit(solution)/shard_map/ppermute | solution.py:337
  96.7 70.1 %all-gather.5.cloned.1.call-done = bf16[2048,4480]{1,0:T(8,128)(2,1)} async-done(((bf16[64,4480]{1,0:T(8,128)(2,1)}), bf16[2048,4480]{1,0:T(8,128)(2,1)}) %all-gather.5.cloned.1.call-update) | async-done | bytes 18350096 | tf_op jit(solution)/shard_map/all_gather | solution.py:460
  181.6 17.4 %collective-permute-done.5 = bf16[1,256,768]{2,1,0:T(8,128)(2,1)S(1)} collective-permute-done((bf16[1,256,768]{2,1,0:T(8,128)(2,1)}, bf16[1,256,768]{2,1,0:T(8,128)(2,1)S(1)}, u32[]{:S(2)}, u32[]{:S(2)}) %collective-permute-start.5) | collective-permute-done | bytes 393248 | tf_op jit(solution)/shard_map/ppermute | solution.py:337
  208.2 21.8 %collective-permute-done.6 = bf16[2,256,768]{2,1,0:T(8,128)(2,1)} collective-permute-done((bf16[2,256,768]{2,1,0:T(8,128)(2,1)}, bf16[2,256,768]{2,1,0:T(8,128)(2,1)}, u32[]{:S(2)}, u32[]{:S(2)}) %collective-permute-start.6) | collective-permute-done | bytes 786464 | tf_op jit(solution)/shard_map/ppermute | solution.py:337
  245.8 30.0 %collective-permute-done.16 = bf16[2,128,1216]{1,2,0:T(8,128)(2,1)} collective-permute-done((bf16[2,128,1216]{1,2,0:T(8,128)(2,1)}, bf16[2,128,1216]{1,2,0:T(8,128)(2,1)}, u32[]{:S(2)}, u32[]{:S(2)}) %collective-permute-start.16) | collective-permute-done | bytes 622624 | tf_op jit(solution)/shard_map/ppermute | solution.py:337
  287.6 9.1 slice.236
  309.6 16.1 %attention_forward.3 = (bf16[256,1536]{1,0:T(8,128)(2,1)}, f32[256,1536]{1,0:T(8,128)}) custom-call(s32[1]{0:T(128)} %bitcast.seen_ref, f32[512,1536]{1,0:T(8,128)} %fusion.15.q_ref, bf16[1024,768]{1,0:T(8,128)(2,1)} %bitcast.329, bf16[1024,768]{1,0:T(8,128)(2,1)} %bitcast.330, f32[1,64]{1,0:T(1,128)} %reshape.780.gain_ref, ...), custom_call_target="tpu_custom_call" | custom-call | flops 1000 | bytes 1000 | tf_op jit(solution)/shard_map/attention_forward/pallas_call | solution.py:163
  331.2 16.8 %attention_forward.2 = (bf16[256,1536]{1,0:T(8,128)(2,1)}, f32[256,1536]{1,0:T(8,128)}) custom-call(s32[1]{0:T(128)} %bitcast.seen_ref, f32[512,1536]{1,0:T(8,128)} %fusion.15.q_ref, bf16[1024,768]{1,0:T(8,128)(2,1)} %bitcast.333, bf16[1024,768]{1,0:T(8,128)(2,1)} %bitcast.334, f32[1,64]{1,0:T(1,128)} %reshape.780.gain_ref, ...), custom_call_target="tpu_custom_call" | custom-call | flops 1000 | bytes 1000 | tf_op jit(solution)/shard_map/attention_forward/pallas_call | solution.py:163
  371.7 11.3 %fusion.45 = f32[1024,1216]{1,0:T(8,128)} fusion(bf16[2048,1216]{1,0:T(8,128)(2,1)} %bitcast.420, bf16[512,2048]{1,0:T(8,128)(2,1)} %collective-permute-done.11, bf16[256,2048]{1,0:T(8,128)(2,1)} %get-tuple-element.166, bf16[256,2048]{1,0:T(8,128)(2,1)S(1)} %get-tuple-element.168), kind=kOutput, calls=%fused_computation.92 | convolution fusion | flops 5112856576 | bytes 14155776 | tf_op jit(solution)/shard_map/dot_general | solution.py:28
  383.0 14.3 %multiply_convert_fusion.5 = (bf16[1024,1216]{1,0:T(8,128)(2,1)}, f32[1024,1216]{1,0:T(8,128)}) fusion(f32[1024,1216]{1,0:T(8,128)} %fusion.45, bf16[2048,1216]{1,0:T(8,128)(2,1)} %bitcast.426, bf16[512,2048]{1,0:T(8,128)(2,1)} %collective-permute-done.11, bf16[256,2048]{1,0:T(8,128)(2,1)} %get-tuple-element.166, bf16[256,2048]{1,0:T(8,128)(2,1)S(1)} %get-tuple-element.168), kind=kOutput, calls=%fused_computation.31 | convolution fusion | flops 5120327680 | bytes 21626880 | tf_op jit(solution)/shard_map/dot_general | solution.py:28
  397.3 17.9 %collective-permute-done.18 = bf16[256,2048]{1,0:T(8,128)(2,1)S(1)} collective-permute-done((bf16[256,2048]{1,0:T(8,128)(2,1)}, bf16[256,2048]{1,0:T(8,128)(2,1)S(1)}, u32[]{:S(2)}, u32[]{:S(2)}) %collective-permute-start.18) | collective-permute-done | bytes 1048608 | tf_op jit(solution)/shard_map/ppermute | solution.py:337
  427.7 9.9 multiply_convert_fusion.4
  439.7 14.9 %fusion.9 = bf16[1216,2048]{1,0:T(8,128)(2,1)} fusion(bf16[512,2048]{1,0:T(8,128)(2,1)S(1)} %collective-permute-done.10, bf16[512,2048]{1,0:T(8,128)(2,1)} %collective-permute-done.4, bf16[512,2048]{1,0:T(8,128)(2,1)S(1)} %collective-permute-done.20, bf16[512,2048]{1,0:T(8,128)(2,1)} %bitcast.19, bf16[1024,1216]{1,0:T(8,128)(2,1)} %get-tuple-element.126, ...), kind=kOutput, calls=%fused_computation.11 | convolution fusion | flops 10246553600 | bytes 18350080 | tf_op jit(solution)/shard_map/dot_general | solution.py:28
  460.3 13.7 %multiply_convert_fusion.2 = (bf16[1024,1216]{1,0:T(8,128)(2,1)S(1)}, bf16[1024,1216]{1,0:T(8,128)(2,1)S(1)}) fusion(f32[1024,1216]{1,0:T(8,128)} %fusion.80, f32[1024,1216]{1,0:T(8,128)} %get-tuple-element.256, bf16[1216,2048]{1,0:T(8,128)(2,1)} %bitcast.432, bf16[512,2048]{1,0:T(8,128)(2,1)} %copy-done.60, bf16[512,2048]{1,0:T(8,128)(2,1)} %collective-permute-done.4), kind=kOutput, calls=%fused_computation.26 | convolution fusion | flops 5124849664 | bytes 24117248 | tf_op jit(solution)/shard_map/dot_general | solution.py:28
  473.9 10.7 fusion.81
  484.6 9.8 convolution_add_fusion.1
  501.1 11.3 %multiply_convert_fusion = (bf16[1024,1216]{1,0:T(8,128)(2,1)S(1)}, bf16[1024,1216]{1,0:T(8,128)(2,1)S(1)}) fusion(f32[1024,1216]{1,0:T(8,128)} %fusion.45, f32[1024,1216]{1,0:T(8,128)} %get-tuple-element.254, bf16[1024,2048]{1,0:T(8,128)(2,1)S(1)} %pad_maximum_fusion.3, bf16[1216,2048]{1,0:T(8,128)(2,1)} %bitcast.433), kind=kOutput, calls=%fused_computation.24 | convolution fusion | flops 5116461056 | bytes 24117248 | tf_op jit(solution)/shard_map/dot_general | solution.py:28
  519.2 29.1 %two_gradients.1 = (bf16[2048,1216]{1,0:T(8,128)(2,1)}, bf16[2048,1216]{1,0:T(8,128)(2,1)}) custom-call(bf16[2048,2048]{1,0:T(8,128)(2,1)} %copy-done.9, bf16[2048,1216]{1,0:T(8,128)(2,1)} %pad_maximum_fusion.dg_ref, bf16[2048,1216]{1,0:T(8,128)(2,1)} %pad_maximum_fusion.1.du_ref), custom_call_target="tpu_custom_call" | custom-call | flops 1000 | bytes 1000 | tf_op jit(solution)/shard_map/two_gradients/pallas_call | solution.py:291
  548.5 10.8 %fusion.82 = f32[1024,2048]{1,0:T(8,128)} fusion(bf16[1024,1216]{1,0:T(8,128)(2,1)} %copy-done.22, bf16[2048,1216]{1,0:T(8,128)(2,1)} %bitcast.422), kind=kOutput, calls=%fused_computation.265 | convolution fusion | flops 5100273664 | bytes 15859712 | tf_op jit(solution)/shard_map/dot_general | solution.py:28
  559.3 9.6 convolution_add_fusion
  617.4 36.1 %collective-permute-done.22 = bf16[512,2048]{1,0:T(8,128)(2,1)} collective-permute-done((bf16[512,2048]{1,0:T(8,128)(2,1)}, bf16[512,2048]{1,0:T(8,128)(2,1)}, u32[]{:S(2)}, u32[]{:S(2)}) %collective-permute-start.22) | collective-permute-done | bytes 2097184 | tf_op jit(solution)/shard_map/ppermute | solution.py:337
  685.6 13.2 %collective-permute-start.26 = (bf16[152,2048]{1,0:T(8,128)(2,1)S(1)}, bf16[152,2048]{1,0:T(8,128)(2,1)S(1)}, u32[]{:S(2)}, u32[]{:S(2)}) collective-permute-start(bf16[152,2048]{1,0:T(8,128)(2,1)S(1)} %dynamic-slice_bitcast_fusion.6), channel_id=1, source_target_pairs={{0,16},{16,0},{1,17},{17,1},{2,18},{18,2},{3,19},{19,3},{4,20},{20... | collective-permute-start | bytes 1867784 | tf_op jit(solution)/shard_map/ppermute | solution.py:337
  698.8 8.7 convolution_convert_fusion.2.d_ref
  707.5 50.5 %collective-permute-done.26 = bf16[152,2048]{1,0:T(8,128)(2,1)S(1)} collective-permute-done((bf16[152,2048]{1,0:T(8,128)(2,1)S(1)}, bf16[152,2048]{1,0:T(8,128)(2,1)S(1)}, u32[]{:S(2)}, u32[]{:S(2)}) %collective-permute-start.26) | collective-permute-done | bytes 622624 | tf_op jit(solution)/shard_map/ppermute | solution.py:337
  765.9 30.6 %attention_backward.2 = (bf16[256,1536]{1,0:T(8,128)(2,1)}, bf16[1024,384]{1,0:T(8,128)(2,1)}, bf16[1024,384]{1,0:T(8,128)(2,1)}, f32[3,8,64]{2,1,0:T(8,128)}) custom-call(s32[1]{0:T(128)} %bitcast.seen_ref, f32[512,1536]{1,0:T(8,128)} %fusion.15.q_ref, bf16[1024,768]{1,0:T(8,128)(2,1)} %bitcast.335, bf16[1024,768]{1,0:T(8,128)(2,1)} %bitcast.336, ...), custom_call_target="tpu_custom_call" | custom-call | flops 1000 | bytes 1000 | tf_op jit(solution)/shard_map/attention_backward/pallas_call | solution.py:181
  796.5 30.8 %attention_backward.3 = (bf16[256,1536]{1,0:T(8,128)(2,1)}, bf16[1024,384]{1,0:T(8,128)(2,1)}, bf16[1024,384]{1,0:T(8,128)(2,1)}, f32[3,8,64]{2,1,0:T(8,128)}) custom-call(s32[1]{0:T(128)} %bitcast.seen_ref, f32[512,1536]{1,0:T(8,128)} %fusion.15.q_ref, bf16[1024,768]{1,0:T(8,128)(2,1)} %bitcast.331, bf16[1024,768]{1,0:T(8,128)(2,1)} %bitcast.332, ...), custom_call_target="tpu_custom_call" | custom-call | flops 1000 | bytes 1000 | tf_op jit(solution)/shard_map/attention_backward/pallas_call | solution.py:181
  852.9 19.3 %collective-permute-start.31 = (bf16[1,256,768]{2,1,0:T(8,128)(2,1)}, bf16[1,256,768]{2,1,0:T(8,128)(2,1)S(1)}, u32[]{:S(2)}, u32[]{:S(2)}) collective-permute-start(bf16[1,256,768]{2,1,0:T(8,128)(2,1)} %constant_dynamic-slice_fusion.3), channel_id=1, source_target_pairs={{0,16},{8,24},{16,0},{24,8},{1,17},{9,25},{17,1},{25,9},{2,18},{10... | collective-permute-start | bytes 1179656 | tf_op jit(solution)/shard_map/ppermute | solution.py:337
  874.3 21.1 %collective-permute-start.33 = (bf16[1,256,768]{2,1,0:T(8,128)(2,1)}, bf16[1,256,768]{2,1,0:T(8,128)(2,1)}, u32[]{:S(2)}, u32[]{:S(2)}) collective-permute-start(bf16[1,256,768]{2,1,0:T(8,128)(2,1)} %constant_dynamic-slice_fusion.2), channel_id=1, source_target_pairs={{0,16},{8,24},{16,0},{24,8},{1,17},{9,25},{17,1},{25,9},{2,18},{10... | collective-permute-start | bytes 1179656 | tf_op jit(solution)/shard_map/ppermute | solution.py:337
  942.1 12.6 %collective-permute-done.53 = bf16[152,2048]{1,0:T(8,128)(2,1)S(1)} collective-permute-done((bf16[152,2048]{1,0:T(8,128)(2,1)S(1)}, bf16[152,2048]{1,0:T(8,128)(2,1)S(1)}, u32[]{:S(2)}, u32[]{:S(2)}) %collective-permute-start.53) | collective-permute-done | bytes 622624 | tf_op jit(solution)/shard_map/ppermute | solution.py:602
  979.9 12.8 %collective-permute-done.36 = bf16[48,2048]{1,0:T(8,128)(2,1)S(1)} collective-permute-done((bf16[48,2048]{1,0:T(8,128)(2,1)S(1)}, bf16[48,2048]{1,0:T(8,128)(2,1)S(1)}, u32[]{:S(2)}, u32[]{:S(2)}) %collective-permute-start.36) | collective-permute-done | bytes 196640 | tf_op jit(solution)/shard_map/ppermute | solution.py:337
  1001.2 8.8 fusion.36
  1045.4 10.8 %collective-permute-done.45 = bf16[64,2304]{1,0:T(8,128)(2,1)S(1)} collective-permute-done((bf16[64,2304]{1,0:T(8,128)(2,1)S(1)}, bf16[64,2304]{1,0:T(8,128)(2,1)S(1)}, u32[]{:S(2)}, u32[]{:S(2)}) %collective-permute-start.45) | collective-permute-done | bytes 294944 | tf_op jit(solution)/shard_map/ppermute | solution.py:337
  (441 shorter events, 416.0 us)
Async XLA Ops:
  7.2 159.6 %all-gather.5.cloned.1.call-start = ((), (), s32[]{:S(2)}) async-start(), calls=%async_computation.5 | async-start | bytes 18923520 | tf_op jit(solution)/shard_map/all_gather | solution.py:460
  21.0 348.7 %all-gather.9.cloned.1.call-start = ((), (), s32[]{:S(2)}) async-start(), calls=%async_computation.7 | async-start | bytes 6553600 | tf_op jit(solution)/shard_map/all_gather | solution.py:400
  23.4 72.0 %collective-permute-start.7 = (bf16[64,1216]{1,0:T(8,128)(2,1)}, bf16[64,1216]{1,0:T(8,128)(2,1)}, u32[]{:S(2)}, u32[]{:S(2)}) collective-permute-start(bf16[64,1216]{1,0:T(8,128)(2,1)} %get-tuple-element.236), channel_id=1, source_target_pairs={{0,1},{1,0},{8,9},{9,8},{2,3},{3,2},{10,11},{11,10},{4,5},{5,4},{1... | collective-permute-start | bytes 466952 | tf_op jit(solution)/shard_map/ppermute | solution.py:337
  23.4 72.0 %collective-permute-start.8 = (bf16[64,1216]{1,0:T(8,128)(2,1)}, bf16[64,1216]{1,0:T(8,128)(2,1)}, u32[]{:S(2)}, u32[]{:S(2)}) collective-permute-start(bf16[64,1216]{1,0:T(8,128)(2,1)} %get-tuple-element.238), channel_id=1, source_target_pairs={{0,8},{1,9},{8,0},{9,1},{2,10},{3,11},{10,2},{11,3},{4,12},{5,13},... | collective-permute-start | bytes 466952 | tf_op jit(solution)/shard_map/ppermute | solution.py:337
  27.2 68.2 %collective-permute-start.9 = (bf16[64,1216]{1,0:T(8,128)(2,1)}, bf16[64,1216]{1,0:T(8,128)(2,1)}, u32[]{:S(2)}, u32[]{:S(2)}) collective-permute-start(bf16[64,1216]{1,0:T(8,128)(2,1)} %get-tuple-element.237), channel_id=1, source_target_pairs={{0,9},{1,8},{8,1},{9,0},{2,11},{3,10},{10,3},{11,2},{4,13},{5,12},... | collective-permute-start | bytes 466952 | tf_op jit(solution)/shard_map/ppermute | solution.py:337
  43.5 46.0 %collective-permute-start.15 = (bf16[2,128,1216]{1,2,0:T(8,128)(2,1)}, bf16[2,128,1216]{1,2,0:T(8,128)(2,1)}, u32[]{:S(2)}, u32[]{:S(2)}) collective-permute-start(bf16[2,128,1216]{1,2,0:T(8,128)(2,1)} %copy.170), channel_id=1, source_target_pairs={{0,16},{16,0},{1,17},{17,1},{2,18},{18,2},{3,19},{19,3},{4,20},{20... | collective-permute-start | bytes 1867784 | tf_op jit(solution)/shard_map/ppermute | solution.py:337
  93.3 289.7 %all-gather.11.cloned.1.call-start = ((), (), s32[]{:S(2)}) async-start(), calls=%async_computation.8 | async-start | bytes 6553600 | tf_op jit(solution)/shard_map/all_gather | solution.py:400
  201.3 28.7 %collective-permute-start.6 = (bf16[2,256,768]{2,1,0:T(8,128)(2,1)}, bf16[2,256,768]{2,1,0:T(8,128)(2,1)}, u32[]{:S(2)}, u32[]{:S(2)}) collective-permute-start(bf16[2,256,768]{2,1,0:T(8,128)(2,1)} %maximum_bitcast_fusion.3), channel_id=1, source_target_pairs={{0,8},{8,0},{16,24},{24,16},{1,9},{9,1},{17,25},{25,17},{2,10},{10... | collective-permute-start | bytes 2359304 | tf_op jit(solution)/shard_map/ppermute | solution.py:337
  207.8 32.9 %collective-permute-start = (bf16[1,256,768]{2,1,0:T(8,128)(2,1)}, bf16[1,256,768]{2,1,0:T(8,128)(2,1)}, u32[]{:S(2)}, u32[]{:S(2)}) collective-permute-start(bf16[1,256,768]{2,1,0:T(8,128)(2,1)} %bitcast.387), channel_id=1, source_target_pairs={{0,16},{8,24},{16,0},{24,8},{1,17},{9,25},{17,1},{25,9},{2,18},{10... | collective-permute-start | bytes 1179656 | tf_op jit(solution)/shard_map/ppermute | solution.py:337
  233.9 42.0 %collective-permute-start.16 = (bf16[2,128,1216]{1,2,0:T(8,128)(2,1)}, bf16[2,128,1216]{1,2,0:T(8,128)(2,1)}, u32[]{:S(2)}, u32[]{:S(2)}) collective-permute-start(bf16[2,128,1216]{1,2,0:T(8,128)(2,1)} %copy.175), channel_id=1, source_target_pairs={{0,16},{16,0},{1,17},{17,1},{2,18},{18,2},{3,19},{19,3},{4,20},{20... | collective-permute-start | bytes 1867784 | tf_op jit(solution)/shard_map/ppermute | solution.py:337
  238.6 68.0 %collective-permute-start.2 = (bf16[152,2048]{1,0:T(8,128)(2,1)}, bf16[152,2048]{1,0:T(8,128)(2,1)}, u32[]{:S(2)}, u32[]{:S(2)}) collective-permute-start(bf16[152,2048]{1,0:T(8,128)(2,1)} %param.28), channel_id=1, source_target_pairs={{0,0},{1,2},{2,4},{3,6},{4,16},{5,18},{6,20},{7,22},{8,1},{9,3},{1... | collective-permute-start | bytes 1867784 | tf_op jit(solution)/shard_map/ppermute | solution.py:464
  242.9 60.9 %collective-permute-start.1 = (bf16[2,256,768]{2,1,0:T(8,128)(2,1)}, bf16[2,256,768]{2,1,0:T(8,128)(2,1)}, u32[]{:S(2)}, u32[]{:S(2)}) collective-permute-start(bf16[2,256,768]{2,1,0:T(8,128)(2,1)} %maximum_bitcast_fusion.2), channel_id=1, source_target_pairs={{0,8},{8,0},{16,24},{24,16},{1,9},{9,1},{17,25},{25,17},{2,10},{10... | collective-permute-start | bytes 2359304 | tf_op jit(solution)/shard_map/ppermute | solution.py:337
  278.8 175.7 %all-gather.7.cloned.1.call-start = ((), (), s32[]{:S(2)}) async-start(), calls=%async_computation.6 | async-start | bytes 6225920 | tf_op jit(solution)/shard_map/all_gather | solution.py:400
  306.5 42.8 %collective-permute-start.3 = (bf16[152,2048]{1,0:T(8,128)(2,1)}, bf16[152,2048]{1,0:T(8,128)(2,1)}, u32[]{:S(2)}, u32[]{:S(2)}) collective-permute-start(bf16[152,2048]{1,0:T(8,128)(2,1)} %collective-permute-done.2), channel_id=1, source_target_pairs={{0,16},{16,0},{1,17},{17,1},{2,18},{18,2},{3,19},{19,3},{4,20},{20... | collective-permute-start | bytes 1867784 | tf_op jit(solution)/shard_map/ppermute | solution.py:337
  309.6 46.6 %collective-permute-start.4 = (bf16[512,2048]{1,0:T(8,128)(2,1)}, bf16[512,2048]{1,0:T(8,128)(2,1)}, u32[]{:S(2)}, u32[]{:S(2)}) collective-permute-start(bf16[512,2048]{1,0:T(8,128)(2,1)} %bitcast.19), channel_id=1, source_target_pairs={{0,8},{8,0},{1,9},{9,1},{2,10},{10,2},{3,11},{11,3},{4,12},{12,4},... | collective-permute-start | bytes 6291464 | tf_op jit(solution)/shard_map/ppermute | solution.py:337
  367.2 30.1 %collective-permute-start.17 = (bf16[256,2048]{1,0:T(8,128)(2,1)S(1)}, bf16[256,2048]{1,0:T(8,128)(2,1)S(1)}, u32[]{:S(2)}, u32[]{:S(2)}) collective-permute-start(bf16[256,2048]{1,0:T(8,128)(2,1)S(1)} %get-tuple-element.168), channel_id=1, source_target_pairs={{0,8},{8,0},{1,9},{9,1},{2,10},{10,2},{3,11},{11,3},{4,12},{12,4},... | collective-permute-start | bytes 3145736 | tf_op jit(solution)/shard_map/ppermute | solution.py:337
  368.8 46.4 %collective-permute-start.18 = (bf16[256,2048]{1,0:T(8,128)(2,1)}, bf16[256,2048]{1,0:T(8,128)(2,1)S(1)}, u32[]{:S(2)}, u32[]{:S(2)}) collective-permute-start(bf16[256,2048]{1,0:T(8,128)(2,1)} %get-tuple-element.166), channel_id=1, source_target_pairs={{0,8},{8,0},{1,9},{9,1},{2,10},{10,2},{3,11},{11,3},{4,12},{12,4},... | collective-permute-start | bytes 3145736 | tf_op jit(solution)/shard_map/ppermute | solution.py:337
  369.2 284.2 %reduce-scatter.16.cloned.1.call-start = ((), (), s32[]{:S(2)}) async-start(), calls=%async_computation.13 | async-start | bytes 6225920
  460.0 299.0 %reduce-scatter.10.cloned.1.call-start = ((), (), s32[]{:S(2)}) async-start(), calls=%async_computation.10 | async-start | bytes 6553600 | tf_op jit(solution)/shard_map/reduce_scatter | solution.py:408
  548.4 210.6 %reduce-scatter.8.cloned.1.call-start = ((), (), s32[]{:S(2)}) async-start(), calls=%async_computation.9 | async-start | bytes 6553600 | tf_op jit(solution)/shard_map/reduce_scatter | solution.py:408
  574.2 337.6 %reduce-scatter.12.cloned.1.call-start = ((), (), s32[]{:S(2)}) async-start(), calls=%async_computation.11 | async-start | bytes 3932160 | tf_op jit(solution)/shard_map/reduce_scatter | solution.py:408
  605.3 48.2 %collective-permute-start.22 = (bf16[512,2048]{1,0:T(8,128)(2,1)}, bf16[512,2048]{1,0:T(8,128)(2,1)}, u32[]{:S(2)}, u32[]{:S(2)}) collective-permute-start(bf16[512,2048]{1,0:T(8,128)(2,1)} %fusion.23), channel_id=1, source_target_pairs={{0,8},{8,0},{1,9},{9,1},{2,10},{10,2},{3,11},{11,3},{4,12},{12,4},... | collective-permute-start | bytes 6291464 | tf_op jit(solution)/shard_map/ppermute | solution.py:337
  684.1 348.7 %reduce-scatter.14.cloned.1.call-start = ((), (), s32[]{:S(2)}) async-start(), calls=%async_computation.12 | async-start | bytes 5898240 | tf_op jit(solution)/shard_map/reduce_scatter | solution.py:408
  684.2 145.9 %collective-permute-start.29 = (bf16[512,2048]{1,0:T(8,128)(2,1)}, bf16[512,2048]{1,0:T(8,128)(2,1)}, u32[]{:S(2)}, u32[]{:S(2)}) collective-permute-start(bf16[512,2048]{1,0:T(8,128)(2,1)} %fusion.22), channel_id=1, source_target_pairs={{0,8},{8,0},{1,9},{9,1},{2,10},{10,2},{3,11},{11,3},{4,12},{12,4},... | collective-permute-start | bytes 6291464 | tf_op jit(solution)/shard_map/ppermute | solution.py:337
  685.6 72.4 %collective-permute-start.26 = (bf16[152,2048]{1,0:T(8,128)(2,1)S(1)}, bf16[152,2048]{1,0:T(8,128)(2,1)S(1)}, u32[]{:S(2)}, u32[]{:S(2)}) collective-permute-start(bf16[152,2048]{1,0:T(8,128)(2,1)S(1)} %dynamic-slice_bitcast_fusion.6), channel_id=1, source_target_pairs={{0,16},{16,0},{1,17},{17,1},{2,18},{18,2},{3,19},{19,3},{4,20},{20... | collective-permute-start | bytes 1867784 | tf_op jit(solution)/shard_map/ppermute | solution.py:337
  761.0 74.7 %collective-permute-start.28 = (bf16[4,64,1216]{2,1,0:T(8,128)(2,1)}, bf16[4,64,1216]{2,1,0:T(8,128)(2,1)}, u32[]{:S(2)}, u32[]{:S(2)}) collective-permute-start(bf16[4,64,1216]{2,1,0:T(8,128)(2,1)} %dynamic-slice_bitcast_fusion.4), channel_id=1, source_target_pairs={{0,16},{16,0},{1,17},{17,1},{2,18},{18,2},{3,19},{19,3},{4,20},{20... | collective-permute-start | bytes 1867784 | tf_op jit(solution)/shard_map/ppermute | solution.py:337
  763.0 75.1 %collective-permute-start.27 = (bf16[4,64,1216]{2,1,0:T(8,128)(2,1)}, bf16[4,64,1216]{2,1,0:T(8,128)(2,1)}, u32[]{:S(2)}, u32[]{:S(2)}) collective-permute-start(bf16[4,64,1216]{2,1,0:T(8,128)(2,1)} %dynamic-slice_bitcast_fusion.5), channel_id=1, source_target_pairs={{0,16},{16,0},{1,17},{17,1},{2,18},{18,2},{3,19},{19,3},{4,20},{20... | collective-permute-start | bytes 1867784 | tf_op jit(solution)/shard_map/ppermute | solution.py:337
  841.1 31.1 %collective-permute-start.32 = (bf16[2,256,768]{2,1,0:T(8,128)(2,1)}, bf16[2,256,768]{2,1,0:T(8,128)(2,1)}, u32[]{:S(2)}, u32[]{:S(2)}) collective-permute-start(bf16[2,256,768]{2,1,0:T(8,128)(2,1)} %dynamic-slice_bitcast_fusion.2), channel_id=1, source_target_pairs={{0,8},{8,0},{16,24},{24,16},{1,9},{9,1},{17,25},{25,17},{2,10},{10... | collective-permute-start | bytes 2359304 | tf_op jit(solution)/shard_map/ppermute | solution.py:337
  852.9 42.5 %collective-permute-start.31 = (bf16[1,256,768]{2,1,0:T(8,128)(2,1)}, bf16[1,256,768]{2,1,0:T(8,128)(2,1)S(1)}, u32[]{:S(2)}, u32[]{:S(2)}) collective-permute-start(bf16[1,256,768]{2,1,0:T(8,128)(2,1)} %constant_dynamic-slice_fusion.3), channel_id=1, source_target_pairs={{0,16},{8,24},{16,0},{24,8},{1,17},{9,25},{17,1},{25,9},{2,18},{10... | collective-permute-start | bytes 1179656 | tf_op jit(solution)/shard_map/ppermute | solution.py:337
  874.3 35.5 %collective-permute-start.33 = (bf16[1,256,768]{2,1,0:T(8,128)(2,1)}, bf16[1,256,768]{2,1,0:T(8,128)(2,1)}, u32[]{:S(2)}, u32[]{:S(2)}) collective-permute-start(bf16[1,256,768]{2,1,0:T(8,128)(2,1)} %constant_dynamic-slice_fusion.2), channel_id=1, source_target_pairs={{0,16},{8,24},{16,0},{24,8},{1,17},{9,25},{17,1},{25,9},{2,18},{10... | collective-permute-start | bytes 1179656 | tf_op jit(solution)/shard_map/ppermute | solution.py:337
  939.6 24.3 %collective-permute-start.50 = (bf16[64,1216]{1,0:T(8,128)(2,1)S(1)}, bf16[64,1216]{1,0:T(8,128)(2,1)S(1)}, u32[]{:S(2)}, u32[]{:S(2)}) collective-permute-start(bf16[64,1216]{1,0:T(8,128)(2,1)S(1)} %get-tuple-element.207), channel_id=1, source_target_pairs={{0,1},{1,0},{8,9},{9,8},{2,3},{3,2},{10,11},{11,10},{4,5},{5,4},{1... | collective-permute-start | bytes 466952 | tf_op jit(solution)/shard_map/ppermute | solution.py:337
  1036.2 25.6 %collective-permute-start.46 = (bf16[64,2304]{1,0:T(8,128)(2,1)S(1)}, bf16[64,2304]{1,0:T(8,128)(2,1)S(1)}, u32[]{:S(2)}, u32[]{:S(2)}) collective-permute-start(bf16[64,2304]{1,0:T(8,128)(2,1)S(1)} %get-tuple-element.186), channel_id=1, source_target_pairs={{0,24},{8,16},{16,8},{24,0},{1,25},{9,17},{17,9},{25,1},{2,26},{10... | collective-permute-start | bytes 884744 | tf_op jit(solution)/shard_map/ppermute | solution.py:337
  (103 other events, 1249.5 us)
Sparse Core Ops, SparseCore 0:
  21.1 145.6 all-gather.4
  168.6 60.4 all-gather.8
  278.9 62.2 all-gather.10
  369.4 70.3 all-gather.6
  460.1 70.3 reduce-scatter.15
  548.5 72.9 reduce-scatter.9
  624.6 61.3 reduce-scatter.7
  688.9 50.9 reduce-scatter.11
  935.1 68.4 reduce-scatter.13

commit v4 on v3

--- a/solution.py
+++ b/solution.py
@@ -460,7 +460,8 @@
         packed = lax.all_gather(packed, ALL, axis=0, tiled=True)
         wg = whole_rows(spread_line(column_part(w_gate), line).reshape(n_inner, 2 * per, part), part)
         cut_up = column_part(w_up)
-        packed, w_down = tie(packed, w_down)
+        dy = dy_in.reshape(rows, width)
+        packed, w_down, cut_up, dy_far = tie(packed, w_down, cut_up, pair_swap(dy))
         cut_down = lax.ppermute(w_down, ALL, spread)
         wkv = packed[:, :at_gain]
         wq = packed[:, at_query:at_out]
@@ -491,10 +492,7 @@
         kv = [make_key(s, kv_lin, gain_key, cosine, sine) for s in range(seqs)]
         gathered = [gather_inner(v, here).reshape(length, 2 * kv_width) for v in kv]
         q_lin = mm(normed_b, wq)
-        gathered[0], cut_up = tie(gathered[0], cut_up)
-        gathered[-1], cut_down, dy_in = tie(gathered[-1], cut_down, dy_in)
-        dy = dy_in.reshape(rows, width)
-        dy_far = pair_swap(dy)
+        gathered[-1], cut_down = tie(gathered[-1], cut_down)
         cut_down = spread_line(cut_down, line)
         wu = whole_rows(spread_line(cut_up, line).reshape(n_inner, 2 * per, part), part)
         kept = []
@@ -504,7 +502,7 @@
         for s in range(seqs):
             o, total = attend(s, seen, q_lin, gathered[s], gain_row, cosine, sine)
             if s == seqs - 1:
-                o, cut_down, dy_far = tie(o, cut_down, dy_far)
+                o, cut_down = tie(o, cut_down)
                 wd = whole_rows(cut_down, width)
             kept.append((o, total))
             resid = x[s * span : (s + 1) * span] + mm(o, wo)
@@ -545,19 +543,17 @@
         sent = fold(mm_nt(dg_far, wg) + mm_nt(du_far, wu)).astype(BF)
         sent, dy_near = tie(sent, dy_near)
         dg_near, du_near = expand_back(dy_near, gate_near, up_near)
-        dn2 = fold(mm_nt(dg_near, wg) + mm_nt(du_near, wu))
         grad_gate, grad_up = two_gradients(
             n2_all, jnp.concatenate([dg_near, dg_far]), jnp.concatenate([du_near, du_far])
         )
-        got = pair_swap(sent)
+        got, dg_near, du_near, grad_gate, grad_up = tie(pair_swap(sent), dg_near, du_near, grad_gate, grad_up)
+        dn2 = fold(mm_nt(dg_near, wg) + mm_nt(du_near, wu))
         gate_part = scatter_plane(grad_gate, n_inner)
         up_part = scatter_plane(grad_up, n_inner)
         dn2, hidden_near, hidden_far = tie(dn2, hidden_near, hidden_far)
         sent_out = fold(mm(hidden_far, wd)).astype(BF)
         kept_out = fold(mm(hidden_near, wd))
-        got, dn2, grad_gate, grad_up, down_part, sent_out, kept_out = tie(
-            got, dn2, grad_gate, grad_up, down_part, sent_out, kept_out
-        )
+        dn2, down_part, sent_out, kept_out = tie(dn2, down_part, sent_out, kept_out)
         down_sum = sum_pieces(down_part, "line", n_line, line).astype(BF)
         dn2 = dn2 + got.astype(F32)
         back_two, terms_two = rms_back(resid, inv_two, g_two, dn2)
@@ -582,10 +578,8 @@
         drb = d_resid.astype(BF)
         dm = mm_nt(drb, wo).astype(BF)
         out_part = scatter_plane(fold_core(mm_tn(mixed, drb).astype(BF)), n_inner)
-        output = resid + (kept_out + pair_swap(sent_out).astype(F32))
-        dm, down_sum, gate_part, up_part = tie(dm, down_sum, gate_part, up_part)
+        dm, gate_part = tie(dm, gate_part)
         gate_sum = sum_pieces(gate_part.reshape(n_line, n_tp, per, part), "line", n_line, line)
-        up_sum = sum_pieces(up_part.reshape(n_line, n_tp, per, part), "line", n_line, line)
         dq = []
         dkv = []
         gains_q = []
@@ -597,11 +591,12 @@
             gains_q.append(jnp.sum(dg_s[:, 0], axis=0))
             both = jnp.concatenate([dk_s, dv_s], axis=1)
             if s == seqs - 1:
-                both, gate_sum, up_sum, output = tie(both, gate_sum, up_sum, output)
+                both, gate_sum, down_sum = tie(both, gate_sum, down_sum)
             dkv.append(scatter_inner(both.reshape(n_inner, span, 2 * kv_width), here))
         d_down = lax.ppermute(down_sum, ALL, [(b, a) for a, b in spread]).astype(F32)
-        result = output.astype(BF).reshape(seqs, span, width)
-        dkv[-1], out_part = tie(dkv[-1], out_part)
+        dkv[-1], out_part, up_part, sent_out = tie(dkv[-1], out_part, up_part, sent_out)
+        output = resid + (kept_out + pair_swap(sent_out).astype(F32))
+        up_sum = sum_pieces(up_part.reshape(n_line, n_tp, per, part), "line", n_line, line)
         d_out = sum_pieces(out_part, INNER, n_inner, here)
         d_kvs = []
         gains_k = []
@@ -613,7 +608,8 @@
         d_lin = jnp.concatenate([jnp.concatenate(dq), jnp.concatenate(d_kvs)], axis=1)
         grad_qkv = mm_tn(normed_b, d_lin).astype(BF)
         qkv_part = scatter_plane(fold_core(grad_qkv), n_inner)
-        d_lin, grad_qkv, d_out = tie(d_lin, grad_qkv, d_out)
+        d_lin, grad_qkv, d_out, up_sum, output = tie(d_lin, grad_qkv, d_out, up_sum, output)
+        result = output.astype(BF).reshape(seqs, span, width)
         d_gate = column_whole(gate_sum)
         d_up = column_whole(up_sum)
         dn = mm_nt(d_lin[:, :q_width], wq) + mm_nt(d_lin[:, q_width:], wkv)

time: 1080 us -> 1080 us (level)
    ppermute x1, waiting for transfers between devices: 0.01 us -> 31.1 us  [body(): cut_down = lax.ppermute(w_down, ALL, spread)]
    all_gather x1, waiting for transfers between devices: 70.1 us -> 40.1 us  [body(): packed = lax.all_gather(packed, ALL, axis=0, tiled=True)]
    ppermute x52, waiting for transfers between devices: 312 us -> 331 us  [flip(): return lax.ppermute(v, axis, [(i, i ^ bit) for i in range(size)])]
    ppermute x1, waiting for transfers between devices: 12.6 us -> 0.01 us  [body(): lax.ppermute(down_sum, ALL, [(b, a) for a, b in spread]).astype(F32)]
    unnamed x152 -> x174, local copies, waits for them, and re-layouts: 26.6 us -> 31.7 us
  transfers between devices with their start and end apart: 63 -> 63, of which waited for: 28 -> 27; matrix products, arithmetic and copies ran while one was open for 33% -> 32% of each run, Pallas kernels for 13% -> 12%
where the time goes in v4:
time: 1080 us
  waiting for transfers between devices  403 us (37%)
  matrix products  195 us (18%)
  Pallas kernels  139 us (13%)
  other arithmetic  115 us (11%)
  starting transfers between devices  114 us (11%)
  local copies, waits for them, and re-layouts  96.3 us (9%)
  between operations  15.6 us (1%)
    ppermute x52, waiting for transfers between devices, flip(): return lax.ppermute(v, axis, [(i, i ^ bit) for i in range(size)])  331 us
    dot_general x22, matrix products, dot(): return lax.dot_general(a, b, dims, preferred_element_type=F32)  195 us
    ppermute x52, starting transfers between devices, flip(): return lax.ppermute(v, axis, [(i, i ^ bit) for i in range(size)])  103 us
    pallas_call x2, Pallas kernels, backward(): pl.pallas_call(backward_kernel, grid_spec=pltpu.PrefetchScalarGridSpec(nu...  61.6 us
    all_gather x1, waiting for transfers between devices, body(): packed = lax.all_gather(packed, ALL, axis=0, tiled=True)  40.1 us
    pallas_call x2, Pallas kernels, forward(): pl.pallas_call(forward_kernel, grid_spec=pltpu.PrefetchScalarGridSpec(num...  32.9 us
    unnamed x174, local copies, waits for them, and re-layouts  31.7 us
    ppermute x1, waiting for transfers between devices, body(): cut_down = lax.ppermute(w_down, ALL, spread)  31.1 us
  transfers between devices with their start and end apart: 63, of which 27 were waited for; matrix products, arithmetic and copies ran while one was open for 32% of the time, Pallas kernels for 12%

profile of v4, /device:TPU:12, one launch (start us, length us, event | category | flops | bytes accessed | tf_op | source)
XLA Modules:
  0.0 1077.9 jit_solution(13804483519073860939)
XLA Ops:
  37.4 102.4 %collective-permute-done.15 = bf16[2,128,1216]{1,2,0:T(8,128)(2,1)} collective-permute-done((bf16[2,128,1216]{1,2,0:T(8,128)(2,1)}, bf16[2,128,1216]{1,2,0:T(8,128)(2,1)}, u32[]{:S(2)}, u32[]{:S(2)}) %collective-permute-start.15) | collective-permute-done | bytes 622624 | tf_op jit(solution)/shard_map/ppermute | solution.py:337
  147.2 40.1 %all-gather.5.cloned.1.call-done = bf16[2048,4480]{1,0:T(8,128)(2,1)} async-done(((bf16[64,4480]{1,0:T(8,128)(2,1)}), bf16[2048,4480]{1,0:T(8,128)(2,1)}) %all-gather.5.cloned.1.call-update) | async-done | bytes 18350096 | tf_op jit(solution)/shard_map/all_gather | solution.py:460
  212.0 30.3 %collective-permute-done.4 = bf16[1,256,768]{2,1,0:T(8,128)(2,1)S(1)} collective-permute-done((bf16[1,256,768]{2,1,0:T(8,128)(2,1)}, bf16[1,256,768]{2,1,0:T(8,128)(2,1)S(1)}, u32[]{:S(2)}, u32[]{:S(2)}) %collective-permute-start.4) | collective-permute-done | bytes 393248 | tf_op jit(solution)/shard_map/ppermute | solution.py:337
  255.1 8.6 collective-permute-done.16
  265.8 8.5 fusion.15.q_ref
  274.4 9.3 slice.234
  300.2 31.1 %collective-permute-done.8 = bf16[152,2048]{1,0:T(8,128)(2,1)} collective-permute-done((bf16[152,2048]{1,0:T(8,128)(2,1)S(1)}, bf16[152,2048]{1,0:T(8,128)(2,1)}, u32[]{:S(2)}, u32[]{:S(2)}) %collective-permute-start.8) | collective-permute-done | bytes 622624 | tf_op jit(solution)/shard_map/ppermute | solution.py:465
  331.2 16.1 %attention_forward.2 = (bf16[256,1536]{1,0:T(8,128)(2,1)}, f32[256,1536]{1,0:T(8,128)}) custom-call(s32[1]{0:T(128)} %bitcast.seen_ref, f32[512,1536]{1,0:T(8,128)} %fusion.15.q_ref, bf16[1024,768]{1,0:T(8,128)(2,1)} %bitcast.329, bf16[1024,768]{1,0:T(8,128)(2,1)} %bitcast.330, f32[1,64]{1,0:T(1,128)} %reshape.784.gain_ref, ...), custom_call_target="tpu_custom_call" | custom-call | flops 1000 | bytes 1000 | tf_op jit(solution)/shard_map/attention_forward/pallas_call | solution.py:163
  352.9 16.8 %attention_forward.3 = (bf16[256,1536]{1,0:T(8,128)(2,1)}, f32[256,1536]{1,0:T(8,128)}) custom-call(s32[1]{0:T(128)} %bitcast.seen_ref, f32[512,1536]{1,0:T(8,128)} %fusion.15.q_ref, bf16[1024,768]{1,0:T(8,128)(2,1)} %bitcast.333, bf16[1024,768]{1,0:T(8,128)(2,1)} %bitcast.334, f32[1,64]{1,0:T(1,128)} %reshape.784.gain_ref, ...), custom_call_target="tpu_custom_call" | custom-call | flops 1000 | bytes 1000 | tf_op jit(solution)/shard_map/attention_forward/pallas_call | solution.py:163
  390.6 11.3 %fusion.45 = f32[1024,1216]{1,0:T(8,128)} fusion(bf16[2048,1216]{1,0:T(8,128)(2,1)} %bitcast.420, bf16[512,2048]{1,0:T(8,128)(2,1)} %collective-permute-done.11, bf16[256,2048]{1,0:T(8,128)(2,1)} %get-tuple-element.172, bf16[256,2048]{1,0:T(8,128)(2,1)S(1)} %get-tuple-element.174), kind=kOutput, calls=%fused_computation.92 | convolution fusion | flops 5112856576 | bytes 14155776 | tf_op jit(solution)/shard_map/dot_general | solution.py:28
  402.0 14.3 %multiply_convert_fusion.5 = (bf16[1024,1216]{1,0:T(8,128)(2,1)}, f32[1024,1216]{1,0:T(8,128)}) fusion(f32[1024,1216]{1,0:T(8,128)} %fusion.45, bf16[2048,1216]{1,0:T(8,128)(2,1)} %bitcast.426, bf16[512,2048]{1,0:T(8,128)(2,1)} %collective-permute-done.11, bf16[256,2048]{1,0:T(8,128)(2,1)} %get-tuple-element.172, bf16[256,2048]{1,0:T(8,128)(2,1)S(1)} %get-tuple-element.174), kind=kOutput, calls=%fused_computation.31 | convolution fusion | flops 5120327680 | bytes 21626880 | tf_op jit(solution)/shard_map/dot_general | solution.py:28
  416.3 17.9 %collective-permute-done.18 = bf16[256,2048]{1,0:T(8,128)(2,1)S(1)} collective-permute-done((bf16[256,2048]{1,0:T(8,128)(2,1)}, bf16[256,2048]{1,0:T(8,128)(2,1)S(1)}, u32[]{:S(2)}, u32[]{:S(2)}) %collective-permute-start.18) | collective-permute-done | bytes 1048608 | tf_op jit(solution)/shard_map/ppermute | solution.py:337
  446.7 9.9 multiply_convert_fusion.4
  458.7 14.8 %fusion.9 = bf16[1216,2048]{1,0:T(8,128)(2,1)} fusion(bf16[512,2048]{1,0:T(8,128)(2,1)S(1)} %collective-permute-done.10, bf16[512,2048]{1,0:T(8,128)(2,1)} %collective-permute-done.3, bf16[512,2048]{1,0:T(8,128)(2,1)S(1)} %collective-permute-done.20, bf16[512,2048]{1,0:T(8,128)(2,1)} %bitcast.19, bf16[1024,1216]{1,0:T(8,128)(2,1)} %get-tuple-element.129, ...), kind=kOutput, calls=%fused_computation.11 | convolution fusion | flops 10246553600 | bytes 18350080 | tf_op jit(solution)/shard_map/dot_general | solution.py:28
  480.6 12.8 %multiply_convert_fusion.2 = (bf16[1024,1216]{1,0:T(8,128)(2,1)S(1)}, bf16[1024,1216]{1,0:T(8,128)(2,1)S(1)}) fusion(f32[1024,1216]{1,0:T(8,128)} %fusion.80, f32[1024,1216]{1,0:T(8,128)} %get-tuple-element.262, bf16[1216,2048]{1,0:T(8,128)(2,1)} %bitcast.432, bf16[512,2048]{1,0:T(8,128)(2,1)S(1)} %copy-done.70, bf16[512,2048]{1,0:T(8,128)(2,1)} %collective-permute-done.3), kind=kOutput, calls=%fused_computation.26 | convolution fusion | flops 5124849664 | bytes 24117248 | tf_op jit(solution)/shard_map/dot_general | solution.py:28
  493.4 11.3 %fusion.81 = f32[1024,2048]{1,0:T(8,128)} fusion(bf16[1024,1216]{1,0:T(8,128)(2,1)S(1)} %get-tuple-element.178, bf16[2048,1216]{1,0:T(8,128)(2,1)} %bitcast.421), kind=kOutput, calls=%fused_computation.264 | convolution fusion | flops 5100273664 | bytes 15859712 | tf_op jit(solution)/shard_map/dot_general | solution.py:28
  504.7 9.9 convolution_add_fusion.1
  521.6 11.9 %multiply_convert_fusion = (bf16[1024,1216]{1,0:T(8,128)(2,1)S(1)}, bf16[1024,1216]{1,0:T(8,128)(2,1)S(1)}) fusion(f32[1024,1216]{1,0:T(8,128)} %fusion.45, f32[1024,1216]{1,0:T(8,128)} %get-tuple-element.260, bf16[1024,2048]{1,0:T(8,128)(2,1)S(1)} %pad_maximum_fusion.3, bf16[1216,2048]{1,0:T(8,128)(2,1)} %bitcast.433), kind=kOutput, calls=%fused_computation.24 | convolution fusion | flops 5116461056 | bytes 24117248 | tf_op jit(solution)/shard_map/dot_general | solution.py:28
  540.2 28.7 %two_gradients.1 = (bf16[2048,1216]{1,0:T(8,128)(2,1)}, bf16[2048,1216]{1,0:T(8,128)(2,1)}) custom-call(bf16[2048,2048]{1,0:T(8,128)(2,1)} %copy-done.10, bf16[2048,1216]{1,0:T(8,128)(2,1)} %pad_maximum_fusion.dg_ref, bf16[2048,1216]{1,0:T(8,128)(2,1)} %pad_maximum_fusion.1.du_ref), custom_call_target="tpu_custom_call" | custom-call | flops 1000 | bytes 1000 | tf_op jit(solution)/shard_map/two_gradients/pallas_call | solution.py:291
  569.3 11.4 %fusion.82 = f32[1024,2048]{1,0:T(8,128)} fusion(bf16[1024,1216]{1,0:T(8,128)(2,1)} %copy-done.30, bf16[2048,1216]{1,0:T(8,128)(2,1)} %bitcast.428), kind=kOutput, calls=%fused_computation.265 | convolution fusion | flops 5100273664 | bytes 15859712 | tf_op jit(solution)/shard_map/dot_general | solution.py:28
  580.7 9.6 convolution_add_fusion
  669.1 13.8 %collective-permute-start.29 = (bf16[152,2048]{1,0:T(8,128)(2,1)}, bf16[152,2048]{1,0:T(8,128)(2,1)}, u32[]{:S(2)}, u32[]{:S(2)}) collective-permute-start(bf16[152,2048]{1,0:T(8,128)(2,1)} %dynamic-slice_bitcast_fusion.6), channel_id=1, source_target_pairs={{0,16},{16,0},{1,17},{17,1},{2,18},{18,2},{3,19},{19,3},{4,20},{20... | collective-permute-start | bytes 1867784 | tf_op jit(solution)/shard_map/ppermute | solution.py:337
  682.9 8.7 convolution_convert_fusion.2.d_ref
  693.8 31.2 %collective-permute-done.29 = bf16[152,2048]{1,0:T(8,128)(2,1)} collective-permute-done((bf16[152,2048]{1,0:T(8,128)(2,1)}, bf16[152,2048]{1,0:T(8,128)(2,1)}, u32[]{:S(2)}, u32[]{:S(2)}) %collective-permute-start.29) | collective-permute-done | bytes 622624 | tf_op jit(solution)/shard_map/ppermute | solution.py:337
  727.1 30.8 %attention_backward.3 = (bf16[256,1536]{1,0:T(8,128)(2,1)}, bf16[1024,384]{1,0:T(8,128)(2,1)}, bf16[1024,384]{1,0:T(8,128)(2,1)}, f32[3,8,64]{2,1,0:T(8,128)}) custom-call(s32[1]{0:T(128)} %bitcast.seen_ref, f32[512,1536]{1,0:T(8,128)} %fusion.15.q_ref, bf16[1024,768]{1,0:T(8,128)(2,1)} %bitcast.335, bf16[1024,768]{1,0:T(8,128)(2,1)} %bitcast.336, ...), custom_call_target="tpu_custom_call" | custom-call | flops 1000 | bytes 1000 | tf_op jit(solution)/shard_map/attention_backward/pallas_call | solution.py:181
  757.9 30.8 %attention_backward.2 = (bf16[256,1536]{1,0:T(8,128)(2,1)}, bf16[1024,384]{1,0:T(8,128)(2,1)}, bf16[1024,384]{1,0:T(8,128)(2,1)}, f32[3,8,64]{2,1,0:T(8,128)}) custom-call(s32[1]{0:T(128)} %bitcast.seen_ref, f32[512,1536]{1,0:T(8,128)} %fusion.15.q_ref, bf16[1024,768]{1,0:T(8,128)(2,1)} %bitcast.331, bf16[1024,768]{1,0:T(8,128)(2,1)} %bitcast.332, ...), custom_call_target="tpu_custom_call" | custom-call | flops 1000 | bytes 1000 | tf_op jit(solution)/shard_map/attention_backward/pallas_call | solution.py:181
  795.3 15.6 %collective-permute-done.26 = bf16[2,256,768]{2,1,0:T(8,128)(2,1)} collective-permute-done((bf16[2,256,768]{2,1,0:T(8,128)(2,1)S(1)}, bf16[2,256,768]{2,1,0:T(8,128)(2,1)}, u32[]{:S(2)}, u32[]{:S(2)}) %collective-permute-start.26) | collective-permute-done | bytes 786464 | tf_op jit(solution)/shard_map/ppermute | solution.py:337
  813.3 22.5 %collective-permute-start.27 = (bf16[1,256,768]{2,1,0:T(8,128)(2,1)}, bf16[1,256,768]{2,1,0:T(8,128)(2,1)}, u32[]{:S(2)}, u32[]{:S(2)}) collective-permute-start(bf16[1,256,768]{2,1,0:T(8,128)(2,1)} %constant_dynamic-slice_fusion.3), channel_id=1, source_target_pairs={{0,16},{8,24},{16,0},{24,8},{1,17},{9,25},{17,1},{25,9},{2,18},{10... | collective-permute-start | bytes 1179656 | tf_op jit(solution)/shard_map/ppermute | solution.py:337
  839.1 21.1 %collective-permute-start.31 = (bf16[1,256,768]{2,1,0:T(8,128)(2,1)}, bf16[1,256,768]{2,1,0:T(8,128)(2,1)}, u32[]{:S(2)}, u32[]{:S(2)}) collective-permute-start(bf16[1,256,768]{2,1,0:T(8,128)(2,1)} %constant_dynamic-slice_fusion.2), channel_id=1, source_target_pairs={{0,16},{8,24},{16,0},{24,8},{1,17},{9,25},{17,1},{25,9},{2,18},{10... | collective-permute-start | bytes 1179656 | tf_op jit(solution)/shard_map/ppermute | solution.py:337
  921.8 61.2 %collective-permute-done.33 = bf16[48,2048]{1,0:T(8,128)(2,1)S(1)} collective-permute-done((bf16[48,2048]{1,0:T(8,128)(2,1)S(1)}, bf16[48,2048]{1,0:T(8,128)(2,1)S(1)}, u32[]{:S(2)}, u32[]{:S(2)}) %collective-permute-start.33) | collective-permute-done | bytes 196640 | tf_op jit(solution)/shard_map/ppermute | solution.py:337
  998.9 8.8 fusion.36
  1052.1 9.5 collective-permute-done.45
  (463 shorter events, 381.2 us)
Async XLA Ops:
  7.2 180.2 %all-gather.5.cloned.1.call-start = ((), (), s32[]{:S(2)}) async-start(), calls=%async_computation.5 | async-start | bytes 18923520 | tf_op jit(solution)/shard_map/all_gather | solution.py:460
  21.0 367.7 %all-gather.9.cloned.1.call-start = ((), (), s32[]{:S(2)}) async-start(), calls=%async_computation.7 | async-start | bytes 6553600 | tf_op jit(solution)/shard_map/all_gather | solution.py:400
  26.8 119.0 %collective-permute-start.2 = (bf16[64,1216]{1,0:T(8,128)(2,1)}, bf16[64,1216]{1,0:T(8,128)(2,1)}, u32[]{:S(2)}, u32[]{:S(2)}) collective-permute-start(bf16[64,1216]{1,0:T(8,128)(2,1)} %get-tuple-element.243), channel_id=1, source_target_pairs={{0,9},{1,8},{8,1},{9,0},{2,11},{3,10},{10,3},{11,2},{4,13},{5,12},... | collective-permute-start | bytes 466952 | tf_op jit(solution)/shard_map/ppermute | solution.py:337
  27.2 118.6 %collective-permute-start = (bf16[64,1216]{1,0:T(8,128)(2,1)}, bf16[64,1216]{1,0:T(8,128)(2,1)}, u32[]{:S(2)}, u32[]{:S(2)}) collective-permute-start(bf16[64,1216]{1,0:T(8,128)(2,1)} %get-tuple-element.242), channel_id=1, source_target_pairs={{0,1},{1,0},{8,9},{9,8},{2,3},{3,2},{10,11},{11,10},{4,5},{5,4},{1... | collective-permute-start | bytes 466952 | tf_op jit(solution)/shard_map/ppermute | solution.py:337
  27.3 118.4 %collective-permute-start.1 = (bf16[64,1216]{1,0:T(8,128)(2,1)}, bf16[64,1216]{1,0:T(8,128)(2,1)}, u32[]{:S(2)}, u32[]{:S(2)}) collective-permute-start(bf16[64,1216]{1,0:T(8,128)(2,1)} %get-tuple-element.244), channel_id=1, source_target_pairs={{0,8},{1,9},{8,0},{9,1},{2,10},{3,11},{10,2},{11,3},{4,12},{5,13},... | collective-permute-start | bytes 466952 | tf_op jit(solution)/shard_map/ppermute | solution.py:337
  29.8 117.5 %collective-permute-start.3 = (bf16[512,2048]{1,0:T(8,128)(2,1)}, bf16[512,2048]{1,0:T(8,128)(2,1)}, u32[]{:S(2)}, u32[]{:S(2)}) collective-permute-start(bf16[512,2048]{1,0:T(8,128)(2,1)} %bitcast.19), channel_id=1, source_target_pairs={{0,8},{8,0},{1,9},{9,1},{2,10},{10,2},{3,11},{11,3},{4,12},{12,4},... | collective-permute-start | bytes 6291464 | tf_op jit(solution)/shard_map/ppermute | solution.py:337
  33.7 106.1 %collective-permute-start.15 = (bf16[2,128,1216]{1,2,0:T(8,128)(2,1)}, bf16[2,128,1216]{1,2,0:T(8,128)(2,1)}, u32[]{:S(2)}, u32[]{:S(2)}) collective-permute-start(bf16[2,128,1216]{1,2,0:T(8,128)(2,1)} %copy.170), channel_id=1, source_target_pairs={{0,16},{16,0},{1,17},{17,1},{2,18},{18,2},{3,19},{19,3},{4,20},{20... | collective-permute-start | bytes 1867784 | tf_op jit(solution)/shard_map/ppermute | solution.py:337
  143.6 258.4 %all-gather.11.cloned.1.call-start = ((), (), s32[]{:S(2)}) async-start(), calls=%async_computation.8 | async-start | bytes 6553600 | tf_op jit(solution)/shard_map/all_gather | solution.py:400
  200.4 41.9 %collective-permute-start.4 = (bf16[1,256,768]{2,1,0:T(8,128)(2,1)}, bf16[1,256,768]{2,1,0:T(8,128)(2,1)S(1)}, u32[]{:S(2)}, u32[]{:S(2)}) collective-permute-start(bf16[1,256,768]{2,1,0:T(8,128)(2,1)} %bitcast.387), channel_id=1, source_target_pairs={{0,16},{8,24},{16,0},{24,8},{1,17},{9,25},{17,1},{25,9},{2,18},{10... | collective-permute-start | bytes 1179656 | tf_op jit(solution)/shard_map/ppermute | solution.py:337
  208.6 42.1 %collective-permute-start.6 = (bf16[1,256,768]{2,1,0:T(8,128)(2,1)}, bf16[1,256,768]{2,1,0:T(8,128)(2,1)}, u32[]{:S(2)}, u32[]{:S(2)}) collective-permute-start(bf16[1,256,768]{2,1,0:T(8,128)(2,1)} %bitcast.388), channel_id=1, source_target_pairs={{0,16},{8,24},{16,0},{24,8},{1,17},{9,25},{17,1},{25,9},{2,18},{10... | collective-permute-start | bytes 1179656 | tf_op jit(solution)/shard_map/ppermute | solution.py:337
  209.6 54.1 %collective-permute-start.16 = (bf16[2,128,1216]{1,2,0:T(8,128)(2,1)S(1)}, bf16[2,128,1216]{1,2,0:T(8,128)(2,1)S(1)}, u32[]{:S(2)}, u32[]{:S(2)}) collective-permute-start(bf16[2,128,1216]{1,2,0:T(8,128)(2,1)S(1)} %copy.175), channel_id=1, source_target_pairs={{0,16},{16,0},{1,17},{17,1},{2,18},{18,2},{3,19},{19,3},{4,20},{20... | collective-permute-start | bytes 1867784 | tf_op jit(solution)/shard_map/ppermute | solution.py:337
  243.4 49.6 %collective-permute-start.5 = (bf16[2,256,768]{2,1,0:T(8,128)(2,1)}, bf16[2,256,768]{2,1,0:T(8,128)(2,1)}, u32[]{:S(2)}, u32[]{:S(2)}) collective-permute-start(bf16[2,256,768]{2,1,0:T(8,128)(2,1)} %maximum_bitcast_fusion.2), channel_id=1, source_target_pairs={{0,8},{8,0},{16,24},{24,16},{1,9},{9,1},{17,25},{25,17},{2,10},{10... | collective-permute-start | bytes 2359304 | tf_op jit(solution)/shard_map/ppermute | solution.py:337
  252.7 44.8 %collective-permute-start.7 = (bf16[2,256,768]{2,1,0:T(8,128)(2,1)}, bf16[2,256,768]{2,1,0:T(8,128)(2,1)}, u32[]{:S(2)}, u32[]{:S(2)}) collective-permute-start(bf16[2,256,768]{2,1,0:T(8,128)(2,1)} %maximum_bitcast_fusion.3), channel_id=1, source_target_pairs={{0,8},{8,0},{16,24},{24,16},{1,9},{9,1},{17,25},{25,17},{2,10},{10... | collective-permute-start | bytes 2359304 | tf_op jit(solution)/shard_map/ppermute | solution.py:337
  265.6 207.9 %all-gather.7.cloned.1.call-start = ((), (), s32[]{:S(2)}) async-start(), calls=%async_computation.6 | async-start | bytes 6225920 | tf_op jit(solution)/shard_map/all_gather | solution.py:400
  291.0 40.3 %collective-permute-start.8 = (bf16[152,2048]{1,0:T(8,128)(2,1)S(1)}, bf16[152,2048]{1,0:T(8,128)(2,1)}, u32[]{:S(2)}, u32[]{:S(2)}) collective-permute-start(bf16[152,2048]{1,0:T(8,128)(2,1)S(1)} %copy-done.71), channel_id=1, source_target_pairs={{0,0},{1,2},{2,4},{3,6},{4,16},{5,18},{6,20},{7,22},{8,1},{9,3},{1... | collective-permute-start | bytes 1867784 | tf_op jit(solution)/shard_map/ppermute | solution.py:465
  331.2 39.7 %collective-permute-start.9 = (bf16[152,2048]{1,0:T(8,128)(2,1)}, bf16[152,2048]{1,0:T(8,128)(2,1)}, u32[]{:S(2)}, u32[]{:S(2)}) collective-permute-start(bf16[152,2048]{1,0:T(8,128)(2,1)} %collective-permute-done.8), channel_id=1, source_target_pairs={{0,16},{16,0},{1,17},{17,1},{2,18},{18,2},{3,19},{19,3},{4,20},{20... | collective-permute-start | bytes 1867784 | tf_op jit(solution)/shard_map/ppermute | solution.py:337
  386.2 48.0 %collective-permute-start.18 = (bf16[256,2048]{1,0:T(8,128)(2,1)}, bf16[256,2048]{1,0:T(8,128)(2,1)S(1)}, u32[]{:S(2)}, u32[]{:S(2)}) collective-permute-start(bf16[256,2048]{1,0:T(8,128)(2,1)} %get-tuple-element.172), channel_id=1, source_target_pairs={{0,8},{8,0},{1,9},{9,1},{2,10},{10,2},{3,11},{11,3},{4,12},{12,4},... | collective-permute-start | bytes 3145736 | tf_op jit(solution)/shard_map/ppermute | solution.py:337
  388.2 248.8 %reduce-scatter.16.cloned.1.call-start = ((), (), s32[]{:S(2)}) async-start(), calls=%async_computation.13 | async-start | bytes 6225920
  479.0 212.5 %reduce-scatter.8.cloned.1.call-start = ((), (), s32[]{:S(2)}) async-start(), calls=%async_computation.9 | async-start | bytes 6553600 | tf_op jit(solution)/shard_map/reduce_scatter | solution.py:408
  521.3 47.9 %collective-permute-start.22 = (bf16[512,2048]{1,0:T(8,128)(2,1)}, bf16[512,2048]{1,0:T(8,128)(2,1)S(1)}, u32[]{:S(2)}, u32[]{:S(2)}) collective-permute-start(bf16[512,2048]{1,0:T(8,128)(2,1)} %fusion.23), channel_id=1, source_target_pairs={{0,8},{8,0},{1,9},{9,1},{2,10},{10,2},{3,11},{11,3},{4,12},{12,4},... | collective-permute-start | bytes 6291464 | tf_op jit(solution)/shard_map/ppermute | solution.py:337
  569.3 307.6 %reduce-scatter.12.cloned.1.call-start = ((), (), s32[]{:S(2)}) async-start(), calls=%async_computation.11 | async-start | bytes 6553600 | tf_op jit(solution)/shard_map/reduce_scatter | solution.py:408
  595.4 281.5 %reduce-scatter.10.cloned.1.call-start = ((), (), s32[]{:S(2)}) async-start(), calls=%async_computation.10 | async-start | bytes 3932160 | tf_op jit(solution)/shard_map/reduce_scatter | solution.py:408
  668.1 370.4 %reduce-scatter.14.cloned.1.call-start = ((), (), s32[]{:S(2)}) async-start(), calls=%async_computation.12 | async-start | bytes 5898240 | tf_op jit(solution)/shard_map/reduce_scatter | solution.py:408
  669.1 55.9 %collective-permute-start.29 = (bf16[152,2048]{1,0:T(8,128)(2,1)}, bf16[152,2048]{1,0:T(8,128)(2,1)}, u32[]{:S(2)}, u32[]{:S(2)}) collective-permute-start(bf16[152,2048]{1,0:T(8,128)(2,1)} %dynamic-slice_bitcast_fusion.6), channel_id=1, source_target_pairs={{0,16},{16,0},{1,17},{17,1},{2,18},{18,2},{3,19},{19,3},{4,20},{20... | collective-permute-start | bytes 1867784 | tf_op jit(solution)/shard_map/ppermute | solution.py:337
  693.6 98.1 %collective-permute-start.28 = (bf16[4,64,1216]{2,1,0:T(8,128)(2,1)}, bf16[4,64,1216]{2,1,0:T(8,128)(2,1)}, u32[]{:S(2)}, u32[]{:S(2)}) collective-permute-start(bf16[4,64,1216]{2,1,0:T(8,128)(2,1)} %dynamic-slice_bitcast_fusion.5), channel_id=1, source_target_pairs={{0,16},{16,0},{1,17},{17,1},{2,18},{18,2},{3,19},{19,3},{4,20},{20... | collective-permute-start | bytes 1867784 | tf_op jit(solution)/shard_map/ppermute | solution.py:337
  794.3 41.5 %collective-permute-start.30 = (bf16[2,256,768]{2,1,0:T(8,128)(2,1)}, bf16[2,256,768]{2,1,0:T(8,128)(2,1)}, u32[]{:S(2)}, u32[]{:S(2)}) collective-permute-start(bf16[2,256,768]{2,1,0:T(8,128)(2,1)} %dynamic-slice_bitcast_fusion.2), channel_id=1, source_target_pairs={{0,8},{8,0},{16,24},{24,16},{1,9},{9,1},{17,25},{25,17},{2,10},{10... | collective-permute-start | bytes 2359304 | tf_op jit(solution)/shard_map/ppermute | solution.py:337
  813.3 46.9 %collective-permute-start.27 = (bf16[1,256,768]{2,1,0:T(8,128)(2,1)}, bf16[1,256,768]{2,1,0:T(8,128)(2,1)}, u32[]{:S(2)}, u32[]{:S(2)}) collective-permute-start(bf16[1,256,768]{2,1,0:T(8,128)(2,1)} %constant_dynamic-slice_fusion.3), channel_id=1, source_target_pairs={{0,16},{8,24},{16,0},{24,8},{1,17},{9,25},{17,1},{25,9},{2,18},{10... | collective-permute-start | bytes 1179656 | tf_op jit(solution)/shard_map/ppermute | solution.py:337
  913.2 79.2 %collective-permute-start.37 = (bf16[512,2048]{1,0:T(8,128)(2,1)}, bf16[512,2048]{1,0:T(8,128)(2,1)S(1)}, u32[]{:S(2)}, u32[]{:S(2)}) collective-permute-start(bf16[512,2048]{1,0:T(8,128)(2,1)} %fusion.22), channel_id=1, source_target_pairs={{0,8},{8,0},{1,9},{9,1},{2,10},{10,2},{3,11},{11,3},{4,12},{12,4},... | collective-permute-start | bytes 6291464 | tf_op jit(solution)/shard_map/ppermute | solution.py:337
  914.6 76.8 %collective-permute-start.36 = (bf16[4,64,1216]{2,1,0:T(8,128)(2,1)S(1)}, bf16[4,64,1216]{2,1,0:T(8,128)(2,1)S(1)}, u32[]{:S(2)}, u32[]{:S(2)}) collective-permute-start(bf16[4,64,1216]{2,1,0:T(8,128)(2,1)S(1)} %dynamic-slice_bitcast_fusion.4), channel_id=1, source_target_pairs={{0,16},{16,0},{1,17},{17,1},{2,18},{18,2},{3,19},{19,3},{4,20},{20... | collective-permute-start | bytes 1867784 | tf_op jit(solution)/shard_map/ppermute | solution.py:337
  917.4 65.6 %collective-permute-start.33 = (bf16[48,2048]{1,0:T(8,128)(2,1)S(1)}, bf16[48,2048]{1,0:T(8,128)(2,1)S(1)}, u32[]{:S(2)}, u32[]{:S(2)}) collective-permute-start(bf16[48,2048]{1,0:T(8,128)(2,1)S(1)} %get-tuple-element.198), channel_id=1, source_target_pairs={{0,8},{8,0},{16,24},{24,16},{1,9},{9,1},{17,25},{25,17},{2,10},{10... | collective-permute-start | bytes 589832 | tf_op jit(solution)/shard_map/ppermute | solution.py:337
  918.9 71.6 %collective-permute-start.34 = (bf16[48,2048]{1,0:T(8,128)(2,1)S(1)}, bf16[48,2048]{1,0:T(8,128)(2,1)S(1)}, u32[]{:S(2)}, u32[]{:S(2)}) collective-permute-start(bf16[48,2048]{1,0:T(8,128)(2,1)S(1)} %get-tuple-element.200), channel_id=1, source_target_pairs={{0,16},{8,24},{16,0},{24,8},{1,17},{9,25},{17,1},{25,9},{2,18},{10... | collective-permute-start | bytes 589832 | tf_op jit(solution)/shard_map/ppermute | solution.py:337
  918.9 71.6 %collective-permute-start.35 = (bf16[48,2048]{1,0:T(8,128)(2,1)S(1)}, bf16[48,2048]{1,0:T(8,128)(2,1)S(1)}, u32[]{:S(2)}, u32[]{:S(2)}) collective-permute-start(bf16[48,2048]{1,0:T(8,128)(2,1)S(1)} %get-tuple-element.199), channel_id=1, source_target_pairs={{0,24},{8,16},{16,8},{24,0},{1,25},{9,17},{17,9},{25,1},{2,26},{10... | collective-permute-start | bytes 589832 | tf_op jit(solution)/shard_map/ppermute | solution.py:337
  (114 other events, 1414.4 us)
Sparse Core Ops, SparseCore 0:
  21.1 166.1 all-gather.4
  189.2 62.1 all-gather.8
  265.7 75.1 all-gather.10
  388.3 70.4 all-gather.6
  479.1 70.5 reduce-scatter.15
  569.4 72.7 reduce-scatter.7
  645.2 61.3 reduce-scatter.11
  709.5 43.8 reduce-scatter.9
  911.2 58.2 reduce-scatter.13

commit v5 on v4

--- a/solution.py
+++ b/solution.py
@@ -492,6 +492,7 @@
         kv = [make_key(s, kv_lin, gain_key, cosine, sine) for s in range(seqs)]
         gathered = [gather_inner(v, here).reshape(length, 2 * kv_width) for v in kv]
         q_lin = mm(normed_b, wq)
+        gathered[0], cut_down = tie(gathered[0], cut_down)
         gathered[-1], cut_down = tie(gathered[-1], cut_down)
         cut_down = spread_line(cut_down, line)
         wu = whole_rows(spread_line(cut_up, line).reshape(n_inner, 2 * per, part), part)
@@ -554,7 +555,6 @@
         sent_out = fold(mm(hidden_far, wd)).astype(BF)
         kept_out = fold(mm(hidden_near, wd))
         dn2, down_part, sent_out, kept_out = tie(dn2, down_part, sent_out, kept_out)
-        down_sum = sum_pieces(down_part, "line", n_line, line).astype(BF)
         dn2 = dn2 + got.astype(F32)
         back_two, terms_two = rms_back(resid, inv_two, g_two, dn2)
         grad_gain_two = jnp.sum(terms_two, axis=0)
@@ -578,7 +578,9 @@
         drb = d_resid.astype(BF)
         dm = mm_nt(drb, wo).astype(BF)
         out_part = scatter_plane(fold_core(mm_tn(mixed, drb).astype(BF)), n_inner)
-        dm, gate_part = tie(dm, gate_part)
+        dm, gate_part, down_part = tie(dm, gate_part, down_part)
+        down_sum = sum_pieces(down_part, "line", n_line, line).astype(BF)
+        output = resid + (kept_out + pair_swap(sent_out).astype(F32))
         gate_sum = sum_pieces(gate_part.reshape(n_line, n_tp, per, part), "line", n_line, line)
         dq = []
         dkv = []
@@ -591,11 +593,10 @@
             gains_q.append(jnp.sum(dg_s[:, 0], axis=0))
             both = jnp.concatenate([dk_s, dv_s], axis=1)
             if s == seqs - 1:
-                both, gate_sum, down_sum = tie(both, gate_sum, down_sum)
+                both, gate_sum, down_sum, output = tie(both, gate_sum, down_sum, output)
             dkv.append(scatter_inner(both.reshape(n_inner, span, 2 * kv_width), here))
         d_down = lax.ppermute(down_sum, ALL, [(b, a) for a, b in spread]).astype(F32)
-        dkv[-1], out_part, up_part, sent_out = tie(dkv[-1], out_part, up_part, sent_out)
-        output = resid + (kept_out + pair_swap(sent_out).astype(F32))
+        dkv[-1], out_part, up_part = tie(dkv[-1], out_part, up_part)
         up_sum = sum_pieces(up_part.reshape(n_line, n_tp, per, part), "line", n_line, line)
         d_out = sum_pieces(out_part, INNER, n_inner, here)
         d_kvs = []
@@ -608,7 +609,7 @@
         d_lin = jnp.concatenate([jnp.concatenate(dq), jnp.concatenate(d_kvs)], axis=1)
         grad_qkv = mm_tn(normed_b, d_lin).astype(BF)
         qkv_part = scatter_plane(fold_core(grad_qkv), n_inner)
-        d_lin, grad_qkv, d_out, up_sum, output = tie(d_lin, grad_qkv, d_out, up_sum, output)
+        d_lin, grad_qkv, d_out, up_sum = tie(d_lin, grad_qkv, d_out, up_sum)
         result = output.astype(BF).reshape(seqs, span, width)
         d_gate = column_whole(gate_sum)
         d_up = column_whole(up_sum)

time: 1080 us -> 1040 us (0.963)
  waiting for transfers between devices: 403 us -> 355 us
    ppermute x1, waiting for transfers between devices: 31.1 us -> 0.01 us  [body(): cut_down = lax.ppermute(w_down, ALL, spread)]
    ppermute x52, waiting for transfers between devices: 331 us -> 314 us  [flip(): return lax.ppermute(v, axis, [(i, i ^ bit) for i in range(size)])]
    ppermute x1, starting transfers between devices: 2.03 us -> 14.4 us  [body(): cut_down = lax.ppermute(w_down, ALL, spread)]
    unnamed x174 -> x166, local copies, waits for them, and re-layouts: 31.7 us -> 29.5 us
  transfers between devices with their start and end apart: 63 -> 63, of which waited for: 27 -> 26; matrix products, arithmetic and copies ran while one was open for 32% -> 34% of each run, Pallas kernels for 12% -> 13%
where the time goes in v5:
time: 1040 us; the launch traced here: 1030 us
  waiting for transfers between devices  355 us (34%)
  matrix products  196 us (19%)
  Pallas kernels  139 us (13%)
  starting transfers between devices  115 us (11%)
  other arithmetic  115 us (11%)
  local copies, waits for them, and re-layouts  93.8 us (9%)
  between operations  15.5 us (1%)
    ppermute x52, waiting for transfers between devices, flip(): return lax.ppermute(v, axis, [(i, i ^ bit) for i in range(size)])  314 us
    dot_general x22, matrix products, dot(): return lax.dot_general(a, b, dims, preferred_element_type=F32)  196 us
    ppermute x52, starting transfers between devices, flip(): return lax.ppermute(v, axis, [(i, i ^ bit) for i in range(size)])  98 us
    pallas_call x2, Pallas kernels, backward(): pl.pallas_call(backward_kernel, grid_spec=pltpu.PrefetchScalarGridSpec(nu...  61.6 us
    all_gather x1, waiting for transfers between devices, body(): packed = lax.all_gather(packed, ALL, axis=0, tiled=True)  40.3 us
    pallas_call x2, Pallas kernels, forward(): pl.pallas_call(forward_kernel, grid_spec=pltpu.PrefetchScalarGridSpec(num...  33.2 us
    unnamed x166, local copies, waits for them, and re-layouts  29.5 us
    pallas_call x1, Pallas kernels, two_gradients(): pl.pallas_call(kernel, grid=(width // unit,), in_specs=[pl.BlockSpec((tok...  28.7 us
  transfers between devices with their start and end apart: 63, of which 26 were waited for; matrix products, arithmetic and copies ran while one was open for 34% of the time, Pallas kernels for 13%

profile of v5, /device:TPU:12, one launch (start us, length us, event | category | flops | bytes accessed | tf_op | source)
XLA Modules:
  0.0 1030.4 jit_solution(16583910225882411053)
XLA Ops:
  37.4 102.4 %collective-permute-done.15 = bf16[2,128,1216]{1,2,0:T(8,128)(2,1)} collective-permute-done((bf16[2,128,1216]{1,2,0:T(8,128)(2,1)}, bf16[2,128,1216]{1,2,0:T(8,128)(2,1)}, u32[]{:S(2)}, u32[]{:S(2)}) %collective-permute-start.15) | collective-permute-done | bytes 622624 | tf_op jit(solution)/shard_map/ppermute | solution.py:337
  147.0 40.3 %all-gather.5.cloned.1.call-done = bf16[2048,4480]{1,0:T(8,128)(2,1)} async-done(((bf16[64,4480]{1,0:T(8,128)(2,1)}), bf16[2048,4480]{1,0:T(8,128)(2,1)}) %all-gather.5.cloned.1.call-update) | async-done | bytes 18350096 | tf_op jit(solution)/shard_map/all_gather | solution.py:460
  208.7 14.4 %collective-permute-start.8 = (bf16[152,2048]{1,0:T(8,128)(2,1)}, bf16[152,2048]{1,0:T(8,128)(2,1)}, u32[]{:S(2)}, u32[]{:S(2)}) collective-permute-start(bf16[152,2048]{1,0:T(8,128)(2,1)} %param.28), channel_id=1, source_target_pairs={{0,0},{1,2},{2,4},{3,6},{4,16},{5,18},{6,20},{7,22},{8,1},{9,3},{1... | collective-permute-start | bytes 1867784 | tf_op jit(solution)/shard_map/ppermute | solution.py:465
  226.4 29.2 %collective-permute-done.6 = bf16[1,256,768]{2,1,0:T(8,128)(2,1)S(1)} collective-permute-done((bf16[1,256,768]{2,1,0:T(8,128)(2,1)}, bf16[1,256,768]{2,1,0:T(8,128)(2,1)S(1)}, u32[]{:S(2)}, u32[]{:S(2)}) %collective-permute-start.6) | collective-permute-done | bytes 393248 | tf_op jit(solution)/shard_map/ppermute | solution.py:337
  256.8 20.7 %collective-permute-done.4 = bf16[1,256,768]{2,1,0:T(8,128)(2,1)} collective-permute-done((bf16[1,256,768]{2,1,0:T(8,128)(2,1)}, bf16[1,256,768]{2,1,0:T(8,128)(2,1)}, u32[]{:S(2)}, u32[]{:S(2)}) %collective-permute-start.4) | collective-permute-done | bytes 393248 | tf_op jit(solution)/shard_map/ppermute | solution.py:337
  279.5 10.9 %collective-permute-done.16 = bf16[2,128,1216]{1,2,0:T(8,128)(2,1)S(1)} collective-permute-done((bf16[2,128,1216]{1,2,0:T(8,128)(2,1)S(1)}, bf16[2,128,1216]{1,2,0:T(8,128)(2,1)S(1)}, u32[]{:S(2)}, u32[]{:S(2)}) %collective-permute-start.16) | collective-permute-done | bytes 622624 | tf_op jit(solution)/shard_map/ppermute | solution.py:337
  300.9 9.3 slice.236
  326.0 16.4 %attention_forward.3 = (bf16[256,1536]{1,0:T(8,128)(2,1)}, f32[256,1536]{1,0:T(8,128)}) custom-call(s32[1]{0:T(128)} %bitcast.seen_ref, f32[512,1536]{1,0:T(8,128)} %fusion.15.q_ref, bf16[1024,768]{1,0:T(8,128)(2,1)} %bitcast.329, bf16[1024,768]{1,0:T(8,128)(2,1)} %bitcast.330, f32[1,64]{1,0:T(1,128)} %reshape.785.gain_ref, ...), custom_call_target="tpu_custom_call" | custom-call | flops 1000 | bytes 1000 | tf_op jit(solution)/shard_map/attention_forward/pallas_call | solution.py:163
  347.9 16.8 %attention_forward.2 = (bf16[256,1536]{1,0:T(8,128)(2,1)}, f32[256,1536]{1,0:T(8,128)}) custom-call(s32[1]{0:T(128)} %bitcast.seen_ref, f32[512,1536]{1,0:T(8,128)} %fusion.15.q_ref, bf16[1024,768]{1,0:T(8,128)(2,1)} %bitcast.333, bf16[1024,768]{1,0:T(8,128)(2,1)} %bitcast.334, f32[1,64]{1,0:T(1,128)} %reshape.785.gain_ref, ...), custom_call_target="tpu_custom_call" | custom-call | flops 1000 | bytes 1000 | tf_op jit(solution)/shard_map/attention_forward/pallas_call | solution.py:163
  385.6 11.3 %fusion.45 = f32[1024,1216]{1,0:T(8,128)} fusion(bf16[2048,1216]{1,0:T(8,128)(2,1)} %bitcast.420, bf16[512,2048]{1,0:T(8,128)(2,1)} %collective-permute-done.11, bf16[256,2048]{1,0:T(8,128)(2,1)} %get-tuple-element.176, bf16[256,2048]{1,0:T(8,128)(2,1)S(1)} %get-tuple-element.178), kind=kOutput, calls=%fused_computation.92 | convolution fusion | flops 5112856576 | bytes 14155776 | tf_op jit(solution)/shard_map/dot_general | solution.py:28
  397.0 15.2 %multiply_convert_fusion.5 = (bf16[1024,1216]{1,0:T(8,128)(2,1)}, f32[1024,1216]{1,0:T(8,128)}) fusion(f32[1024,1216]{1,0:T(8,128)} %fusion.45, bf16[2048,1216]{1,0:T(8,128)(2,1)} %bitcast.426, bf16[512,2048]{1,0:T(8,128)(2,1)} %collective-permute-done.11, bf16[256,2048]{1,0:T(8,128)(2,1)} %get-tuple-element.176, bf16[256,2048]{1,0:T(8,128)(2,1)S(1)} %get-tuple-element.178), kind=kOutput, calls=%fused_computation.31 | convolution fusion | flops 5120327680 | bytes 21626880 | tf_op jit(solution)/shard_map/dot_general | solution.py:28
  412.1 17.0 %collective-permute-done.18 = bf16[256,2048]{1,0:T(8,128)(2,1)S(1)} collective-permute-done((bf16[256,2048]{1,0:T(8,128)(2,1)}, bf16[256,2048]{1,0:T(8,128)(2,1)S(1)}, u32[]{:S(2)}, u32[]{:S(2)}) %collective-permute-start.18) | collective-permute-done | bytes 1048608 | tf_op jit(solution)/shard_map/ppermute | solution.py:337
  441.9 9.9 multiply_convert_fusion.4
  453.8 14.8 %fusion.9 = bf16[1216,2048]{1,0:T(8,128)(2,1)} fusion(bf16[512,2048]{1,0:T(8,128)(2,1)S(1)} %collective-permute-done.10, bf16[512,2048]{1,0:T(8,128)(2,1)} %collective-permute-done.3, bf16[512,2048]{1,0:T(8,128)(2,1)S(1)} %collective-permute-done.20, bf16[512,2048]{1,0:T(8,128)(2,1)} %bitcast.19, bf16[1024,1216]{1,0:T(8,128)(2,1)} %get-tuple-element.133, ...), kind=kOutput, calls=%fused_computation.11 | convolution fusion | flops 10246553600 | bytes 18350080 | tf_op jit(solution)/shard_map/dot_general | solution.py:28
  475.6 12.7 %multiply_convert_fusion.2 = (bf16[1024,1216]{1,0:T(8,128)(2,1)S(1)}, bf16[1024,1216]{1,0:T(8,128)(2,1)S(1)}) fusion(f32[1024,1216]{1,0:T(8,128)} %fusion.80, f32[1024,1216]{1,0:T(8,128)} %get-tuple-element.266, bf16[1216,2048]{1,0:T(8,128)(2,1)} %bitcast.432, bf16[512,2048]{1,0:T(8,128)(2,1)S(1)} %copy-done.67, bf16[512,2048]{1,0:T(8,128)(2,1)} %collective-permute-done.3), kind=kOutput, calls=%fused_computation.26 | convolution fusion | flops 5124849664 | bytes 24117248 | tf_op jit(solution)/shard_map/dot_general | solution.py:28
  488.4 11.9 %fusion.81 = f32[1024,2048]{1,0:T(8,128)} fusion(bf16[1024,1216]{1,0:T(8,128)(2,1)S(1)} %get-tuple-element.182, bf16[2048,1216]{1,0:T(8,128)(2,1)} %bitcast.421), kind=kOutput, calls=%fused_computation.264 | convolution fusion | flops 5100273664 | bytes 15859712 | tf_op jit(solution)/shard_map/dot_general | solution.py:28
  500.3 9.8 convolution_add_fusion.1
  517.2 11.7 %multiply_convert_fusion = (bf16[1024,1216]{1,0:T(8,128)(2,1)S(1)}, bf16[1024,1216]{1,0:T(8,128)(2,1)S(1)}) fusion(f32[1024,1216]{1,0:T(8,128)} %fusion.45, f32[1024,1216]{1,0:T(8,128)} %get-tuple-element.264, bf16[1024,2048]{1,0:T(8,128)(2,1)S(1)} %pad_maximum_fusion.3, bf16[1216,2048]{1,0:T(8,128)(2,1)} %bitcast.433), kind=kOutput, calls=%fused_computation.24 | convolution fusion | flops 5116461056 | bytes 24117248 | tf_op jit(solution)/shard_map/dot_general | solution.py:28
  535.6 28.7 %two_gradients.1 = (bf16[2048,1216]{1,0:T(8,128)(2,1)}, bf16[2048,1216]{1,0:T(8,128)(2,1)}) custom-call(bf16[2048,2048]{1,0:T(8,128)(2,1)} %copy-done.10, bf16[2048,1216]{1,0:T(8,128)(2,1)} %pad_maximum_fusion.dg_ref, bf16[2048,1216]{1,0:T(8,128)(2,1)} %pad_maximum_fusion.1.du_ref), custom_call_target="tpu_custom_call" | custom-call | flops 1000 | bytes 1000 | tf_op jit(solution)/shard_map/two_gradients/pallas_call | solution.py:291
  564.9 11.4 %fusion.82 = f32[1024,2048]{1,0:T(8,128)} fusion(bf16[1024,1216]{1,0:T(8,128)(2,1)} %copy-done.28, bf16[2048,1216]{1,0:T(8,128)(2,1)} %bitcast.428), kind=kOutput, calls=%fused_computation.265 | convolution fusion | flops 5100273664 | bytes 15859712 | tf_op jit(solution)/shard_map/dot_general | solution.py:28
  576.3 9.6 convolution_add_fusion
  662.6 9.0 convolution_convert_fusion.2.d_ref
  671.6 27.1 %collective-permute-done.28 = bf16[512,2048]{1,0:T(8,128)(2,1)} collective-permute-done((bf16[512,2048]{1,0:T(8,128)(2,1)}, bf16[512,2048]{1,0:T(8,128)(2,1)}, u32[]{:S(2)}, u32[]{:S(2)}) %collective-permute-start.28) | collective-permute-done | bytes 2097184 | tf_op jit(solution)/shard_map/ppermute | solution.py:337
  704.9 10.9 %collective-permute-start.26 = (bf16[4,64,1216]{2,1,0:T(8,128)(2,1)}, bf16[4,64,1216]{2,1,0:T(8,128)(2,1)}, u32[]{:S(2)}, u32[]{:S(2)}) collective-permute-start(bf16[4,64,1216]{2,1,0:T(8,128)(2,1)} %dynamic-slice_bitcast_fusion.5), channel_id=1, source_target_pairs={{0,16},{16,0},{1,17},{17,1},{2,18},{18,2},{3,19},{19,3},{4,20},{20... | collective-permute-start | bytes 1867784 | tf_op jit(solution)/shard_map/ppermute | solution.py:337
  716.7 30.6 %attention_backward.2 = (bf16[256,1536]{1,0:T(8,128)(2,1)}, bf16[1024,384]{1,0:T(8,128)(2,1)}, bf16[1024,384]{1,0:T(8,128)(2,1)}, f32[3,8,64]{2,1,0:T(8,128)}) custom-call(s32[1]{0:T(128)} %bitcast.seen_ref, f32[512,1536]{1,0:T(8,128)} %fusion.15.q_ref, bf16[1024,768]{1,0:T(8,128)(2,1)} %bitcast.335, bf16[1024,768]{1,0:T(8,128)(2,1)} %bitcast.336, ...), custom_call_target="tpu_custom_call" | custom-call | flops 1000 | bytes 1000 | tf_op jit(solution)/shard_map/attention_backward/pallas_call | solution.py:181
  747.3 31.0 %attention_backward.3 = (bf16[256,1536]{1,0:T(8,128)(2,1)}, bf16[1024,384]{1,0:T(8,128)(2,1)}, bf16[1024,384]{1,0:T(8,128)(2,1)}, f32[3,8,64]{2,1,0:T(8,128)}) custom-call(s32[1]{0:T(128)} %bitcast.seen_ref, f32[512,1536]{1,0:T(8,128)} %fusion.15.q_ref, bf16[1024,768]{1,0:T(8,128)(2,1)} %bitcast.331, bf16[1024,768]{1,0:T(8,128)(2,1)} %bitcast.332, ...), custom_call_target="tpu_custom_call" | custom-call | flops 1000 | bytes 1000 | tf_op jit(solution)/shard_map/attention_backward/pallas_call | solution.py:181
  788.2 13.5 %collective-permute-done.29 = bf16[2,256,768]{2,1,0:T(8,128)(2,1)} collective-permute-done((bf16[2,256,768]{2,1,0:T(8,128)(2,1)}, bf16[2,256,768]{2,1,0:T(8,128)(2,1)}, u32[]{:S(2)}, u32[]{:S(2)}) %collective-permute-start.29) | collective-permute-done | bytes 786464 | tf_op jit(solution)/shard_map/ppermute | solution.py:337
  803.8 22.2 %collective-permute-start.30 = (bf16[1,256,768]{2,1,0:T(8,128)(2,1)}, bf16[1,256,768]{2,1,0:T(8,128)(2,1)S(1)}, u32[]{:S(2)}, u32[]{:S(2)}) collective-permute-start(bf16[1,256,768]{2,1,0:T(8,128)(2,1)} %constant_dynamic-slice_fusion.3), channel_id=1, source_target_pairs={{0,16},{8,24},{16,0},{24,8},{1,17},{9,25},{17,1},{25,9},{2,18},{10... | collective-permute-start | bytes 1179656 | tf_op jit(solution)/shard_map/ppermute | solution.py:337
  828.2 21.1 %collective-permute-start.32 = (bf16[1,256,768]{2,1,0:T(8,128)(2,1)}, bf16[1,256,768]{2,1,0:T(8,128)(2,1)}, u32[]{:S(2)}, u32[]{:S(2)}) collective-permute-start(bf16[1,256,768]{2,1,0:T(8,128)(2,1)} %constant_dynamic-slice_fusion.2), channel_id=1, source_target_pairs={{0,16},{8,24},{16,0},{24,8},{1,17},{9,25},{17,1},{25,9},{2,18},{10... | collective-permute-start | bytes 1179656 | tf_op jit(solution)/shard_map/ppermute | solution.py:337
  906.7 16.0 %collective-permute-done.34 = bf16[48,2048]{1,0:T(8,128)(2,1)S(1)} collective-permute-done((bf16[48,2048]{1,0:T(8,128)(2,1)S(1)}, bf16[48,2048]{1,0:T(8,128)(2,1)S(1)}, u32[]{:S(2)}, u32[]{:S(2)}) %collective-permute-start.34) | collective-permute-done | bytes 196640 | tf_op jit(solution)/shard_map/ppermute | solution.py:337
  922.7 20.9 %collective-permute-done.35 = bf16[48,2048]{1,0:T(8,128)(2,1)S(1)} collective-permute-done((bf16[48,2048]{1,0:T(8,128)(2,1)S(1)}, bf16[48,2048]{1,0:T(8,128)(2,1)S(1)}, u32[]{:S(2)}, u32[]{:S(2)}) %collective-permute-start.35) | collective-permute-done | bytes 196640 | tf_op jit(solution)/shard_map/ppermute | solution.py:337
  1003.0 11.2 %collective-permute-done.45 = bf16[64,2304]{1,0:T(8,128)(2,1)} collective-permute-done((bf16[64,2304]{1,0:T(8,128)(2,1)S(1)}, bf16[64,2304]{1,0:T(8,128)(2,1)}, u32[]{:S(2)}, u32[]{:S(2)}) %collective-permute-start.45) | collective-permute-done | bytes 294944 | tf_op jit(solution)/shard_map/ppermute | solution.py:337
  (455 shorter events, 376.9 us)
Async XLA Ops:
  7.2 180.2 %all-gather.5.cloned.1.call-start = ((), (), s32[]{:S(2)}) async-start(), calls=%async_computation.5 | async-start | bytes 18923520 | tf_op jit(solution)/shard_map/all_gather | solution.py:460
  21.0 362.4 %all-gather.9.cloned.1.call-start = ((), (), s32[]{:S(2)}) async-start(), calls=%async_computation.7 | async-start | bytes 6553600 | tf_op jit(solution)/shard_map/all_gather | solution.py:400
  26.8 118.7 %collective-permute-start.2 = (bf16[64,1216]{1,0:T(8,128)(2,1)}, bf16[64,1216]{1,0:T(8,128)(2,1)}, u32[]{:S(2)}, u32[]{:S(2)}) collective-permute-start(bf16[64,1216]{1,0:T(8,128)(2,1)} %get-tuple-element.247), channel_id=1, source_target_pairs={{0,9},{1,8},{8,1},{9,0},{2,11},{3,10},{10,3},{11,2},{4,13},{5,12},... | collective-permute-start | bytes 466952 | tf_op jit(solution)/shard_map/ppermute | solution.py:337
  27.2 118.3 %collective-permute-start = (bf16[64,1216]{1,0:T(8,128)(2,1)}, bf16[64,1216]{1,0:T(8,128)(2,1)}, u32[]{:S(2)}, u32[]{:S(2)}) collective-permute-start(bf16[64,1216]{1,0:T(8,128)(2,1)} %get-tuple-element.246), channel_id=1, source_target_pairs={{0,1},{1,0},{8,9},{9,8},{2,3},{3,2},{10,11},{11,10},{4,5},{5,4},{1... | collective-permute-start | bytes 466952 | tf_op jit(solution)/shard_map/ppermute | solution.py:337
  27.3 118.2 %collective-permute-start.1 = (bf16[64,1216]{1,0:T(8,128)(2,1)}, bf16[64,1216]{1,0:T(8,128)(2,1)}, u32[]{:S(2)}, u32[]{:S(2)}) collective-permute-start(bf16[64,1216]{1,0:T(8,128)(2,1)} %get-tuple-element.248), channel_id=1, source_target_pairs={{0,8},{1,9},{8,0},{9,1},{2,10},{3,11},{10,2},{11,3},{4,12},{5,13},... | collective-permute-start | bytes 466952 | tf_op jit(solution)/shard_map/ppermute | solution.py:337
  29.8 117.2 %collective-permute-start.3 = (bf16[512,2048]{1,0:T(8,128)(2,1)}, bf16[512,2048]{1,0:T(8,128)(2,1)}, u32[]{:S(2)}, u32[]{:S(2)}) collective-permute-start(bf16[512,2048]{1,0:T(8,128)(2,1)} %bitcast.19), channel_id=1, source_target_pairs={{0,8},{8,0},{1,9},{9,1},{2,10},{10,2},{3,11},{11,3},{4,12},{12,4},... | collective-permute-start | bytes 6291464 | tf_op jit(solution)/shard_map/ppermute | solution.py:337
  33.7 106.1 %collective-permute-start.15 = (bf16[2,128,1216]{1,2,0:T(8,128)(2,1)}, bf16[2,128,1216]{1,2,0:T(8,128)(2,1)}, u32[]{:S(2)}, u32[]{:S(2)}) collective-permute-start(bf16[2,128,1216]{1,2,0:T(8,128)(2,1)} %copy.170), channel_id=1, source_target_pairs={{0,16},{16,0},{1,17},{17,1},{2,18},{18,2},{3,19},{19,3},{4,20},{20... | collective-permute-start | bytes 1867784 | tf_op jit(solution)/shard_map/ppermute | solution.py:337
  143.5 253.5 %all-gather.11.cloned.1.call-start = ((), (), s32[]{:S(2)}) async-start(), calls=%async_computation.8 | async-start | bytes 6553600 | tf_op jit(solution)/shard_map/all_gather | solution.py:400
  200.4 55.3 %collective-permute-start.6 = (bf16[1,256,768]{2,1,0:T(8,128)(2,1)}, bf16[1,256,768]{2,1,0:T(8,128)(2,1)S(1)}, u32[]{:S(2)}, u32[]{:S(2)}) collective-permute-start(bf16[1,256,768]{2,1,0:T(8,128)(2,1)} %bitcast.387), channel_id=1, source_target_pairs={{0,16},{8,24},{16,0},{24,8},{1,17},{9,25},{17,1},{25,9},{2,18},{10... | collective-permute-start | bytes 1179656 | tf_op jit(solution)/shard_map/ppermute | solution.py:337
  208.7 111.4 %collective-permute-start.8 = (bf16[152,2048]{1,0:T(8,128)(2,1)}, bf16[152,2048]{1,0:T(8,128)(2,1)}, u32[]{:S(2)}, u32[]{:S(2)}) collective-permute-start(bf16[152,2048]{1,0:T(8,128)(2,1)} %param.28), channel_id=1, source_target_pairs={{0,0},{1,2},{2,4},{3,6},{4,16},{5,18},{6,20},{7,22},{8,1},{9,3},{1... | collective-permute-start | bytes 1867784 | tf_op jit(solution)/shard_map/ppermute | solution.py:465
  223.0 54.4 %collective-permute-start.4 = (bf16[1,256,768]{2,1,0:T(8,128)(2,1)}, bf16[1,256,768]{2,1,0:T(8,128)(2,1)}, u32[]{:S(2)}, u32[]{:S(2)}) collective-permute-start(bf16[1,256,768]{2,1,0:T(8,128)(2,1)} %bitcast.388), channel_id=1, source_target_pairs={{0,16},{8,24},{16,0},{24,8},{1,17},{9,25},{17,1},{25,9},{2,18},{10... | collective-permute-start | bytes 1179656 | tf_op jit(solution)/shard_map/ppermute | solution.py:337
  223.5 67.0 %collective-permute-start.16 = (bf16[2,128,1216]{1,2,0:T(8,128)(2,1)S(1)}, bf16[2,128,1216]{1,2,0:T(8,128)(2,1)S(1)}, u32[]{:S(2)}, u32[]{:S(2)}) collective-permute-start(bf16[2,128,1216]{1,2,0:T(8,128)(2,1)S(1)} %copy.175), channel_id=1, source_target_pairs={{0,16},{16,0},{1,17},{17,1},{2,18},{18,2},{3,19},{19,3},{4,20},{20... | collective-permute-start | bytes 1867784 | tf_op jit(solution)/shard_map/ppermute | solution.py:337
  256.8 60.6 %collective-permute-start.7 = (bf16[2,256,768]{2,1,0:T(8,128)(2,1)}, bf16[2,256,768]{2,1,0:T(8,128)(2,1)}, u32[]{:S(2)}, u32[]{:S(2)}) collective-permute-start(bf16[2,256,768]{2,1,0:T(8,128)(2,1)} %maximum_bitcast_fusion.3), channel_id=1, source_target_pairs={{0,8},{8,0},{16,24},{24,16},{1,9},{9,1},{17,25},{25,17},{2,10},{10... | collective-permute-start | bytes 2359304 | tf_op jit(solution)/shard_map/ppermute | solution.py:337
  279.5 40.6 %collective-permute-start.5 = (bf16[2,256,768]{2,1,0:T(8,128)(2,1)}, bf16[2,256,768]{2,1,0:T(8,128)(2,1)}, u32[]{:S(2)}, u32[]{:S(2)}) collective-permute-start(bf16[2,256,768]{2,1,0:T(8,128)(2,1)} %maximum_bitcast_fusion.2), channel_id=1, source_target_pairs={{0,8},{8,0},{16,24},{24,16},{1,9},{9,1},{17,25},{25,17},{2,10},{10... | collective-permute-start | bytes 2359304 | tf_op jit(solution)/shard_map/ppermute | solution.py:337
  292.3 176.3 %all-gather.7.cloned.1.call-start = ((), (), s32[]{:S(2)}) async-start(), calls=%async_computation.6 | async-start | bytes 6225920 | tf_op jit(solution)/shard_map/all_gather | solution.py:400
  322.8 43.2 %collective-permute-start.9 = (bf16[152,2048]{1,0:T(8,128)(2,1)}, bf16[152,2048]{1,0:T(8,128)(2,1)}, u32[]{:S(2)}, u32[]{:S(2)}) collective-permute-start(bf16[152,2048]{1,0:T(8,128)(2,1)} %collective-permute-done.8), channel_id=1, source_target_pairs={{0,16},{16,0},{1,17},{17,1},{2,18},{18,2},{3,19},{19,3},{4,20},{20... | collective-permute-start | bytes 1867784 | tf_op jit(solution)/shard_map/ppermute | solution.py:337
  381.1 48.0 %collective-permute-start.18 = (bf16[256,2048]{1,0:T(8,128)(2,1)}, bf16[256,2048]{1,0:T(8,128)(2,1)S(1)}, u32[]{:S(2)}, u32[]{:S(2)}) collective-permute-start(bf16[256,2048]{1,0:T(8,128)(2,1)} %get-tuple-element.176), channel_id=1, source_target_pairs={{0,8},{8,0},{1,9},{9,1},{2,10},{10,2},{3,11},{11,3},{4,12},{12,4},... | collective-permute-start | bytes 3145736 | tf_op jit(solution)/shard_map/ppermute | solution.py:337
  383.2 249.0 %reduce-scatter.16.cloned.1.call-start = ((), (), s32[]{:S(2)}) async-start(), calls=%async_computation.13 | async-start | bytes 6225920
  474.1 228.8 %reduce-scatter.8.cloned.1.call-start = ((), (), s32[]{:S(2)}) async-start(), calls=%async_computation.9 | async-start | bytes 6553600 | tf_op jit(solution)/shard_map/reduce_scatter | solution.py:408
  516.8 48.1 %collective-permute-start.22 = (bf16[512,2048]{1,0:T(8,128)(2,1)}, bf16[512,2048]{1,0:T(8,128)(2,1)S(1)}, u32[]{:S(2)}, u32[]{:S(2)}) collective-permute-start(bf16[512,2048]{1,0:T(8,128)(2,1)} %fusion.23), channel_id=1, source_target_pairs={{0,8},{8,0},{1,9},{9,1},{2,10},{10,2},{3,11},{11,3},{4,12},{12,4},... | collective-permute-start | bytes 6291464 | tf_op jit(solution)/shard_map/ppermute | solution.py:337
  564.9 300.7 %reduce-scatter.12.cloned.1.call-start = ((), (), s32[]{:S(2)}) async-start(), calls=%async_computation.11 | async-start | bytes 6553600 | tf_op jit(solution)/shard_map/reduce_scatter | solution.py:408
  590.9 274.7 %reduce-scatter.10.cloned.1.call-start = ((), (), s32[]{:S(2)}) async-start(), calls=%async_computation.10 | async-start | bytes 3932160 | tf_op jit(solution)/shard_map/reduce_scatter | solution.py:408
  650.7 48.0 %collective-permute-start.28 = (bf16[512,2048]{1,0:T(8,128)(2,1)}, bf16[512,2048]{1,0:T(8,128)(2,1)}, u32[]{:S(2)}, u32[]{:S(2)}) collective-permute-start(bf16[512,2048]{1,0:T(8,128)(2,1)} %fusion.22), channel_id=1, source_target_pairs={{0,8},{8,0},{1,9},{9,1},{2,10},{10,2},{3,11},{11,3},{4,12},{12,4},... | collective-permute-start | bytes 6291464 | tf_op jit(solution)/shard_map/ppermute | solution.py:337
  662.5 328.6 %reduce-scatter.14.cloned.1.call-start = ((), (), s32[]{:S(2)}) async-start(), calls=%async_computation.12 | async-start | bytes 5898240 | tf_op jit(solution)/shard_map/reduce_scatter | solution.py:408
  704.9 76.2 %collective-permute-start.26 = (bf16[4,64,1216]{2,1,0:T(8,128)(2,1)}, bf16[4,64,1216]{2,1,0:T(8,128)(2,1)}, u32[]{:S(2)}, u32[]{:S(2)}) collective-permute-start(bf16[4,64,1216]{2,1,0:T(8,128)(2,1)} %dynamic-slice_bitcast_fusion.5), channel_id=1, source_target_pairs={{0,16},{16,0},{1,17},{17,1},{2,18},{18,2},{3,19},{19,3},{4,20},{20... | collective-permute-start | bytes 1867784 | tf_op jit(solution)/shard_map/ppermute | solution.py:337
  716.7 66.5 %collective-permute-start.27 = (bf16[152,2048]{1,0:T(8,128)(2,1)}, bf16[152,2048]{1,0:T(8,128)(2,1)}, u32[]{:S(2)}, u32[]{:S(2)}) collective-permute-start(bf16[152,2048]{1,0:T(8,128)(2,1)} %dynamic-slice_bitcast_fusion.6), channel_id=1, source_target_pairs={{0,16},{16,0},{1,17},{17,1},{2,18},{18,2},{3,19},{19,3},{4,20},{20... | collective-permute-start | bytes 1867784 | tf_op jit(solution)/shard_map/ppermute | solution.py:337
  786.2 39.9 %collective-permute-start.31 = (bf16[2,256,768]{2,1,0:T(8,128)(2,1)}, bf16[2,256,768]{2,1,0:T(8,128)(2,1)}, u32[]{:S(2)}, u32[]{:S(2)}) collective-permute-start(bf16[2,256,768]{2,1,0:T(8,128)(2,1)} %dynamic-slice_bitcast_fusion.2), channel_id=1, source_target_pairs={{0,8},{8,0},{16,24},{24,16},{1,9},{9,1},{17,25},{25,17},{2,10},{10... | collective-permute-start | bytes 2359304 | tf_op jit(solution)/shard_map/ppermute | solution.py:337
  803.8 45.5 %collective-permute-start.30 = (bf16[1,256,768]{2,1,0:T(8,128)(2,1)}, bf16[1,256,768]{2,1,0:T(8,128)(2,1)S(1)}, u32[]{:S(2)}, u32[]{:S(2)}) collective-permute-start(bf16[1,256,768]{2,1,0:T(8,128)(2,1)} %constant_dynamic-slice_fusion.3), channel_id=1, source_target_pairs={{0,16},{8,24},{16,0},{24,8},{1,17},{9,25},{17,1},{25,9},{2,18},{10... | collective-permute-start | bytes 1179656 | tf_op jit(solution)/shard_map/ppermute | solution.py:337
  885.2 84.2 %collective-permute-start.53 = (bf16[152,2048]{1,0:T(8,128)(2,1)}, bf16[152,2048]{1,0:T(8,128)(2,1)}, u32[]{:S(2)}, u32[]{:S(2)}) collective-permute-start(bf16[152,2048]{1,0:T(8,128)(2,1)} %fusion.52), channel_id=1, source_target_pairs={{0,0},{2,1},{4,2},{6,3},{16,4},{18,5},{20,6},{22,7},{1,8},{3,9},{5... | collective-permute-start | bytes 1867784 | tf_op jit(solution)/shard_map/ppermute | solution.py:598
  898.8 51.4 %collective-permute-start.37 = (bf16[4,64,1216]{2,1,0:T(8,128)(2,1)S(1)}, bf16[4,64,1216]{2,1,0:T(8,128)(2,1)S(1)}, u32[]{:S(2)}, u32[]{:S(2)}) collective-permute-start(bf16[4,64,1216]{2,1,0:T(8,128)(2,1)S(1)} %dynamic-slice_bitcast_fusion.4), channel_id=1, source_target_pairs={{0,16},{16,0},{1,17},{17,1},{2,18},{18,2},{3,19},{19,3},{4,20},{20... | collective-permute-start | bytes 1867784 | tf_op jit(solution)/shard_map/ppermute | solution.py:337
  903.0 40.6 %collective-permute-start.35 = (bf16[48,2048]{1,0:T(8,128)(2,1)S(1)}, bf16[48,2048]{1,0:T(8,128)(2,1)S(1)}, u32[]{:S(2)}, u32[]{:S(2)}) collective-permute-start(bf16[48,2048]{1,0:T(8,128)(2,1)S(1)} %get-tuple-element.204), channel_id=1, source_target_pairs={{0,16},{8,24},{16,0},{24,8},{1,17},{9,25},{17,1},{25,9},{2,18},{10... | collective-permute-start | bytes 589832 | tf_op jit(solution)/shard_map/ppermute | solution.py:337
  903.2 46.2 %collective-permute-start.36 = (bf16[48,2048]{1,0:T(8,128)(2,1)S(1)}, bf16[48,2048]{1,0:T(8,128)(2,1)S(1)}, u32[]{:S(2)}, u32[]{:S(2)}) collective-permute-start(bf16[48,2048]{1,0:T(8,128)(2,1)S(1)} %get-tuple-element.203), channel_id=1, source_target_pairs={{0,24},{8,16},{16,8},{24,0},{1,25},{9,17},{17,9},{25,1},{2,26},{10... | collective-permute-start | bytes 589832 | tf_op jit(solution)/shard_map/ppermute | solution.py:337
  (110 other events, 1419.1 us)
Sparse Core Ops, SparseCore 0:
  21.1 166.1 all-gather.4
  189.2 79.1 all-gather.8
  292.4 63.2 all-gather.10
  383.3 68.2 all-gather.6
  474.2 68.2 reduce-scatter.15
  565.0 69.8 reduce-scatter.7
  637.9 61.3 reduce-scatter.11
  702.2 43.9 reduce-scatter.9
  897.3 60.9 reduce-scatter.13
